TPU v7x, 32 devices: a whole 2x2x4 slice. The times are simulated.
32 devices in a mesh: dom: 32 (over z, y, x, core).
Axes of the slice: x: 2, y: 2, z: 4, core: 2. Of those that a mesh axis runs over, the one named last changes fastest.
Arguments:
- right_side: float32 [1024, 16, 128], P('dom')
- band_blocks: float32 [1024, 5, 128, 128], P('dom'), as said below
- link_blocks: float32 [32, 6, 4, 128, 128], P('dom'), as said below
- link_rows: int32 [32, 6, 4], P('dom'), may hold values from 0 to 32, as said below
Outputs:
- solution: float32 [1024, 16, 128], P('dom')
- residual: float32 [1024, 16, 128], P('dom')
Inputs may be any that keep to these rules, and one draw needn't show every extreme that they name: `link_rows`: entries are a row of device d (0 to 31) or 32 for an unused slot. Slot s of interface j of device d is paired with slot s of interface j xor 1 of the device it faces, and is used exactly when that one is. Each interface uses its first 1 to 4 slots and no row twice; in every draw some interface uses all 4. link_blocks[d, j, s] is the transpose of link_blocks[e, j xor 1, s] for the device e that interface j of d faces; blocks of unused slots are zero. band_blocks[g, 2 + m] is the transpose of band_blocks[g + m, 2 - m]; blocks whose column falls outside the device are zero. A is symmetric with a positive diagonal that exceeds the sum of magnitudes of the rest of its row.
All inputs are finite; a program needn't handle non-finite values.
Results may differ from a plain program's by a relative error of at most 0.0003.
Values sent between devices are 32-bit elements; how exact they have to be, the bound alone decides.
No kernel may reach another device: no remote copies, remote signals or barrier semaphores. Data moves between devices by JAX's collectives and lax.ppermute only.
A program may use at most 64 MiB of HBM per device.

v0:
```python
import functools

import jax
import jax.numpy as jnp
from jax import lax
from jax.experimental import pallas as pl
from jax.experimental.pallas import tpu as pltpu
from jax.sharding import PartitionSpec as P


ITERS = 3
LEVELS = ITERS + 1
PIECES = 3
F32 = jnp.float32
BF16 = jnp.bfloat16
MIB = 1 << 20

MATCHINGS = ((0, 1), (1, 1), (2, 1), (2, 0), (1, 0), (0, 0))


def offsets(dev_count):
    return (1, dev_count // 16, dev_count // 4)


def matching_pairs(dev_count, pair, phase):
    off = offsets(dev_count)[pair]
    return [
        (i, (i + off) % dev_count if (i // off + phase) % 2 == 0 else (i - off) % dev_count)
        for i in range(dev_count)
    ]


def matching_face(dev_count, pair, phase):
    me = lax.axis_index("dom")
    return 2 * pair + lax.rem(me // offsets(dev_count)[pair] + phase, 2)


def pieces_of(value):
    high = value.astype(BF16)
    rest = value - high.astype(F32)
    mid = rest.astype(BF16)
    low = (rest - mid.astype(F32)).astype(BF16)
    return high, mid, low


def vmem(count):
    return [pl.BlockSpec(memory_space=pltpu.VMEM)] * count


def smem():
    return pl.BlockSpec(memory_space=pltpu.SMEM)


def params(mib):
    return pltpu.CompilerParams(vmem_limit_bytes=mib * MIB)


def send_rows(dev_count, rows_ref, field_ref, out_refs):
    block_rows = field_ref.shape[0]
    for (pair, phase), out_ref in zip(MATCHINGS, out_refs):
        face = matching_face(dev_count, pair, phase)
        for slot in range(rows_ref.shape[2]):
            row = jnp.minimum(rows_ref[0, face, slot], block_rows - 1)
            out_ref[slot] = field_ref[row]


def split_field(field_ref, split_ref, pad):
    block_rows, width, size = field_ref.shape
    zero = jnp.zeros((split_ref.shape[0], pad * size), BF16)
    split_ref[:, : pad * size] = zero
    split_ref[:, (pad + block_rows) * size :] = zero
    for row in range(block_rows):
        cols = slice((pad + row) * size, (pad + row + 1) * size)
        for piece, value in enumerate(pieces_of(field_ref[row])):
            split_ref[piece * width : (piece + 1) * width, cols] = value


def first_send_kernel(dev_count, rows_ref, field_ref, *out_refs):
    send_rows(dev_count, rows_ref, field_ref, out_refs)


def prepare_kernel(half, field_ref, band_ref, link_ref, weights_ref, links_ref, split_ref, held, sems, link_held, link_sem):
    block_rows, band, size, _ = band_ref.shape
    pairs = block_rows // 2
    span = band + 1
    slots = held.shape[0]

    def fetch(row, slot):
        return pltpu.make_async_copy(band_ref.at[row], held.at[slot], sems.at[slot])

    link_copy = pltpu.make_async_copy(link_ref.at[0], link_held, link_sem)
    for row in range(slots):
        fetch(row, row).start()
    link_copy.start()
    split_field(field_ref, split_ref, half)
    zero = jnp.zeros((size, size), BF16)

    def clear(pair, carry):
        for copy in range(2):
            weights_ref[pair, copy * span, :, size:] = zero
            weights_ref[pair, copy * span + span - 1, :, :size] = zero
        return carry

    lax.fori_loop(0, pairs + 2, clear, 0)
    wide = jnp.zeros((size, 2 * size), BF16)
    for copy in range(2):
        for place in range(half):
            weights_ref[1, copy * span + place] = wide
            weights_ref[pairs, copy * span + span - 1 - place] = wide

    def convert(step, carry):
        for even in range(slots):
            row = slots * step + even
            fetch(row, even).wait()
            base = slots // 2 * step + even // 2
            for k in range(band):
                shift = (even % 2 + k - half) // 2
                col = (even % 2 + k - half) % 2
                place = even % 2 + half - 2 * shift
                block = held[even, k]
                high = block.astype(BF16)
                low = (block - high.astype(F32)).astype(BF16)
                cols = slice(col * size, (col + 1) * size)
                weights_ref[base + shift + 1, place, :, cols] = high
                weights_ref[base + shift + 1, span + place, :, cols] = low

            @pl.when(row + slots < block_rows)
            def _():
                fetch(row + slots, even).start()

        return carry

    lax.fori_loop(0, block_rows // slots, convert, 0)
    link_copy.wait()
    faces, count = link_held.shape[0], link_held.shape[1]

    def convert_links(face, carry):
        for slot in range(count):
            block = link_held[face, slot].T
            high = block.astype(BF16)
            low = (block - high.astype(F32)).astype(BF16)
            cols = slice(slot % 2 * size, (slot % 2 + 1) * size)
            links_ref[face, slot // 2, :size, cols] = high
            links_ref[face, slot // 2, size:, cols] = low
        return carry

    lax.fori_loop(0, faces, convert_links, 0)


def fold(value, width):
    total = value[(PIECES - 1) * width : PIECES * width]
    for piece in range(PIECES - 2, -1, -1):
        total = total + value[piece * width : (piece + 1) * width]
    return total


def band_kernel(weights_ref, split_ref, out_ref):
    block_rows, width, size = out_ref.shape
    pairs = block_rows // 2
    depth = weights_ref.shape[1] * size
    span = depth // 2

    def pair_product(pair, carry):
        start = pl.multiple_of(pair * 2 * size, 2 * size)
        rows = split_ref[:, pl.ds(start, span)]
        both = jnp.concatenate([rows, rows], axis=1)
        weights = weights_ref[pair + 1].reshape(depth, 2 * size)
        total = fold(jnp.dot(both, weights, preferred_element_type=F32), width)
        out_ref[2 * pair] = total[:, :size]
        out_ref[2 * pair + 1] = total[:, size:]
        return carry

    lax.fori_loop(0, pairs, pair_product, 0, unroll=4)


def add_links(dev_count, rows_ref, base_ref, links_ref, far_refs, field_ref):
    block_rows, width, size = base_ref.shape
    field_ref[...] = base_ref[...]
    for (pair, phase), far_ref in zip(MATCHINGS, far_refs):
        face = matching_face(dev_count, pair, phase)
        for two in range(far_ref.shape[0] // 2):
            stacked = []
            for slot in (2 * two, 2 * two + 1):
                stacked.extend(pieces_of(far_ref[slot]))
            rows = jnp.concatenate(stacked, axis=0)
            both = jnp.concatenate([rows, rows], axis=1)
            product = jnp.dot(both, links_ref[face, two], preferred_element_type=F32)
            for k in range(2):
                part = product[k * PIECES * width : (k + 1) * PIECES * width, k * size : (k + 1) * size]
                row = jnp.minimum(rows_ref[0, face, 2 * two + k], block_rows - 1)
                field_ref[row] = field_ref[row] + fold(part, width)


def link_kernel(dev_count, pad, rows_ref, base_ref, links_ref, *refs):
    count = len(MATCHINGS)
    far_refs, split_ref, out_refs, field_ref = refs[:count], refs[count], refs[count + 1 : -1], refs[-1]
    add_links(dev_count, rows_ref, base_ref, links_ref, far_refs, field_ref)
    send_rows(dev_count, rows_ref, field_ref, out_refs)
    split_field(field_ref, split_ref, pad)


def gram_rows(left, split_refs, cols):
    width = split_refs[0].shape[0] // PIECES
    right = [ref[piece * width : (piece + 1) * width, cols] for piece in range(PIECES) for ref in split_refs]
    fill = [jnp.zeros_like(right[0])] * (2 * 128 // width - len(right))
    return lax.dot_general(
        left, jnp.concatenate(right + fill, axis=0), (((1,), (1,)), ((), ())), preferred_element_type=F32
    )


def fold_lanes(value):
    first = value[:, :128]
    return value[:, 128:] + (first + pltpu.roll(first, 64, 1))


def gram_kernel(pad, split0, split1, split2, out_ref, total):
    rows, lanes = split0.shape
    width = rows // PIECES
    refs = (split0, split1, split2, split2)
    inner = lanes - 2 * pad * 128
    chunk = inner // 8
    total[...] = jnp.zeros_like(total)

    def body(step, carry):
        cols = pl.ds(pl.multiple_of(pad * 128 + step * chunk, 128), chunk)
        left = jnp.concatenate([ref[:, cols] for ref in refs[:3]], axis=0)
        total[...] += gram_rows(left, refs, cols)
        return carry

    lax.fori_loop(0, 8, body, 0)
    z = [fold_lanes(fold(total[rows * k : rows * (k + 1)], width)) for k in range(3)]
    lane = lax.broadcasted_iota(jnp.int32, z[0].shape, 1)
    out_ref[...] = jnp.where(
        lane < 2 * width,
        z[0],
        jnp.where(lane < 4 * width, pltpu.roll(z[1], width, 1), pltpu.roll(z[2], 2 * width, 1)),
    )


def last_link_kernel(dev_count, pad, rows_ref, base_ref, links_ref, split2, moments_ref, *refs):
    count = len(MATCHINGS)
    far_refs, split_ref, out_ref, field_ref = refs[:count], refs[count], refs[count + 1], refs[-1]
    add_links(dev_count, rows_ref, base_ref, links_ref, far_refs, field_ref)
    split_field(field_ref, split_ref, pad)
    rows, lanes = split2.shape
    width = rows // PIECES
    cols = slice(pad * 128, lanes - pad * 128)
    z = fold_lanes(fold(gram_rows(split2[:, cols], (split2, split2, split2, split_ref), cols), width))
    lane = lax.broadcasted_iota(jnp.int32, z.shape, 1)
    mine = jnp.where(lane < 5 * width, moments_ref[...], pltpu.roll(z, 2 * width, 1))
    mine = jnp.where(lane < 6 * width, mine, 0.0)
    for peer in range(out_ref.shape[0]):
        out_ref[peer] = mine


def finish_kernel(pad, gathered_ref, split0, split1, split2, split3, solution_ref, residual_ref):
    peers, width, lanes = gathered_ref.shape
    block_rows = solution_ref.shape[0]
    moments = gathered_ref[0]
    for peer in range(1, peers):
        moments = moments + gathered_ref[peer]
    table = [pltpu.roll(moments, lanes - width * (k + 1), 1) for k in range(ITERS)] + [moments]
    table = jnp.concatenate(table, axis=0)
    lane = lax.broadcasted_iota(jnp.int32, (1, lanes), 1)
    for k in range(ITERS * width):
        row = table[k : k + 1, :]
        column = table[:, k : k + 1] * (1.0 / table[k : k + 1, k : k + 1])
        table = jnp.where(lane == k, column, table - column * row)
    coeffs = table[ITERS * width :]
    lane = lax.broadcasted_iota(jnp.int32, coeffs.shape, 1)
    unit = (lane == lax.broadcasted_iota(jnp.int32, coeffs.shape, 0)).astype(F32)
    for_solution = jnp.where(lane < ITERS * width, coeffs, 0.0)
    for_residual = jnp.where(lane < width, unit, jnp.where(lane < LEVELS * width, -pltpu.roll(coeffs, width, 1), 0.0))
    both = jnp.concatenate([for_solution, for_residual], axis=0)
    both = jnp.concatenate([both + pltpu.roll(both, 64, 1), both], axis=1)[:, : PIECES * LEVELS * width]
    left = jnp.concatenate(pieces_of(both), axis=0)
    refs = (split0, split1, split2, split3)
    step = 4

    def body(index, carry):
        cols = pl.ds(pl.multiple_of((pad + index * step) * 128, 128), step * 128)
        right = [ref[piece * width : (piece + 1) * width, cols] for piece in range(PIECES) for ref in refs]
        total = fold(jnp.dot(left, jnp.concatenate(right, axis=0), preferred_element_type=F32), 2 * width)
        for k in range(step):
            solution_ref[index * step + k] = total[:width, k * 128 : (k + 1) * 128]
            residual_ref[index * step + k] = total[width:, k * 128 : (k + 1) * 128]
        return carry

    lax.fori_loop(0, block_rows // step, body, 0, unroll=2)


def shards(right_side, band_blocks, link_blocks, link_rows):
    dev_count = lax.axis_size("dom")
    block_rows, width, size = right_side.shape
    band = band_blocks.shape[1]
    half = band // 2
    faces, slots = link_rows.shape[1:]
    pairs = block_rows // 2
    count = len(MATCHINGS)
    message = jax.ShapeDtypeStruct((slots, width, size), F32)
    split = jax.ShapeDtypeStruct((PIECES * width, (block_rows + 2 * half) * size), BF16)
    field = jax.ShapeDtypeStruct(right_side.shape, F32)

    def exchange(messages):
        got = []
        for index, (pair, phase) in enumerate(MATCHINGS):
            got.append(lax.ppermute(messages[index], "dom", matching_pairs(dev_count, pair, phase)))
        return got

    messages = pl.pallas_call(
        functools.partial(first_send_kernel, dev_count),
        out_shape=[message] * count,
        in_specs=[smem()] + vmem(1),
        out_specs=vmem(count),
        compiler_params=params(8),
        name="first_send",
    )(link_rows, right_side)
    far = exchange(messages)
    weights, links, split0 = pl.pallas_call(
        functools.partial(prepare_kernel, half),
        out_shape=[
            jax.ShapeDtypeStruct((pairs + 2, 2 * (band + 1), size, 2 * size), BF16),
            jax.ShapeDtypeStruct((faces, slots // 2, 2 * size, 2 * size), BF16),
            split,
        ],
        in_specs=vmem(1) + [pl.BlockSpec(memory_space=pl.ANY)] * 2,
        out_specs=vmem(3),
        scratch_shapes=[
            pltpu.VMEM((4, band, size, size), F32),
            pltpu.SemaphoreType.DMA((4,)),
            pltpu.VMEM((faces, slots, size, size), F32),
            pltpu.SemaphoreType.DMA,
        ],
        compiler_params=params(28),
        cost_estimate=pl.CostEstimate(flops=10**7, bytes_accessed=12 * 10**6, transcendentals=0),
        name="prepare",
    )(right_side, band_blocks, link_blocks)

    splits = [split0]
    for level in range(ITERS):
        base = pl.pallas_call(
            band_kernel,
            out_shape=field,
            in_specs=vmem(2),
            out_specs=vmem(1)[0],
            compiler_params=params(24),
            cost_estimate=pl.CostEstimate(flops=10**9, bytes_accessed=12 * 10**6, transcendentals=0),
            name="band",
        )(weights, splits[-1])
        if level + 1 < ITERS:
            outs = pl.pallas_call(
                functools.partial(link_kernel, dev_count, half),
                out_shape=[split] + [message] * count,
                in_specs=[smem()] + vmem(2 + count),
                out_specs=vmem(1 + count),
                scratch_shapes=[pltpu.VMEM(right_side.shape, F32)],
                compiler_params=params(12),
                name="link",
            )(link_rows, base, links, *far)
            splits.append(outs[0])
            far = exchange(outs[1:])
    moments = pl.pallas_call(
        functools.partial(gram_kernel, half),
        out_shape=jax.ShapeDtypeStruct((width, 128), F32),
        in_specs=vmem(ITERS),
        out_specs=vmem(1)[0],
        scratch_shapes=[pltpu.VMEM((ITERS * PIECES * width, 256), F32)],
        compiler_params=params(8),
        cost_estimate=pl.CostEstimate(flops=10**9, bytes_accessed=4 * 10**6, transcendentals=0),
        name="gram",
    )(*splits)
    split3, mine = pl.pallas_call(
        functools.partial(last_link_kernel, dev_count, half),
        out_shape=[split, jax.ShapeDtypeStruct((dev_count, width, 128), F32)],
        in_specs=[smem()] + vmem(4 + count),
        out_specs=vmem(2),
        scratch_shapes=[pltpu.VMEM(right_side.shape, F32)],
        compiler_params=params(12),
        name="last_link",
    )(link_rows, base, links, splits[-1], moments, *far)
    splits.append(split3)
    gathered = lax.all_to_all(mine, "dom", 0, 0)
    return pl.pallas_call(
        functools.partial(finish_kernel, half),
        out_shape=[field, field],
        in_specs=vmem(1 + LEVELS),
        out_specs=vmem(2),
        compiler_params=params(12),
        name="finish",
    )(gathered, *splits)


def solution(mesh):
    in_specs = (
        P("dom", None, None),
        P("dom", None, None, None),
        P("dom", None, None, None, None),
        P("dom", None, None),
    )
    out_specs = (P("dom", None, None), P("dom", None, None))
    return jax.shard_map(
        lambda *args: tuple(shards(*args)), mesh=mesh, in_specs=in_specs, out_specs=out_specs, check_vma=False
    )
```

profile of v0, /device:TPU:0, one launch (start us, length us, event | category | flops | bytes accessed | tf_op | source)
XLA Modules:
  0.0 86.7 jit_solution(14138658751876921649)
XLA Ops:
  0.6 0.8 copy.9.rows_ref
  1.4 0.9 %copy-done.3 = f32[32,16,128]{2,1,0:T(8,128)S(1)} copy-done((f32[32,16,128]{2,1,0:T(8,128)S(1)}, f32[32,16,128]{2,1,0:T(8,128)}, u32[]{:S(2)}) %copy-start.3) | copy-done | bytes 262168
  2.3 0.7 first_send.1
  3.0 6.5 %collective-permute-start = (f32[4,16,128]{2,1,0:T(8,128)S(1)}, f32[4,16,128]{2,1,0:T(8,128)S(1)}, u32[]{:S(2)}, u32[]{:S(2)}) collective-permute-start(f32[4,16,128]{2,1,0:T(8,128)S(1)} %get-tuple-element.30), channel_id=1, source_target_pairs={{0,31},{1,2},{2,1},{3,4},{4,3},{5,6},{6,5},{7,8},{8,7},{9,10},{10,... | collective-permute-start | bytes 98312 | tf_op jit(solution)/shard_map/ppermute | solution.py:307
  9.5 0.6 collective-permute-start.1
  10.1 0.4 collective-permute-start.2
  10.6 0.0 collective-permute-start.3
  10.6 1.4 %collective-permute-start.4 = (f32[4,16,128]{2,1,0:T(8,128)S(1)}, f32[4,16,128]{2,1,0:T(8,128)S(1)}, u32[]{:S(2)}, u32[]{:S(2)}) collective-permute-start(f32[4,16,128]{2,1,0:T(8,128)S(1)} %get-tuple-element.34), channel_id=1, source_target_pairs={{0,2},{1,3},{2,0},{3,1},{4,6},{5,7},{6,4},{7,5},{8,10},{9,11},{10,... | collective-permute-start | bytes 98312 | tf_op jit(solution)/shard_map/ppermute | solution.py:307
  12.0 4.0 %copy-done.1 = f32[32,5,128,128]{3,2,1,0:T(8,128)S(1)} copy-done((f32[32,5,128,128]{3,2,1,0:T(8,128)S(1)}, f32[32,5,128,128]{3,2,1,0:T(8,128)}, u32[]{:S(2)}) %copy-start.1) | copy-done | bytes 10485784
  16.0 1.4 %copy-done.2 = f32[1,6,4,128,128]{4,3,2,1,0:T(8,128)S(1)} copy-done((f32[1,6,4,128,128]{4,3,2,1,0:T(8,128)S(1)}, f32[1,6,4,128,128]{4,3,2,1,0:T(8,128)}, u32[]{:S(2)}) %copy-start.2) | copy-done | bytes 1572888
  17.4 0.9 %copy-done.4 = f32[32,16,128]{2,1,0:T(8,128)S(1)} copy-done((f32[32,16,128]{2,1,0:T(8,128)S(1)}, f32[32,16,128]{2,1,0:T(8,128)}, u32[]{:S(2)}) %copy-start.4) | copy-done | bytes 262168
  18.4 11.5 %prepare.1 = (bf16[18,12,128,256]{3,2,1,0:T(8,128)(2,1)}, bf16[6,2,256,256]{3,2,1,0:T(8,128)(2,1)S(1)}, bf16[48,4608]{1,0:T(8,128)(2,1)S(1)}) custom-call(f32[32,16,128]{2,1,0:T(8,128)S(1)} %copy-done.4, f32[32,5,128,128]{3,2,1,0:T(8,128)S(1)} %copy-done.1, f32[1,6,4,128,128]{4,3,2,1,0:T(8,128)S(1)} %copy-done.2), custom_call_target="tpu_custom_call" | custom-call | flops 10000000 | bytes 12000000 | tf_op jit(solution)/shard_map/prepare/pallas_call | solution.py:319
  29.8 0.0 collective-permute-done.refs_0_
  29.8 0.1 collective-permute-start.5
  29.9 5.0 %copy-done = bf16[18,12,128,256]{3,2,1,0:T(8,128)(2,1)S(1)} copy-done((bf16[18,12,128,256]{3,2,1,0:T(8,128)(2,1)S(1)}, bf16[18,12,128,256]{3,2,1,0:T(8,128)(2,1)}, u32[]{:S(2)}) %copy-start) | copy-done | bytes 14155800
  34.9 2.4 %band.3.base_ref = f32[32,16,128]{2,1,0:T(8,128)S(1)} custom-call(bf16[18,12,128,256]{3,2,1,0:T(8,128)(2,1)S(1)} %copy-done, bf16[48,4608]{1,0:T(8,128)(2,1)S(1)} %get-tuple-element.28.split_ref.split0), custom_call_target="tpu_custom_call" | custom-call | flops 1000000000 | bytes 12000000 | tf_op jit(solution)/shard_map/band/pallas_call | solution.py:341
  37.4 0.0 collective-permute-done.1.refs_1_
  37.4 0.0 collective-permute-done.2.refs_2_
  37.4 0.0 collective-permute-done.3.refs_3_
  37.4 0.0 collective-permute-done.4.refs_4_
  37.4 0.0 collective-permute-done.5.refs_5_
  37.4 1.1 %link.2 = (bf16[48,4608]{1,0:T(8,128)(2,1)S(1)}, f32[4,16,128]{2,1,0:T(8,128)S(1)}, f32[4,16,128]{2,1,0:T(8,128)S(1)}, f32[4,16,128]{2,1,0:T(8,128)S(1)}, f32[4,...) custom-call(s32[1,6,4]{2,1,0:T(8,128)S(1)} %copy.9.rows_ref, ...), custom_call_target="tpu_custom_call" | custom-call | tf_op jit(solution)/shard_map/link/pallas_call | solution.py:351
  38.5 3.3 %collective-permute-start.6 = (f32[4,16,128]{2,1,0:T(8,128)S(1)}, f32[4,16,128]{2,1,0:T(8,128)S(1)}, u32[]{:S(2)}, u32[]{:S(2)}) collective-permute-start(f32[4,16,128]{2,1,0:T(8,128)S(1)} %get-tuple-element.37), channel_id=1, source_target_pairs={{0,31},{1,2},{2,1},{3,4},{4,3},{5,6},{6,5},{7,8},{8,7},{9,10},{10,... | collective-permute-start | bytes 98312 | tf_op jit(solution)/shard_map/ppermute | solution.py:307
  41.8 2.0 %collective-permute-start.7 = (f32[4,16,128]{2,1,0:T(8,128)S(1)}, f32[4,16,128]{2,1,0:T(8,128)S(1)}, u32[]{:S(2)}, u32[]{:S(2)}) collective-permute-start(f32[4,16,128]{2,1,0:T(8,128)S(1)} %get-tuple-element.38), channel_id=1, source_target_pairs={{0,30},{1,31},{2,4},{3,5},{4,2},{5,3},{6,8},{7,9},{8,6},{9,7},{10,... | collective-permute-start | bytes 98312 | tf_op jit(solution)/shard_map/ppermute | solution.py:307
  43.8 2.0 %collective-permute-start.8 = (f32[4,16,128]{2,1,0:T(8,128)S(1)}, f32[4,16,128]{2,1,0:T(8,128)S(1)}, u32[]{:S(2)}, u32[]{:S(2)}) collective-permute-start(f32[4,16,128]{2,1,0:T(8,128)S(1)} %get-tuple-element.39), channel_id=1, source_target_pairs={{0,24},{1,25},{2,26},{3,27},{4,28},{5,29},{6,30},{7,31},{8,16},{9,... | collective-permute-start | bytes 98312 | tf_op jit(solution)/shard_map/ppermute | solution.py:307
  45.8 2.0 %collective-permute-start.9 = (f32[4,16,128]{2,1,0:T(8,128)S(1)}, f32[4,16,128]{2,1,0:T(8,128)S(1)}, u32[]{:S(2)}, u32[]{:S(2)}) collective-permute-start(f32[4,16,128]{2,1,0:T(8,128)S(1)} %get-tuple-element.40), channel_id=1, source_target_pairs={{0,8},{1,9},{2,10},{3,11},{4,12},{5,13},{6,14},{7,15},{8,0},{9,1},... | collective-permute-start | bytes 98312 | tf_op jit(solution)/shard_map/ppermute | solution.py:307
  47.9 0.0 collective-permute-start.10
  47.9 0.0 collective-permute-done.6.refs_0_
  47.9 0.0 collective-permute-start.11
  47.9 2.4 %band.4.base_ref = f32[32,16,128]{2,1,0:T(8,128)S(1)} custom-call(bf16[18,12,128,256]{3,2,1,0:T(8,128)(2,1)S(1)} %copy-done, bf16[48,4608]{1,0:T(8,128)(2,1)S(1)} %get-tuple-element.36.split_ref.split1), custom_call_target="tpu_custom_call" | custom-call | flops 1000000000 | bytes 12000000 | tf_op jit(solution)/shard_map/band/pallas_call | solution.py:341
  50.3 0.0 collective-permute-done.9.refs_3_
  50.3 1.4 %collective-permute-done.10.refs_4_ = f32[4,16,128]{2,1,0:T(8,128)S(1)} collective-permute-done((f32[4,16,128]{2,1,0:T(8,128)S(1)}, f32[4,16,128]{2,1,0:T(8,128)S(1)}, u32[]{:S(2)}, u32[]{:S(2)}) %collective-permute-start.10) | collective-permute-done | bytes 32800 | tf_op jit(solution)/shard_map/ppermute | solution.py:307
  51.8 0.0 collective-permute-done.11.refs_5_
  51.8 1.1 %link.3 = (bf16[48,4608]{1,0:T(8,128)(2,1)S(1)}, f32[4,16,128]{2,1,0:T(8,128)S(1)}, f32[4,16,128]{2,1,0:T(8,128)S(1)}, f32[4,16,128]{2,1,0:T(8,128)S(1)}, f32[4,...) custom-call(s32[1,6,4]{2,1,0:T(8,128)S(1)} %copy.9.rows_ref, ...), custom_call_target="tpu_custom_call" | custom-call | tf_op jit(solution)/shard_map/link/pallas_call | solution.py:351
  52.9 1.5 %collective-permute-start.12 = (f32[4,16,128]{2,1,0:T(8,128)S(1)}, f32[4,16,128]{2,1,0:T(8,128)S(1)}, u32[]{:S(2)}, u32[]{:S(2)}) collective-permute-start(f32[4,16,128]{2,1,0:T(8,128)S(1)} %get-tuple-element.44), channel_id=1, source_target_pairs={{0,31},{1,2},{2,1},{3,4},{4,3},{5,6},{6,5},{7,8},{8,7},{9,10},{10,... | collective-permute-start | bytes 98312 | tf_op jit(solution)/shard_map/ppermute | solution.py:307
  54.3 2.4 %band.5.base_ref = f32[32,16,128]{2,1,0:T(8,128)S(1)} custom-call(bf16[18,12,128,256]{3,2,1,0:T(8,128)(2,1)S(1)} %copy-done, bf16[48,4608]{1,0:T(8,128)(2,1)S(1)} %get-tuple-element.43.split_ref.split2), custom_call_target="tpu_custom_call" | custom-call | flops 1000000000 | bytes 12000000 | tf_op jit(solution)/shard_map/band/pallas_call | solution.py:341
  56.8 2.1 %collective-permute-start.13 = (f32[4,16,128]{2,1,0:T(8,128)S(1)}, f32[4,16,128]{2,1,0:T(8,128)S(1)}, u32[]{:S(2)}, u32[]{:S(2)}) collective-permute-start(f32[4,16,128]{2,1,0:T(8,128)S(1)} %get-tuple-element.45), channel_id=1, source_target_pairs={{0,30},{1,31},{2,4},{3,5},{4,2},{5,3},{6,8},{7,9},{8,6},{9,7},{10,... | collective-permute-start | bytes 98312 | tf_op jit(solution)/shard_map/ppermute | solution.py:307
  58.8 0.9 %collective-permute-start.14 = (f32[4,16,128]{2,1,0:T(8,128)S(1)}, f32[4,16,128]{2,1,0:T(8,128)S(1)}, u32[]{:S(2)}, u32[]{:S(2)}) collective-permute-start(f32[4,16,128]{2,1,0:T(8,128)S(1)} %get-tuple-element.46), channel_id=1, source_target_pairs={{0,24},{1,25},{2,26},{3,27},{4,28},{5,29},{6,30},{7,31},{8,16},{9,... | collective-permute-start | bytes 98312 | tf_op jit(solution)/shard_map/ppermute | solution.py:307
  59.7 0.0 collective-permute-start.15
  59.7 0.2 collective-permute-start.16
  60.0 0.0 collective-permute-done.12.refs_0_
  60.0 1.0 %collective-permute-start.17 = (f32[4,16,128]{2,1,0:T(8,128)S(1)}, f32[4,16,128]{2,1,0:T(8,128)S(1)}, u32[]{:S(2)}, u32[]{:S(2)}) collective-permute-start(f32[4,16,128]{2,1,0:T(8,128)S(1)} %get-tuple-element.49), channel_id=1, source_target_pairs={{0,1},{1,0},{2,3},{3,2},{4,5},{5,4},{6,7},{7,6},{8,9},{9,8},{10,11... | collective-permute-start | bytes 98312 | tf_op jit(solution)/shard_map/ppermute | solution.py:307
  60.9 1.9 %gram.1.moments_ref = f32[16,128]{1,0:T(8,128)S(1)} custom-call(bf16[48,4608]{1,0:T(8,128)(2,1)S(1)} %get-tuple-element.28.split_ref.split0, bf16[48,4608]{1,0:T(8,128)(2,1)S(1)} %get-tuple-element.36.split_ref.split1, bf16[48,4608]{1,0:T(8,128)(2,1)S(1)} %get-tuple-element.43.split_ref.split2), custom_call_target="tpu_custom_call" | custom-call | flops 1000000000 | bytes 4000000 | tf_op jit(solution)/shard_map/gram/pallas_call | solution.py:362
  62.8 1.6 %collective-permute-done.13.refs_1_ = f32[4,16,128]{2,1,0:T(8,128)S(1)} collective-permute-done((f32[4,16,128]{2,1,0:T(8,128)S(1)}, f32[4,16,128]{2,1,0:T(8,128)S(1)}, u32[]{:S(2)}, u32[]{:S(2)}) %collective-permute-start.13) | collective-permute-done | bytes 32800 | tf_op jit(solution)/shard_map/ppermute | solution.py:307
  64.4 0.2 collective-permute-done.14.refs_2_
  64.6 1.8 %last_link.1 = (bf16[48,4608]{1,0:T(8,128)(2,1)S(1)}, f32[32,16,128]{2,1,0:T(8,128)S(1)}) custom-call(s32[1,6,4]{2,1,0:T(8,128)S(1)} %copy.9.rows_ref, f32[32,16,128]{2,1,0:T(8,128)S(1)} %band.5.base_ref, bf16[6,2,256,256]{3,2,1,0:T(8,128)(2,1)S(1)} %get-tuple-element.29.links_ref, bf16[48,4608]{1,0:T(8,128)(2,1)S(1)} %get-tuple-element.43.split_ref.split2, ...), custom_call_target="tpu_custom_call" | custom-call | tf_op jit(solution)/shard_map/last_link/pallas_call | solution.py:372
  66.3 14.5 %all_to_all.5.gathered_ref = f32[32,16,128]{2,1,0:T(8,128)S(1)} all-to-all(f32[32,16,128]{2,1,0:T(8,128)S(1)} %get-tuple-element.50), channel_id=1, replica_groups=mesh['dom'=32] {'dom'}, dimensions={0} | all-to-all | bytes 524288 | tf_op jit(solution)/shard_map/all_to_all | solution.py:382
  80.9 5.9 %finish.1 = (f32[32,16,128]{2,1,0:T(8,128)}, f32[32,16,128]{2,1,0:T(8,128)}) custom-call(f32[32,16,128]{2,1,0:T(8,128)S(1)} %all_to_all.5.gathered_ref, bf16[48,4608]{1,0:T(8,128)(2,1)S(1)} %get-tuple-element.28.split_ref.split0, bf16[48,4608]{1,0:T(8,128)(2,1)S(1)} %get-tuple-element.36.split_ref.split1, ...), custom_call_target="tpu_custom_call" | custom-call | tf_op jit(solution)/shard_map/finish/pallas_call | solution.py:383
  (10 shorter events, 0.0 us)
Async XLA Ops:
  1.4 0.9 %copy-start.3 = (f32[32,16,128]{2,1,0:T(8,128)S(1)}, f32[32,16,128]{2,1,0:T(8,128)}, u32[]{:S(2)}) copy-start(f32[32,16,128]{2,1,0:T(8,128)} %field_ref.3) | copy-start | bytes 786436
  3.0 26.8 %collective-permute-start = (f32[4,16,128]{2,1,0:T(8,128)S(1)}, f32[4,16,128]{2,1,0:T(8,128)S(1)}, u32[]{:S(2)}, u32[]{:S(2)}) collective-permute-start(f32[4,16,128]{2,1,0:T(8,128)S(1)} %get-tuple-element.30), channel_id=1, source_target_pairs={{0,31},{1,2},{2,1},{3,4},{4,3},{5,6},{6,5},{7,8},{8,7},{9,10},{10,... | collective-permute-start | bytes 98312 | tf_op jit(solution)/shard_map/ppermute | solution.py:307
  9.5 27.9 %collective-permute-start.1 = (f32[4,16,128]{2,1,0:T(8,128)S(1)}, f32[4,16,128]{2,1,0:T(8,128)S(1)}, u32[]{:S(2)}, u32[]{:S(2)}) collective-permute-start(f32[4,16,128]{2,1,0:T(8,128)S(1)} %get-tuple-element.31), channel_id=1, source_target_pairs={{0,30},{1,31},{2,4},{3,5},{4,2},{5,3},{6,8},{7,9},{8,6},{9,7},{10,... | collective-permute-start | bytes 98312 | tf_op jit(solution)/shard_map/ppermute | solution.py:307
  10.1 27.3 %collective-permute-start.2 = (f32[4,16,128]{2,1,0:T(8,128)S(1)}, f32[4,16,128]{2,1,0:T(8,128)S(1)}, u32[]{:S(2)}, u32[]{:S(2)}) collective-permute-start(f32[4,16,128]{2,1,0:T(8,128)S(1)} %get-tuple-element.32), channel_id=1, source_target_pairs={{0,24},{1,25},{2,26},{3,27},{4,28},{5,29},{6,30},{7,31},{8,16},{9,... | collective-permute-start | bytes 98312 | tf_op jit(solution)/shard_map/ppermute | solution.py:307
  10.6 26.8 %collective-permute-start.3 = (f32[4,16,128]{2,1,0:T(8,128)S(1)}, f32[4,16,128]{2,1,0:T(8,128)S(1)}, u32[]{:S(2)}, u32[]{:S(2)}) collective-permute-start(f32[4,16,128]{2,1,0:T(8,128)S(1)} %get-tuple-element.33), channel_id=1, source_target_pairs={{0,8},{1,9},{2,10},{3,11},{4,12},{5,13},{6,14},{7,15},{8,0},{9,1},... | collective-permute-start | bytes 98312 | tf_op jit(solution)/shard_map/ppermute | solution.py:307
  10.6 26.8 %collective-permute-start.4 = (f32[4,16,128]{2,1,0:T(8,128)S(1)}, f32[4,16,128]{2,1,0:T(8,128)S(1)}, u32[]{:S(2)}, u32[]{:S(2)}) collective-permute-start(f32[4,16,128]{2,1,0:T(8,128)S(1)} %get-tuple-element.34), channel_id=1, source_target_pairs={{0,2},{1,3},{2,0},{3,1},{4,6},{5,7},{6,4},{7,5},{8,10},{9,11},{10,... | collective-permute-start | bytes 98312 | tf_op jit(solution)/shard_map/ppermute | solution.py:307
  12.0 4.0 %copy-start.1 = (f32[32,5,128,128]{3,2,1,0:T(8,128)S(1)}, f32[32,5,128,128]{3,2,1,0:T(8,128)}, u32[]{:S(2)}) copy-start(f32[32,5,128,128]{3,2,1,0:T(8,128)} %band_ref.1) | copy-start | bytes 31457284
  16.0 1.4 %copy-start.2 = (f32[1,6,4,128,128]{4,3,2,1,0:T(8,128)S(1)}, f32[1,6,4,128,128]{4,3,2,1,0:T(8,128)}, u32[]{:S(2)}) copy-start(f32[1,6,4,128,128]{4,3,2,1,0:T(8,128)} %link_ref.1) | copy-start | bytes 4718596
  17.4 0.9 %copy-start.4 = (f32[32,16,128]{2,1,0:T(8,128)S(1)}, f32[32,16,128]{2,1,0:T(8,128)}, u32[]{:S(2)}) copy-start(f32[32,16,128]{2,1,0:T(8,128)} %field_ref.3) | copy-start | bytes 786436
  29.8 7.6 %collective-permute-start.5 = (f32[4,16,128]{2,1,0:T(8,128)S(1)}, f32[4,16,128]{2,1,0:T(8,128)S(1)}, u32[]{:S(2)}, u32[]{:S(2)}) collective-permute-start(f32[4,16,128]{2,1,0:T(8,128)S(1)} %get-tuple-element.35), channel_id=1, source_target_pairs={{0,1},{1,0},{2,3},{3,2},{4,5},{5,4},{6,7},{7,6},{8,9},{9,8},{10,11... | collective-permute-start | bytes 98312 | tf_op jit(solution)/shard_map/ppermute | solution.py:307
  29.9 5.0 %copy-start = (bf16[18,12,128,256]{3,2,1,0:T(8,128)(2,1)S(1)}, bf16[18,12,128,256]{3,2,1,0:T(8,128)(2,1)}, u32[]{:S(2)}) copy-start(bf16[18,12,128,256]{3,2,1,0:T(8,128)(2,1)} %get-tuple-element.27.weights_ref) | copy-start | bytes 42467332
  38.5 9.3 %collective-permute-start.6 = (f32[4,16,128]{2,1,0:T(8,128)S(1)}, f32[4,16,128]{2,1,0:T(8,128)S(1)}, u32[]{:S(2)}, u32[]{:S(2)}) collective-permute-start(f32[4,16,128]{2,1,0:T(8,128)S(1)} %get-tuple-element.37), channel_id=1, source_target_pairs={{0,31},{1,2},{2,1},{3,4},{4,3},{5,6},{6,5},{7,8},{8,7},{9,10},{10,... | collective-permute-start | bytes 98312 | tf_op jit(solution)/shard_map/ppermute | solution.py:307
  41.8 8.5 %collective-permute-start.7 = (f32[4,16,128]{2,1,0:T(8,128)S(1)}, f32[4,16,128]{2,1,0:T(8,128)S(1)}, u32[]{:S(2)}, u32[]{:S(2)}) collective-permute-start(f32[4,16,128]{2,1,0:T(8,128)S(1)} %get-tuple-element.38), channel_id=1, source_target_pairs={{0,30},{1,31},{2,4},{3,5},{4,2},{5,3},{6,8},{7,9},{8,6},{9,7},{10,... | collective-permute-start | bytes 98312 | tf_op jit(solution)/shard_map/ppermute | solution.py:307
  43.8 6.5 %collective-permute-start.8 = (f32[4,16,128]{2,1,0:T(8,128)S(1)}, f32[4,16,128]{2,1,0:T(8,128)S(1)}, u32[]{:S(2)}, u32[]{:S(2)}) collective-permute-start(f32[4,16,128]{2,1,0:T(8,128)S(1)} %get-tuple-element.39), channel_id=1, source_target_pairs={{0,24},{1,25},{2,26},{3,27},{4,28},{5,29},{6,30},{7,31},{8,16},{9,... | collective-permute-start | bytes 98312 | tf_op jit(solution)/shard_map/ppermute | solution.py:307
  45.8 4.5 %collective-permute-start.9 = (f32[4,16,128]{2,1,0:T(8,128)S(1)}, f32[4,16,128]{2,1,0:T(8,128)S(1)}, u32[]{:S(2)}, u32[]{:S(2)}) collective-permute-start(f32[4,16,128]{2,1,0:T(8,128)S(1)} %get-tuple-element.40), channel_id=1, source_target_pairs={{0,8},{1,9},{2,10},{3,11},{4,12},{5,13},{6,14},{7,15},{8,0},{9,1},... | collective-permute-start | bytes 98312 | tf_op jit(solution)/shard_map/ppermute | solution.py:307
  47.9 3.9 %collective-permute-start.10 = (f32[4,16,128]{2,1,0:T(8,128)S(1)}, f32[4,16,128]{2,1,0:T(8,128)S(1)}, u32[]{:S(2)}, u32[]{:S(2)}) collective-permute-start(f32[4,16,128]{2,1,0:T(8,128)S(1)} %get-tuple-element.41), channel_id=1, source_target_pairs={{0,2},{1,3},{2,0},{3,1},{4,6},{5,7},{6,4},{7,5},{8,10},{9,11},{10,... | collective-permute-start | bytes 98312 | tf_op jit(solution)/shard_map/ppermute | solution.py:307
  47.9 3.9 %collective-permute-start.11 = (f32[4,16,128]{2,1,0:T(8,128)S(1)}, f32[4,16,128]{2,1,0:T(8,128)S(1)}, u32[]{:S(2)}, u32[]{:S(2)}) collective-permute-start(f32[4,16,128]{2,1,0:T(8,128)S(1)} %get-tuple-element.42), channel_id=1, source_target_pairs={{0,1},{1,0},{2,3},{3,2},{4,5},{5,4},{6,7},{7,6},{8,9},{9,8},{10,11... | collective-permute-start | bytes 98312 | tf_op jit(solution)/shard_map/ppermute | solution.py:307
  52.9 7.1 %collective-permute-start.12 = (f32[4,16,128]{2,1,0:T(8,128)S(1)}, f32[4,16,128]{2,1,0:T(8,128)S(1)}, u32[]{:S(2)}, u32[]{:S(2)}) collective-permute-start(f32[4,16,128]{2,1,0:T(8,128)S(1)} %get-tuple-element.44), channel_id=1, source_target_pairs={{0,31},{1,2},{2,1},{3,4},{4,3},{5,6},{6,5},{7,8},{8,7},{9,10},{10,... | collective-permute-start | bytes 98312 | tf_op jit(solution)/shard_map/ppermute | solution.py:307
  56.8 7.6 %collective-permute-start.13 = (f32[4,16,128]{2,1,0:T(8,128)S(1)}, f32[4,16,128]{2,1,0:T(8,128)S(1)}, u32[]{:S(2)}, u32[]{:S(2)}) collective-permute-start(f32[4,16,128]{2,1,0:T(8,128)S(1)} %get-tuple-element.45), channel_id=1, source_target_pairs={{0,30},{1,31},{2,4},{3,5},{4,2},{5,3},{6,8},{7,9},{8,6},{9,7},{10,... | collective-permute-start | bytes 98312 | tf_op jit(solution)/shard_map/ppermute | solution.py:307
  58.8 5.7 %collective-permute-start.14 = (f32[4,16,128]{2,1,0:T(8,128)S(1)}, f32[4,16,128]{2,1,0:T(8,128)S(1)}, u32[]{:S(2)}, u32[]{:S(2)}) collective-permute-start(f32[4,16,128]{2,1,0:T(8,128)S(1)} %get-tuple-element.46), channel_id=1, source_target_pairs={{0,24},{1,25},{2,26},{3,27},{4,28},{5,29},{6,30},{7,31},{8,16},{9,... | collective-permute-start | bytes 98312 | tf_op jit(solution)/shard_map/ppermute | solution.py:307
  59.7 4.8 %collective-permute-start.15 = (f32[4,16,128]{2,1,0:T(8,128)S(1)}, f32[4,16,128]{2,1,0:T(8,128)S(1)}, u32[]{:S(2)}, u32[]{:S(2)}) collective-permute-start(f32[4,16,128]{2,1,0:T(8,128)S(1)} %get-tuple-element.47), channel_id=1, source_target_pairs={{0,8},{1,9},{2,10},{3,11},{4,12},{5,13},{6,14},{7,15},{8,0},{9,1},... | collective-permute-start | bytes 98312 | tf_op jit(solution)/shard_map/ppermute | solution.py:307
  59.7 4.8 %collective-permute-start.16 = (f32[4,16,128]{2,1,0:T(8,128)S(1)}, f32[4,16,128]{2,1,0:T(8,128)S(1)}, u32[]{:S(2)}, u32[]{:S(2)}) collective-permute-start(f32[4,16,128]{2,1,0:T(8,128)S(1)} %get-tuple-element.48), channel_id=1, source_target_pairs={{0,2},{1,3},{2,0},{3,1},{4,6},{5,7},{6,4},{7,5},{8,10},{9,11},{10,... | collective-permute-start | bytes 98312 | tf_op jit(solution)/shard_map/ppermute | solution.py:307
  60.0 4.6 %collective-permute-start.17 = (f32[4,16,128]{2,1,0:T(8,128)S(1)}, f32[4,16,128]{2,1,0:T(8,128)S(1)}, u32[]{:S(2)}, u32[]{:S(2)}) collective-permute-start(f32[4,16,128]{2,1,0:T(8,128)S(1)} %get-tuple-element.49), channel_id=1, source_target_pairs={{0,1},{1,0},{2,3},{3,2},{4,5},{5,4},{6,7},{7,6},{8,9},{9,8},{10,11... | collective-permute-start | bytes 98312 | tf_op jit(solution)/shard_map/ppermute | solution.py:307
where the time goes:
time: 87 us; the launch traced here: 86.7 us
  Pallas kernels  31.1 us (36%)
  starting transfers between devices  24 us (28%)
  blocking collectives  14.5 us (17%)
  local copies, waits for them, and re-layouts  13.1 us (15%)
  waiting for transfers between devices  3.23 us (4%)
    ppermute x18, starting transfers between devices, exchange(): lax.ppermute(messages[index], 'dom', matching_pairs(dev_count, pair, phase))  24 us
    all_to_all x1, blocking collectives, shards(): gathered = lax.all_to_all(mine, 'dom', 0, 0)  14.5 us
    unnamed x11, local copies, waits for them, and re-layouts  13.1 us
    pallas_call x1, Pallas kernels, shards(): pl.pallas_call(functools.partial(prepare_kernel, half), out_shape=[jax.Sh...  11.5 us
    pallas_call x3, Pallas kernels, shards(): pl.pallas_call(band_kernel, out_shape=field, in_specs=vmem(2), out_specs=...  7.29 us
    pallas_call x1, Pallas kernels, shards(): pl.pallas_call(functools.partial(finish_kernel, half), out_shape=[field,...  5.85 us
    ppermute x18, waiting for transfers between devices, exchange(): lax.ppermute(messages[index], 'dom', matching_pairs(dev_count, pair, phase))  3.23 us
    pallas_call x2, Pallas kernels, shards(): pl.pallas_call(functools.partial(link_kernel, dev_count, half), out_shape...  2.19 us
  transfers between devices with their start and end apart: 18, of which 3 were waited for; matrix products, arithmetic and copies ran while one was open for 0% of the time, Pallas kernels for 24%

commit v1 on v0

--- a/solution.py
+++ b/solution.py
@@ -59,8 +59,8 @@
     block_rows = field_ref.shape[0]
     for (pair, phase), out_ref in zip(MATCHINGS, out_refs):
         face = matching_face(dev_count, pair, phase)
-        for slot in range(rows_ref.shape[2]):
-            row = jnp.minimum(rows_ref[0, face, slot], block_rows - 1)
+        for slot in range(rows_ref.shape[1]):
+            row = jnp.minimum(rows_ref[0, slot, face], block_rows - 1)
             out_ref[slot] = field_ref[row]
 
 
@@ -75,68 +75,97 @@
             split_ref[piece * width : (piece + 1) * width, cols] = value
 
 
-def first_send_kernel(dev_count, rows_ref, field_ref, *out_refs):
-    send_rows(dev_count, rows_ref, field_ref, out_refs)
-
-
-def prepare_kernel(half, field_ref, band_ref, link_ref, weights_ref, links_ref, split_ref, held, sems, link_held, link_sem):
+def first_send_kernel(dev_count, rows_ref, field_ref, *refs):
+    out_refs, sems = refs[:-1], refs[-1]
+    block_rows = field_ref.shape[0]
+    copies = []
+    for hop, ((pair, phase), out_ref) in enumerate(zip(MATCHINGS, out_refs)):
+        face = matching_face(dev_count, pair, phase)
+        for slot in range(rows_ref.shape[1]):
+            row = jnp.minimum(rows_ref[0, slot, face], block_rows - 1)
+            copies.append(pltpu.make_async_copy(field_ref.at[row], out_ref.at[slot], sems.at[hop, slot]))
+            copies[-1].start()
+    for copy in copies:
+        copy.wait()
+
+
+def fold(value, width):
+    total = value[(PIECES - 1) * width : PIECES * width]
+    for piece in range(PIECES - 2, -1, -1):
+        total = total + value[piece * width : (piece + 1) * width]
+    return total
+
+
+def pair_product(weights_ref, split_ref, out_ref, pair):
+    _, width, size = out_ref.shape
+    depth = weights_ref.shape[1] * size
+    start = pl.multiple_of(pair * 2 * size, 2 * size)
+    rows = split_ref[:, pl.ds(start, depth // 2)]
+    both = jnp.concatenate([rows, rows], axis=1)
+    weights = weights_ref[pair + 1].reshape(depth, 2 * size)
+    total = fold(jnp.dot(both, weights, preferred_element_type=F32), width)
+    out_ref[2 * pair] = total[:, :size]
+    out_ref[2 * pair + 1] = total[:, size:]
+
+
+def band_kernel(weights_ref, split_ref, out_ref):
+    def body(pair, carry):
+        pair_product(weights_ref, split_ref, out_ref, pair)
+        return carry
+
+    lax.fori_loop(0, out_ref.shape[0] // 2, body, 0, unroll=4)
+
+
+def prepare_kernel(
+    half, field_hbm, band_hbm, link_hbm, weights_ref, links_ref, split_ref, out_ref, field_ref, band_ref, link_ref, sems
+):
     block_rows, band, size, _ = band_ref.shape
+    faces, count = link_ref.shape[:2]
     pairs = block_rows // 2
     span = band + 1
-    slots = held.shape[0]
-
-    def fetch(row, slot):
-        return pltpu.make_async_copy(band_ref.at[row], held.at[slot], sems.at[slot])
-
-    link_copy = pltpu.make_async_copy(link_ref.at[0], link_held, link_sem)
-    for row in range(slots):
-        fetch(row, row).start()
-    link_copy.start()
-    split_field(field_ref, split_ref, half)
-    zero = jnp.zeros((size, size), BF16)
-
-    def clear(pair, carry):
-        for copy in range(2):
-            weights_ref[pair, copy * span, :, size:] = zero
-            weights_ref[pair, copy * span + span - 1, :, :size] = zero
-        return carry
-
-    lax.fori_loop(0, pairs + 2, clear, 0)
+    copies = [pltpu.make_async_copy(field_hbm, field_ref, sems.at[pairs])]
+    copies += [
+        pltpu.make_async_copy(band_hbm.at[pl.ds(2 * pair, 2)], band_ref.at[pl.ds(2 * pair, 2)], sems.at[pair])
+        for pair in range(pairs)
+    ]
+    copies.append(pltpu.make_async_copy(link_hbm.at[0], link_ref, sems.at[pairs + 1]))
+    for copy in copies:
+        copy.start()
     wide = jnp.zeros((size, 2 * size), BF16)
     for copy in range(2):
         for place in range(half):
             weights_ref[1, copy * span + place] = wide
             weights_ref[pairs, copy * span + span - 1 - place] = wide
+        for pair in range(1, pairs + 1):
+            weights_ref[pair, copy * span, :, size:] = wide[:, :size]
+            weights_ref[pair, copy * span + span - 1, :, :size] = wide[:, :size]
+    copies[0].wait()
+    split_field(field_ref, split_ref, half)
 
     def convert(step, carry):
-        for even in range(slots):
-            row = slots * step + even
-            fetch(row, even).wait()
-            base = slots // 2 * step + even // 2
+        here = pl.ds(2 * step, 2)
+        pltpu.make_async_copy(band_hbm.at[here], band_ref.at[here], sems.at[step]).wait()
+        for even in range(2):
             for k in range(band):
-                shift = (even % 2 + k - half) // 2
-                col = (even % 2 + k - half) % 2
-                place = even % 2 + half - 2 * shift
-                block = held[even, k]
+                shift = (even + k - half) // 2
+                col = (even + k - half) % 2
+                place = even + half - 2 * shift
+                block = band_ref[2 * step + even, k]
                 high = block.astype(BF16)
                 low = (block - high.astype(F32)).astype(BF16)
                 cols = slice(col * size, (col + 1) * size)
-                weights_ref[base + shift + 1, place, :, cols] = high
-                weights_ref[base + shift + 1, span + place, :, cols] = low
-
-            @pl.when(row + slots < block_rows)
-            def _():
-                fetch(row + slots, even).start()
-
+                weights_ref[step + shift + 1, place, :, cols] = high
+                weights_ref[step + shift + 1, span + place, :, cols] = low
+        pair_product(weights_ref, split_ref, out_ref, jnp.maximum(step - 1, 0))
         return carry
 
-    lax.fori_loop(0, block_rows // slots, convert, 0)
-    link_copy.wait()
-    faces, count = link_held.shape[0], link_held.shape[1]
+    lax.fori_loop(0, pairs, convert, 0)
+    pair_product(weights_ref, split_ref, out_ref, pairs - 1)
+    copies[-1].wait()
 
     def convert_links(face, carry):
         for slot in range(count):
-            block = link_held[face, slot].T
+            block = link_ref[face, slot].T
             high = block.astype(BF16)
             low = (block - high.astype(F32)).astype(BF16)
             cols = slice(slot % 2 * size, (slot % 2 + 1) * size)
@@ -145,32 +174,6 @@
         return carry
 
     lax.fori_loop(0, faces, convert_links, 0)
-
-
-def fold(value, width):
-    total = value[(PIECES - 1) * width : PIECES * width]
-    for piece in range(PIECES - 2, -1, -1):
-        total = total + value[piece * width : (piece + 1) * width]
-    return total
-
-
-def band_kernel(weights_ref, split_ref, out_ref):
-    block_rows, width, size = out_ref.shape
-    pairs = block_rows // 2
-    depth = weights_ref.shape[1] * size
-    span = depth // 2
-
-    def pair_product(pair, carry):
-        start = pl.multiple_of(pair * 2 * size, 2 * size)
-        rows = split_ref[:, pl.ds(start, span)]
-        both = jnp.concatenate([rows, rows], axis=1)
-        weights = weights_ref[pair + 1].reshape(depth, 2 * size)
-        total = fold(jnp.dot(both, weights, preferred_element_type=F32), width)
-        out_ref[2 * pair] = total[:, :size]
-        out_ref[2 * pair + 1] = total[:, size:]
-        return carry
-
-    lax.fori_loop(0, pairs, pair_product, 0, unroll=4)
 
 
 def add_links(dev_count, rows_ref, base_ref, links_ref, far_refs, field_ref):
@@ -187,7 +190,7 @@
             product = jnp.dot(both, links_ref[face, two], preferred_element_type=F32)
             for k in range(2):
                 part = product[k * PIECES * width : (k + 1) * PIECES * width, k * size : (k + 1) * size]
-                row = jnp.minimum(rows_ref[0, face, 2 * two + k], block_rows - 1)
+                row = jnp.minimum(rows_ref[0, 2 * two + k, face], block_rows - 1)
                 field_ref[row] = field_ref[row] + fold(part, width)
 
 
@@ -307,46 +310,54 @@
             got.append(lax.ppermute(messages[index], "dom", matching_pairs(dev_count, pair, phase)))
         return got
 
+    hbm = [pl.BlockSpec(memory_space=pltpu.HBM)]
+    right_side, band_blocks, link_blocks = (
+        pltpu.with_memory_space_constraint(value, pltpu.HBM) for value in (right_side, band_blocks, link_blocks)
+    )
+    slot_rows = jnp.swapaxes(link_rows, 1, 2)
     messages = pl.pallas_call(
         functools.partial(first_send_kernel, dev_count),
         out_shape=[message] * count,
-        in_specs=[smem()] + vmem(1),
+        in_specs=[smem()] + hbm,
         out_specs=vmem(count),
+        scratch_shapes=[pltpu.SemaphoreType.DMA((count, slots))],
         compiler_params=params(8),
         name="first_send",
-    )(link_rows, right_side)
+    )(slot_rows, right_side)
     far = exchange(messages)
-    weights, links, split0 = pl.pallas_call(
+    weights, links, split0, base = pl.pallas_call(
         functools.partial(prepare_kernel, half),
         out_shape=[
-            jax.ShapeDtypeStruct((pairs + 2, 2 * (band + 1), size, 2 * size), BF16),
-            jax.ShapeDtypeStruct((faces, slots // 2, 2 * size, 2 * size), BF16),
+            pltpu.VMEM((pairs + 2, 2 * (band + 1), size, 2 * size), BF16),
+            pltpu.VMEM((faces, slots // 2, 2 * size, 2 * size), BF16),
             split,
+            field,
         ],
-        in_specs=vmem(1) + [pl.BlockSpec(memory_space=pl.ANY)] * 2,
-        out_specs=vmem(3),
+        in_specs=hbm * 3,
+        out_specs=vmem(4),
         scratch_shapes=[
-            pltpu.VMEM((4, band, size, size), F32),
-            pltpu.SemaphoreType.DMA((4,)),
-            pltpu.VMEM((faces, slots, size, size), F32),
-            pltpu.SemaphoreType.DMA,
+            pltpu.VMEM(right_side.shape, F32),
+            pltpu.VMEM(band_blocks.shape, F32),
+            pltpu.VMEM(link_blocks.shape[1:], F32),
+            pltpu.SemaphoreType.DMA((pairs + 2,)),
         ],
-        compiler_params=params(28),
-        cost_estimate=pl.CostEstimate(flops=10**7, bytes_accessed=12 * 10**6, transcendentals=0),
+        compiler_params=params(18),
+        cost_estimate=pl.CostEstimate(flops=10**9, bytes_accessed=12 * 10**6, transcendentals=0),
         name="prepare",
     )(right_side, band_blocks, link_blocks)
 
     splits = [split0]
     for level in range(ITERS):
-        base = pl.pallas_call(
-            band_kernel,
-            out_shape=field,
-            in_specs=vmem(2),
-            out_specs=vmem(1)[0],
-            compiler_params=params(24),
-            cost_estimate=pl.CostEstimate(flops=10**9, bytes_accessed=12 * 10**6, transcendentals=0),
-            name="band",
-        )(weights, splits[-1])
+        if level > 0:
+            base = pl.pallas_call(
+                band_kernel,
+                out_shape=field,
+                in_specs=vmem(2),
+                out_specs=vmem(1)[0],
+                compiler_params=params(8),
+                cost_estimate=pl.CostEstimate(flops=10**9, bytes_accessed=12 * 10**6, transcendentals=0),
+                name="band",
+            )(weights, splits[-1])
         if level + 1 < ITERS:
             outs = pl.pallas_call(
                 functools.partial(link_kernel, dev_count, half),
@@ -354,9 +365,9 @@
                 in_specs=[smem()] + vmem(2 + count),
                 out_specs=vmem(1 + count),
                 scratch_shapes=[pltpu.VMEM(right_side.shape, F32)],
-                compiler_params=params(12),
+                compiler_params=params(8),
                 name="link",
-            )(link_rows, base, links, *far)
+            )(slot_rows, base, links, *far)
             splits.append(outs[0])
             far = exchange(outs[1:])
     moments = pl.pallas_call(
@@ -375,9 +386,9 @@
         in_specs=[smem()] + vmem(4 + count),
         out_specs=vmem(2),
         scratch_shapes=[pltpu.VMEM(right_side.shape, F32)],
-        compiler_params=params(12),
+        compiler_params=params(8),
         name="last_link",
-    )(link_rows, base, links, splits[-1], moments, *far)
+    )(slot_rows, base, links, splits[-1], moments, *far)
     splits.append(split3)
     gathered = lax.all_to_all(mine, "dom", 0, 0)
     return pl.pallas_call(
@@ -385,7 +396,7 @@
         out_shape=[field, field],
         in_specs=vmem(1 + LEVELS),
         out_specs=vmem(2),
-        compiler_params=params(12),
+        compiler_params=params(8),
         name="finish",
     )(gathered, *splits)
 

time: 87 us -> 70 us (0.80)
  local copies, waits for them, and re-layouts: 13.1 us -> 0.68 us
  Pallas kernels: 31.1 us -> 26.6 us
    unnamed x11 -> x4, local copies, waits for them, and re-layouts: 13.1 us -> 0.68 us
    pallas_call x1, Pallas kernels: 11.5 us -> 8.17 us  [shards(): pl.pallas_call(functools.partial(prepare_kernel, half), out_shape=[pltpu....]
    pallas_call x3 -> x2, Pallas kernels: 7.29 us -> 4.86 us  [shards(): pl.pallas_call(band_kernel, out_shape=field, in_specs=vmem(2), out_specs=...]
    pallas_call x1, Pallas kernels: 0.66 us -> 1.97 us  [shards(): pl.pallas_call(functools.partial(first_send_kernel, dev_count), out_shape...]
  transfers between devices with their start and end apart: 18 -> 18, of which waited for: 3 -> 5; matrix products, arithmetic and copies ran while one was open for 0% -> 0% of each run, Pallas kernels for 24% -> 21%
where the time goes in v1:
time: 70 us; the launch traced here: 69.8 us
  Pallas kernels  26.6 us (38%)
  starting transfers between devices  24.1 us (34%)
  blocking collectives  14.2 us (20%)
  waiting for transfers between devices  3.52 us (5%)
  between operations  0.75 us (1%)
    ppermute x18, starting transfers between devices, exchange(): lax.ppermute(messages[index], 'dom', matching_pairs(dev_count, pair, phase))  24.1 us
    all_to_all x1, blocking collectives, shards(): gathered = lax.all_to_all(mine, 'dom', 0, 0)  14.2 us
    pallas_call x1, Pallas kernels, shards(): pl.pallas_call(functools.partial(prepare_kernel, half), out_shape=[pltpu....  8.17 us
    pallas_call x1, Pallas kernels, shards(): pl.pallas_call(functools.partial(finish_kernel, half), out_shape=[field,...  5.86 us
    pallas_call x2, Pallas kernels, shards(): pl.pallas_call(band_kernel, out_shape=field, in_specs=vmem(2), out_specs=...  4.86 us
    ppermute x18, waiting for transfers between devices, exchange(): lax.ppermute(messages[index], 'dom', matching_pairs(dev_count, pair, phase))  3.52 us
    pallas_call x2, Pallas kernels, shards(): pl.pallas_call(functools.partial(link_kernel, dev_count, half), out_shape...  2.13 us
    pallas_call x1, Pallas kernels, shards(): pl.pallas_call(functools.partial(first_send_kernel, dev_count), out_shape...  1.97 us
  transfers between devices with their start and end apart: 18, of which 5 were waited for; matrix products, arithmetic and copies ran while one was open for 0% of the time, Pallas kernels for 21%

profile of v1, /device:TPU:0, one launch (start us, length us, event | category | flops | bytes accessed | tf_op | source)
XLA Modules:
  0.0 69.8 jit_solution(6965610442549890549)
XLA Ops:
  0.6 0.0 copy-start
  0.6 0.7 copy-done
  1.3 2.0 %first_send.1 = (f32[4,16,128]{2,1,0:T(8,128)S(1)}, f32[4,16,128]{2,1,0:T(8,128)S(1)}, f32[4,16,128]{2,1,0:T(8,128)S(1)}, f32[4,16,128]{2,1,0:T(8,128)S(1)}, f32...) custom-call(s32[1,4,6]{2,1,0:T(4,128)S(1)} %bitcast.1, f32[32,16,128]{2,1,0:T(8,128)} %field_ref.1), custom_call_target="tpu_custom_call" | custom-call | tf_op jit(solution)/shard_map/first_send/pallas_call | solution.py:318
  3.3 6.5 %collective-permute-start = (f32[4,16,128]{2,1,0:T(8,128)S(1)}, f32[4,16,128]{2,1,0:T(8,128)S(1)}, u32[]{:S(2)}, u32[]{:S(2)}) collective-permute-start(f32[4,16,128]{2,1,0:T(8,128)S(1)} %get-tuple-element.31), channel_id=1, source_target_pairs={{0,31},{1,2},{2,1},{3,4},{4,3},{5,6},{6,5},{7,8},{8,7},{9,10},{10,... | collective-permute-start | bytes 98312 | tf_op jit(solution)/shard_map/ppermute | solution.py:310
  9.8 0.5 collective-permute-start.1
  10.3 0.5 collective-permute-start.2
  10.8 0.0 collective-permute-start.3
  10.8 1.4 %collective-permute-start.4 = (f32[4,16,128]{2,1,0:T(8,128)S(1)}, f32[4,16,128]{2,1,0:T(8,128)S(1)}, u32[]{:S(2)}, u32[]{:S(2)}) collective-permute-start(f32[4,16,128]{2,1,0:T(8,128)S(1)} %get-tuple-element.35), channel_id=1, source_target_pairs={{0,2},{1,3},{2,0},{3,1},{4,6},{5,7},{6,4},{7,5},{8,10},{9,11},{10,... | collective-permute-start | bytes 98312 | tf_op jit(solution)/shard_map/ppermute | solution.py:310
  12.2 0.0 collective-permute-done.refs_0_
  12.2 0.0 collective-permute-start.5
  12.2 8.2 %prepare.1 = (bf16[18,12,128,256]{3,2,1,0:T(8,128)(2,1)S(1)}, bf16[6,2,256,256]{3,2,1,0:T(8,128)(2,1)S(1)}, bf16[48,4608]{1,0:T(8,128)(2,1)S(1)}, f32[32,16,128]{2,1,0:T(8,128)S(1)}) custom-call(f32[32,16,128]{2,1,0:T(8,128)} %field_ref.1, f32[32,5,128,128]{3,2,1,0:T(8,128)} %band_hbm.1, f32[1,6,4,128,128]{4,3,2,1,0:T(8,128)} %link_hbm.1), custom_call_target="tpu_custom_call" | custom-call | flops 1000000000 | bytes 12000000 | tf_op jit(solution)/shard_map/prepare/pallas_call | solution.py:328
  20.4 0.0 collective-permute-done.1.refs_1_
  20.4 0.0 collective-permute-done.2.refs_2_
  20.4 0.0 collective-permute-done.3.refs_3_
  20.4 0.0 collective-permute-done.4.refs_4_
  20.4 0.0 collective-permute-done.5.refs_5_
  20.5 1.1 %link.2 = (bf16[48,4608]{1,0:T(8,128)(2,1)S(1)}, f32[4,16,128]{2,1,0:T(8,128)S(1)}, f32[4,16,128]{2,1,0:T(8,128)S(1)}, f32[4,16,128]{2,1,0:T(8,128)S(1)}, f32[4,...) custom-call(s32[1,4,6]{2,1,0:T(4,128)S(1)} %bitcast.2, ...), custom_call_target="tpu_custom_call" | custom-call | tf_op jit(solution)/shard_map/link/pallas_call | solution.py:362
  21.5 4.6 %collective-permute-start.6 = (f32[4,16,128]{2,1,0:T(8,128)S(1)}, f32[4,16,128]{2,1,0:T(8,128)S(1)}, u32[]{:S(2)}, u32[]{:S(2)}) collective-permute-start(f32[4,16,128]{2,1,0:T(8,128)S(1)} %get-tuple-element.38), channel_id=1, source_target_pairs={{0,31},{1,2},{2,1},{3,4},{4,3},{5,6},{6,5},{7,8},{8,7},{9,10},{10,... | collective-permute-start | bytes 98312 | tf_op jit(solution)/shard_map/ppermute | solution.py:310
  26.2 0.7 %collective-permute-start.7 = (f32[4,16,128]{2,1,0:T(8,128)S(1)}, f32[4,16,128]{2,1,0:T(8,128)S(1)}, u32[]{:S(2)}, u32[]{:S(2)}) collective-permute-start(f32[4,16,128]{2,1,0:T(8,128)S(1)} %get-tuple-element.39), channel_id=1, source_target_pairs={{0,30},{1,31},{2,4},{3,5},{4,2},{5,3},{6,8},{7,9},{8,6},{9,7},{10,... | collective-permute-start | bytes 98312 | tf_op jit(solution)/shard_map/ppermute | solution.py:310
  26.9 2.1 %collective-permute-start.8 = (f32[4,16,128]{2,1,0:T(8,128)S(1)}, f32[4,16,128]{2,1,0:T(8,128)S(1)}, u32[]{:S(2)}, u32[]{:S(2)}) collective-permute-start(f32[4,16,128]{2,1,0:T(8,128)S(1)} %get-tuple-element.40), channel_id=1, source_target_pairs={{0,24},{1,25},{2,26},{3,27},{4,28},{5,29},{6,30},{7,31},{8,16},{9,... | collective-permute-start | bytes 98312 | tf_op jit(solution)/shard_map/ppermute | solution.py:310
  29.0 2.0 %collective-permute-start.9 = (f32[4,16,128]{2,1,0:T(8,128)S(1)}, f32[4,16,128]{2,1,0:T(8,128)S(1)}, u32[]{:S(2)}, u32[]{:S(2)}) collective-permute-start(f32[4,16,128]{2,1,0:T(8,128)S(1)} %get-tuple-element.41), channel_id=1, source_target_pairs={{0,8},{1,9},{2,10},{3,11},{4,12},{5,13},{6,14},{7,15},{8,0},{9,1},... | collective-permute-start | bytes 98312 | tf_op jit(solution)/shard_map/ppermute | solution.py:310
  31.0 0.0 collective-permute-start.10
  31.0 0.0 collective-permute-done.6.refs_0_
  31.0 0.0 collective-permute-start.11
  31.0 2.4 %band.2.base_ref = f32[32,16,128]{2,1,0:T(8,128)S(1)} custom-call(bf16[18,12,128,256]{3,2,1,0:T(8,128)(2,1)S(1)} %get-tuple-element.28.weights_ref, bf16[48,4608]{1,0:T(8,128)(2,1)S(1)} %get-tuple-element.37.split_ref.split1), custom_call_target="tpu_custom_call" | custom-call | flops 1000000000 | bytes 12000000 | tf_op jit(solution)/shard_map/band/pallas_call | solution.py:352
  33.5 0.2 collective-permute-done.7.refs_1_
  33.7 0.0 collective-permute-done.8.refs_2_
  33.7 0.0 collective-permute-done.9.refs_3_
  33.7 1.2 %collective-permute-done.10.refs_4_ = f32[4,16,128]{2,1,0:T(8,128)S(1)} collective-permute-done((f32[4,16,128]{2,1,0:T(8,128)S(1)}, f32[4,16,128]{2,1,0:T(8,128)S(1)}, u32[]{:S(2)}, u32[]{:S(2)}) %collective-permute-start.10) | collective-permute-done | bytes 32800 | tf_op jit(solution)/shard_map/ppermute | solution.py:310
  34.9 0.0 collective-permute-done.11.refs_5_
  34.9 1.1 %link.3 = (bf16[48,4608]{1,0:T(8,128)(2,1)S(1)}, f32[4,16,128]{2,1,0:T(8,128)S(1)}, f32[4,16,128]{2,1,0:T(8,128)S(1)}, f32[4,16,128]{2,1,0:T(8,128)S(1)}, f32[4,...) custom-call(s32[1,4,6]{2,1,0:T(4,128)S(1)} %bitcast.3, ...), custom_call_target="tpu_custom_call" | custom-call | tf_op jit(solution)/shard_map/link/pallas_call | solution.py:362
  36.0 1.4 %collective-permute-start.12 = (f32[4,16,128]{2,1,0:T(8,128)S(1)}, f32[4,16,128]{2,1,0:T(8,128)S(1)}, u32[]{:S(2)}, u32[]{:S(2)}) collective-permute-start(f32[4,16,128]{2,1,0:T(8,128)S(1)} %get-tuple-element.46), channel_id=1, source_target_pairs={{0,31},{1,2},{2,1},{3,4},{4,3},{5,6},{6,5},{7,8},{8,7},{9,10},{10,... | collective-permute-start | bytes 98312 | tf_op jit(solution)/shard_map/ppermute | solution.py:310
  37.4 2.4 %band.3.base_ref = f32[32,16,128]{2,1,0:T(8,128)S(1)} custom-call(bf16[18,12,128,256]{3,2,1,0:T(8,128)(2,1)S(1)} %get-tuple-element.28.weights_ref, bf16[48,4608]{1,0:T(8,128)(2,1)S(1)} %get-tuple-element.44.split_ref.split2), custom_call_target="tpu_custom_call" | custom-call | flops 1000000000 | bytes 12000000 | tf_op jit(solution)/shard_map/band/pallas_call | solution.py:352
  39.8 2.1 %collective-permute-start.13 = (f32[4,16,128]{2,1,0:T(8,128)S(1)}, f32[4,16,128]{2,1,0:T(8,128)S(1)}, u32[]{:S(2)}, u32[]{:S(2)}) collective-permute-start(f32[4,16,128]{2,1,0:T(8,128)S(1)} %get-tuple-element.47), channel_id=1, source_target_pairs={{0,30},{1,31},{2,4},{3,5},{4,2},{5,3},{6,8},{7,9},{8,6},{9,7},{10,... | collective-permute-start | bytes 98312 | tf_op jit(solution)/shard_map/ppermute | solution.py:310
  41.9 1.0 %collective-permute-start.14 = (f32[4,16,128]{2,1,0:T(8,128)S(1)}, f32[4,16,128]{2,1,0:T(8,128)S(1)}, u32[]{:S(2)}, u32[]{:S(2)}) collective-permute-start(f32[4,16,128]{2,1,0:T(8,128)S(1)} %get-tuple-element.48), channel_id=1, source_target_pairs={{0,24},{1,25},{2,26},{3,27},{4,28},{5,29},{6,30},{7,31},{8,16},{9,... | collective-permute-start | bytes 98312 | tf_op jit(solution)/shard_map/ppermute | solution.py:310
  42.9 1.1 %collective-permute-start.15 = (f32[4,16,128]{2,1,0:T(8,128)S(1)}, f32[4,16,128]{2,1,0:T(8,128)S(1)}, u32[]{:S(2)}, u32[]{:S(2)}) collective-permute-start(f32[4,16,128]{2,1,0:T(8,128)S(1)} %get-tuple-element.49), channel_id=1, source_target_pairs={{0,8},{1,9},{2,10},{3,11},{4,12},{5,13},{6,14},{7,15},{8,0},{9,1},... | collective-permute-start | bytes 98312 | tf_op jit(solution)/shard_map/ppermute | solution.py:310
  44.1 0.0 collective-permute-start.16
  44.1 0.0 collective-permute-done.12.refs_0_
  44.1 0.0 collective-permute-start.17
  44.1 1.9 %gram.1.moments_ref = f32[16,128]{1,0:T(8,128)S(1)} custom-call(bf16[48,4608]{1,0:T(8,128)(2,1)S(1)} %get-tuple-element.45.split0, bf16[48,4608]{1,0:T(8,128)(2,1)S(1)} %get-tuple-element.37.split_ref.split1, bf16[48,4608]{1,0:T(8,128)(2,1)S(1)} %get-tuple-element.44.split_ref.split2), custom_call_target="tpu_custom_call" | custom-call | flops 1000000000 | bytes 4000000 | tf_op jit(solution)/shard_map/gram/pallas_call | solution.py:373
  45.9 1.6 %collective-permute-done.13.refs_1_ = f32[4,16,128]{2,1,0:T(8,128)S(1)} collective-permute-done((f32[4,16,128]{2,1,0:T(8,128)S(1)}, f32[4,16,128]{2,1,0:T(8,128)S(1)}, u32[]{:S(2)}, u32[]{:S(2)}) %collective-permute-start.13) | collective-permute-done | bytes 32800 | tf_op jit(solution)/shard_map/ppermute | solution.py:310
  47.5 0.2 collective-permute-done.14.refs_2_
  47.6 0.0 collective-permute-done.15.refs_3_
  47.6 0.3 collective-permute-done.16.refs_4_
  48.0 0.0 collective-permute-done.17.refs_5_
  48.0 1.7 %last_link.1 = (bf16[48,4608]{1,0:T(8,128)(2,1)S(1)}, f32[32,16,128]{2,1,0:T(8,128)S(1)}) custom-call(s32[1,4,6]{2,1,0:T(4,128)S(1)} %bitcast.4, f32[32,16,128]{2,1,0:T(8,128)S(1)} %band.3.base_ref, bf16[6,2,256,256]{3,2,1,0:T(8,128)(2,1)S(1)} %get-tuple-element.30.links_ref, bf16[48,4608]{1,0:T(8,128)(2,1)S(1)} %get-tuple-element.44.split_ref.split2, ...), custom_call_target="tpu_custom_call" | custom-call | tf_op jit(solution)/shard_map/last_link/pallas_call | solution.py:383
  49.7 14.2 %all_to_all.5.gathered_ref = f32[32,16,128]{2,1,0:T(8,128)S(1)} all-to-all(f32[32,16,128]{2,1,0:T(8,128)S(1)} %get-tuple-element.52), channel_id=1, replica_groups=mesh['dom'=32] {'dom'}, dimensions={0} | all-to-all | bytes 524288 | tf_op jit(solution)/shard_map/all_to_all | solution.py:393
  63.9 5.9 %finish.1 = (f32[32,16,128]{2,1,0:T(8,128)}, f32[32,16,128]{2,1,0:T(8,128)}) custom-call(f32[32,16,128]{2,1,0:T(8,128)S(1)} %all_to_all.5.gathered_ref, bf16[48,4608]{1,0:T(8,128)(2,1)S(1)} %get-tuple-element.45.split0, bf16[48,4608]{1,0:T(8,128)(2,1)S(1)} %get-tuple-element.37.split_ref.split1, bf16[48,4608]{1,0:T(8,128)(2,1)S(1)} %get-tuple-element.44.split_ref.split2, ...), custom_call_target="tpu_custom_call" | custom-call | tf_op jit(solution)/shard_map/finish/pallas_call | solution.py:394
  (2 shorter events, 0.0 us)
Async XLA Ops:
  0.6 0.7 copy-start
  1.3 19.1 %copy-start.1 = (s32[1,6,4]{1,2,0:T(4,128)S(1)}, s32[1,6,4]{1,2,0:T(4,128)}, u32[]{:S(2)}) copy-start(s32[1,6,4]{1,2,0:T(4,128)} %param.7) | copy-start | bytes 292
  3.3 8.9 %collective-permute-start = (f32[4,16,128]{2,1,0:T(8,128)S(1)}, f32[4,16,128]{2,1,0:T(8,128)S(1)}, u32[]{:S(2)}, u32[]{:S(2)}) collective-permute-start(f32[4,16,128]{2,1,0:T(8,128)S(1)} %get-tuple-element.31), channel_id=1, source_target_pairs={{0,31},{1,2},{2,1},{3,4},{4,3},{5,6},{6,5},{7,8},{8,7},{9,10},{10,... | collective-permute-start | bytes 98312 | tf_op jit(solution)/shard_map/ppermute | solution.py:310
  9.8 10.6 %collective-permute-start.1 = (f32[4,16,128]{2,1,0:T(8,128)S(1)}, f32[4,16,128]{2,1,0:T(8,128)S(1)}, u32[]{:S(2)}, u32[]{:S(2)}) collective-permute-start(f32[4,16,128]{2,1,0:T(8,128)S(1)} %get-tuple-element.32), channel_id=1, source_target_pairs={{0,30},{1,31},{2,4},{3,5},{4,2},{5,3},{6,8},{7,9},{8,6},{9,7},{10,... | collective-permute-start | bytes 98312 | tf_op jit(solution)/shard_map/ppermute | solution.py:310
  10.3 10.1 %collective-permute-start.2 = (f32[4,16,128]{2,1,0:T(8,128)S(1)}, f32[4,16,128]{2,1,0:T(8,128)S(1)}, u32[]{:S(2)}, u32[]{:S(2)}) collective-permute-start(f32[4,16,128]{2,1,0:T(8,128)S(1)} %get-tuple-element.33), channel_id=1, source_target_pairs={{0,24},{1,25},{2,26},{3,27},{4,28},{5,29},{6,30},{7,31},{8,16},{9,... | collective-permute-start | bytes 98312 | tf_op jit(solution)/shard_map/ppermute | solution.py:310
  10.8 9.7 %collective-permute-start.3 = (f32[4,16,128]{2,1,0:T(8,128)S(1)}, f32[4,16,128]{2,1,0:T(8,128)S(1)}, u32[]{:S(2)}, u32[]{:S(2)}) collective-permute-start(f32[4,16,128]{2,1,0:T(8,128)S(1)} %get-tuple-element.34), channel_id=1, source_target_pairs={{0,8},{1,9},{2,10},{3,11},{4,12},{5,13},{6,14},{7,15},{8,0},{9,1},... | collective-permute-start | bytes 98312 | tf_op jit(solution)/shard_map/ppermute | solution.py:310
  10.8 9.7 %collective-permute-start.4 = (f32[4,16,128]{2,1,0:T(8,128)S(1)}, f32[4,16,128]{2,1,0:T(8,128)S(1)}, u32[]{:S(2)}, u32[]{:S(2)}) collective-permute-start(f32[4,16,128]{2,1,0:T(8,128)S(1)} %get-tuple-element.35), channel_id=1, source_target_pairs={{0,2},{1,3},{2,0},{3,1},{4,6},{5,7},{6,4},{7,5},{8,10},{9,11},{10,... | collective-permute-start | bytes 98312 | tf_op jit(solution)/shard_map/ppermute | solution.py:310
  12.2 8.2 %collective-permute-start.5 = (f32[4,16,128]{2,1,0:T(8,128)S(1)}, f32[4,16,128]{2,1,0:T(8,128)S(1)}, u32[]{:S(2)}, u32[]{:S(2)}) collective-permute-start(f32[4,16,128]{2,1,0:T(8,128)S(1)} %get-tuple-element.36), channel_id=1, source_target_pairs={{0,1},{1,0},{2,3},{3,2},{4,5},{5,4},{6,7},{7,6},{8,9},{9,8},{10,11... | collective-permute-start | bytes 98312 | tf_op jit(solution)/shard_map/ppermute | solution.py:310
  21.5 9.5 %collective-permute-start.6 = (f32[4,16,128]{2,1,0:T(8,128)S(1)}, f32[4,16,128]{2,1,0:T(8,128)S(1)}, u32[]{:S(2)}, u32[]{:S(2)}) collective-permute-start(f32[4,16,128]{2,1,0:T(8,128)S(1)} %get-tuple-element.38), channel_id=1, source_target_pairs={{0,31},{1,2},{2,1},{3,4},{4,3},{5,6},{6,5},{7,8},{8,7},{9,10},{10,... | collective-permute-start | bytes 98312 | tf_op jit(solution)/shard_map/ppermute | solution.py:310
  26.2 7.5 %collective-permute-start.7 = (f32[4,16,128]{2,1,0:T(8,128)S(1)}, f32[4,16,128]{2,1,0:T(8,128)S(1)}, u32[]{:S(2)}, u32[]{:S(2)}) collective-permute-start(f32[4,16,128]{2,1,0:T(8,128)S(1)} %get-tuple-element.39), channel_id=1, source_target_pairs={{0,30},{1,31},{2,4},{3,5},{4,2},{5,3},{6,8},{7,9},{8,6},{9,7},{10,... | collective-permute-start | bytes 98312 | tf_op jit(solution)/shard_map/ppermute | solution.py:310
  26.9 6.8 %collective-permute-start.8 = (f32[4,16,128]{2,1,0:T(8,128)S(1)}, f32[4,16,128]{2,1,0:T(8,128)S(1)}, u32[]{:S(2)}, u32[]{:S(2)}) collective-permute-start(f32[4,16,128]{2,1,0:T(8,128)S(1)} %get-tuple-element.40), channel_id=1, source_target_pairs={{0,24},{1,25},{2,26},{3,27},{4,28},{5,29},{6,30},{7,31},{8,16},{9,... | collective-permute-start | bytes 98312 | tf_op jit(solution)/shard_map/ppermute | solution.py:310
  29.0 4.7 %collective-permute-start.9 = (f32[4,16,128]{2,1,0:T(8,128)S(1)}, f32[4,16,128]{2,1,0:T(8,128)S(1)}, u32[]{:S(2)}, u32[]{:S(2)}) collective-permute-start(f32[4,16,128]{2,1,0:T(8,128)S(1)} %get-tuple-element.41), channel_id=1, source_target_pairs={{0,8},{1,9},{2,10},{3,11},{4,12},{5,13},{6,14},{7,15},{8,0},{9,1},... | collective-permute-start | bytes 98312 | tf_op jit(solution)/shard_map/ppermute | solution.py:310
  31.0 3.9 %collective-permute-start.10 = (f32[4,16,128]{2,1,0:T(8,128)S(1)}, f32[4,16,128]{2,1,0:T(8,128)S(1)}, u32[]{:S(2)}, u32[]{:S(2)}) collective-permute-start(f32[4,16,128]{2,1,0:T(8,128)S(1)} %get-tuple-element.42), channel_id=1, source_target_pairs={{0,2},{1,3},{2,0},{3,1},{4,6},{5,7},{6,4},{7,5},{8,10},{9,11},{10,... | collective-permute-start | bytes 98312 | tf_op jit(solution)/shard_map/ppermute | solution.py:310
  31.0 3.9 %collective-permute-start.11 = (f32[4,16,128]{2,1,0:T(8,128)S(1)}, f32[4,16,128]{2,1,0:T(8,128)S(1)}, u32[]{:S(2)}, u32[]{:S(2)}) collective-permute-start(f32[4,16,128]{2,1,0:T(8,128)S(1)} %get-tuple-element.43), channel_id=1, source_target_pairs={{0,1},{1,0},{2,3},{3,2},{4,5},{5,4},{6,7},{7,6},{8,9},{9,8},{10,11... | collective-permute-start | bytes 98312 | tf_op jit(solution)/shard_map/ppermute | solution.py:310
  36.0 8.1 %collective-permute-start.12 = (f32[4,16,128]{2,1,0:T(8,128)S(1)}, f32[4,16,128]{2,1,0:T(8,128)S(1)}, u32[]{:S(2)}, u32[]{:S(2)}) collective-permute-start(f32[4,16,128]{2,1,0:T(8,128)S(1)} %get-tuple-element.46), channel_id=1, source_target_pairs={{0,31},{1,2},{2,1},{3,4},{4,3},{5,6},{6,5},{7,8},{8,7},{9,10},{10,... | collective-permute-start | bytes 98312 | tf_op jit(solution)/shard_map/ppermute | solution.py:310
  39.8 7.6 %collective-permute-start.13 = (f32[4,16,128]{2,1,0:T(8,128)S(1)}, f32[4,16,128]{2,1,0:T(8,128)S(1)}, u32[]{:S(2)}, u32[]{:S(2)}) collective-permute-start(f32[4,16,128]{2,1,0:T(8,128)S(1)} %get-tuple-element.47), channel_id=1, source_target_pairs={{0,30},{1,31},{2,4},{3,5},{4,2},{5,3},{6,8},{7,9},{8,6},{9,7},{10,... | collective-permute-start | bytes 98312 | tf_op jit(solution)/shard_map/ppermute | solution.py:310
  41.9 5.7 %collective-permute-start.14 = (f32[4,16,128]{2,1,0:T(8,128)S(1)}, f32[4,16,128]{2,1,0:T(8,128)S(1)}, u32[]{:S(2)}, u32[]{:S(2)}) collective-permute-start(f32[4,16,128]{2,1,0:T(8,128)S(1)} %get-tuple-element.48), channel_id=1, source_target_pairs={{0,24},{1,25},{2,26},{3,27},{4,28},{5,29},{6,30},{7,31},{8,16},{9,... | collective-permute-start | bytes 98312 | tf_op jit(solution)/shard_map/ppermute | solution.py:310
  42.9 4.7 %collective-permute-start.15 = (f32[4,16,128]{2,1,0:T(8,128)S(1)}, f32[4,16,128]{2,1,0:T(8,128)S(1)}, u32[]{:S(2)}, u32[]{:S(2)}) collective-permute-start(f32[4,16,128]{2,1,0:T(8,128)S(1)} %get-tuple-element.49), channel_id=1, source_target_pairs={{0,8},{1,9},{2,10},{3,11},{4,12},{5,13},{6,14},{7,15},{8,0},{9,1},... | collective-permute-start | bytes 98312 | tf_op jit(solution)/shard_map/ppermute | solution.py:310
  44.1 3.9 %collective-permute-start.16 = (f32[4,16,128]{2,1,0:T(8,128)S(1)}, f32[4,16,128]{2,1,0:T(8,128)S(1)}, u32[]{:S(2)}, u32[]{:S(2)}) collective-permute-start(f32[4,16,128]{2,1,0:T(8,128)S(1)} %get-tuple-element.50), channel_id=1, source_target_pairs={{0,2},{1,3},{2,0},{3,1},{4,6},{5,7},{6,4},{7,5},{8,10},{9,11},{10,... | collective-permute-start | bytes 98312 | tf_op jit(solution)/shard_map/ppermute | solution.py:310
  44.1 3.9 %collective-permute-start.17 = (f32[4,16,128]{2,1,0:T(8,128)S(1)}, f32[4,16,128]{2,1,0:T(8,128)S(1)}, u32[]{:S(2)}, u32[]{:S(2)}) collective-permute-start(f32[4,16,128]{2,1,0:T(8,128)S(1)} %get-tuple-element.51), channel_id=1, source_target_pairs={{0,1},{1,0},{2,3},{3,2},{4,5},{5,4},{6,7},{7,6},{8,9},{9,8},{10,11... | collective-permute-start | bytes 98312 | tf_op jit(solution)/shard_map/ppermute | solution.py:310

commit v2 on v1

--- a/solution.py
+++ b/solution.py
@@ -9,6 +9,8 @@
 
 
 ITERS = 3
+TRUSTED_PIVOT = 0.008
+HIGHEST = lax.Precision.HIGHEST
 LEVELS = ITERS + 1
 PIECES = 3
 F32 = jnp.float32
@@ -75,18 +77,15 @@
             split_ref[piece * width : (piece + 1) * width, cols] = value
 
 
-def first_send_kernel(dev_count, rows_ref, field_ref, *refs):
-    out_refs, sems = refs[:-1], refs[-1]
-    block_rows = field_ref.shape[0]
-    copies = []
-    for hop, ((pair, phase), out_ref) in enumerate(zip(MATCHINGS, out_refs)):
-        face = matching_face(dev_count, pair, phase)
-        for slot in range(rows_ref.shape[1]):
-            row = jnp.minimum(rows_ref[0, slot, face], block_rows - 1)
-            copies.append(pltpu.make_async_copy(field_ref.at[row], out_ref.at[slot], sems.at[hop, slot]))
-            copies[-1].start()
-    for copy in copies:
-        copy.wait()
+def first_send_kernel(dev_count, rows_hbm, field_hbm, *refs):
+    out_refs, (rows_ref, field_ref, sems) = refs[:-3], refs[-3:]
+    fetch_field = pltpu.make_async_copy(field_hbm, field_ref, sems.at[0])
+    fetch_rows = pltpu.make_async_copy(rows_hbm, rows_ref, sems.at[1])
+    fetch_field.start()
+    fetch_rows.start()
+    fetch_rows.wait()
+    fetch_field.wait()
+    send_rows(dev_count, rows_ref, field_ref, out_refs)
 
 
 def fold(value, width):
@@ -240,6 +239,47 @@
     )
 
 
+def places(width, lanes):
+    row = lax.broadcasted_iota(jnp.int32, (width, lanes), 0)
+    lane = lax.broadcasted_iota(jnp.int32, (width, lanes), 1)
+    return row, lane, lane % width
+
+
+def pack(moments):
+    width, lanes = moments.shape
+    row, lane, col = places(width, lanes)
+    odd = pltpu.roll(moments, lanes - width, 1)
+    tiles = jnp.where(row <= col, moments, odd)
+    diagonal = jnp.sum(jnp.where(row == col, odd, 0.0), axis=0, keepdims=True)
+    half = width // 2
+    row, lane = row[:half], lane[:half]
+    packed = jnp.where(lane % (2 * width) < width, tiles[:half], pltpu.roll(tiles[half:], width, 1))
+    packed = jnp.where(lane < 6 * width, packed, 0.0)
+    for k in range(3):
+        here = (row == k) & (lane >= 6 * width) & (lane < 7 * width)
+        packed = jnp.where(here, pltpu.roll(diagonal, (6 - 2 * k) * width, 1), packed)
+    return packed
+
+
+def unpack(packed):
+    half, lanes = packed.shape
+    width = 2 * half
+    row, lane, col = places(width, lanes)
+    tiles = jnp.concatenate([packed, pltpu.roll(packed, lanes - width, 1)], axis=0)
+    turned = jnp.concatenate([tiles, jnp.zeros((lanes - width, lanes), F32)], axis=0).T
+    mirror = jnp.zeros_like(tiles)
+    diagonal = jnp.zeros_like(tiles)
+    for k in range(3):
+        here = (lane >= 2 * k * width) & (lane < (2 * k + 1) * width)
+        part = turned[2 * k * width : (2 * k + 1) * width]
+        mirror = jnp.where(here, pltpu.roll(part, 2 * k * width, 1) if k else part, mirror)
+        diagonal = jnp.where(here, pltpu.roll(packed[k : k + 1], lanes - (6 - 2 * k) * width, 1), diagonal)
+    even = jnp.where(row <= col, tiles, mirror)
+    odd = jnp.where(row > col, tiles, jnp.where(row < col, mirror, diagonal))
+    both = jnp.where(lane % (2 * width) < width, even, pltpu.roll(odd, width, 1))
+    return jnp.where(lane < 6 * width, both, 0.0)
+
+
 def last_link_kernel(dev_count, pad, rows_ref, base_ref, links_ref, split2, moments_ref, *refs):
     count = len(MATCHINGS)
     far_refs, split_ref, out_ref, field_ref = refs[:count], refs[count], refs[count + 1], refs[-1]
@@ -251,25 +291,44 @@
     z = fold_lanes(fold(gram_rows(split2[:, cols], (split2, split2, split2, split_ref), cols), width))
     lane = lax.broadcasted_iota(jnp.int32, z.shape, 1)
     mine = jnp.where(lane < 5 * width, moments_ref[...], pltpu.roll(z, 2 * width, 1))
-    mine = jnp.where(lane < 6 * width, mine, 0.0)
+    mine = pack(mine)
     for peer in range(out_ref.shape[0]):
         out_ref[peer] = mine
 
 
-def finish_kernel(pad, gathered_ref, split0, split1, split2, split3, solution_ref, residual_ref):
-    peers, width, lanes = gathered_ref.shape
+def finish_kernel(pad, gathered_ref, split0, split1, split2, split3, solution_ref, residual_ref, doubt_ref):
+    peers, half, lanes = gathered_ref.shape
+    width = 2 * half
     block_rows = solution_ref.shape[0]
-    moments = gathered_ref[0]
-    for peer in range(1, peers):
-        moments = moments + gathered_ref[peer]
+    sums = [gathered_ref[peer] for peer in range(peers)]
+    while len(sums) > 1:
+        sums = [sum(sums[k + 1 : k + 2], sums[k]) for k in range(0, len(sums), 2)]
+    moments = unpack(sums[0])
     table = [pltpu.roll(moments, lanes - width * (k + 1), 1) for k in range(ITERS)] + [moments]
     table = jnp.concatenate(table, axis=0)
     lane = lax.broadcasted_iota(jnp.int32, (1, lanes), 1)
-    for k in range(ITERS * width):
-        row = table[k : k + 1, :]
-        column = table[:, k : k + 1] * (1.0 / table[k : k + 1, k : k + 1])
-        table = jnp.where(lane == k, column, table - column * row)
-    coeffs = table[ITERS * width :]
+    across = lax.broadcasted_iota(jnp.int32, table.shape, 1) == lax.broadcasted_iota(jnp.int32, table.shape, 0)
+    diagonal = jnp.sum(jnp.where(across, table, 0.0), axis=0, keepdims=True)
+    pivots = jnp.zeros((1, lanes), F32)
+    for k in range(0, ITERS * width, 2):
+        if k and k % 8 == 0:
+            table = table[8:]
+        at = k % 8
+        first, second = table[at : at + 1], table[at + 1 : at + 2]
+        left, right = table[:, k : k + 1], table[:, k + 1 : k + 2]
+        p11, p12 = left[at : at + 1], right[at : at + 1]
+        p21, p22 = left[at + 1 : at + 2], right[at + 1 : at + 2]
+        det = p11 * p22 - p12 * p21
+        inverse = 1.0 / det
+        pivots = jnp.where(lane == k, p11, jnp.where(lane == k + 1, det / p11, pivots))
+        left, right = (left * p22 - right * p21) * inverse, (right * p11 - left * p12) * inverse
+        rest = table - left * first - right * second
+        table = jnp.where(lane == k, left, jnp.where(lane == k + 1, right, rest))
+    trusted = (pivots > TRUSTED_PIVOT * diagonal) & (pivots < jnp.inf)
+    used = lane < ITERS * width
+    doubt = jnp.where(used & jnp.logical_not(trusted), 1.0, 0.0)
+    doubt_ref[...] = jnp.broadcast_to(jnp.max(doubt, axis=1, keepdims=True), doubt_ref.shape)
+    coeffs = table[-width:]
     lane = lax.broadcasted_iota(jnp.int32, coeffs.shape, 1)
     unit = (lane == lax.broadcasted_iota(jnp.int32, coeffs.shape, 0)).astype(F32)
     for_solution = jnp.where(lane < ITERS * width, coeffs, 0.0)
@@ -292,7 +351,73 @@
     lax.fori_loop(0, block_rows // step, body, 0, unroll=2)
 
 
-def shards(right_side, band_blocks, link_blocks, link_rows):
+def gram_matrix(left, right):
+    return lax.psum(jnp.einsum("nsi,nti->st", left, right, precision=HIGHEST), "dom")
+
+
+def mix_columns(field, coeffs):
+    return jnp.einsum("nsi,st->nti", field, coeffs, precision=HIGHEST)
+
+
+def solve_gram(matrix, target):
+    factor = jnp.linalg.cholesky(0.5 * (matrix + matrix.T))
+    return jax.scipy.linalg.cho_solve((factor, True), target)
+
+
+def plain_kernel(field_ref, band_ref, out_ref):
+    row = pl.program_id(0)
+    total = jnp.zeros(out_ref.shape[1:], F32)
+    for k in range(band_ref.shape[1]):
+        total += lax.dot_general(
+            field_ref[row + k], band_ref[0, k], (((1,), (1,)), ((), ())), precision=HIGHEST, preferred_element_type=F32
+        )
+    out_ref[0] = total
+
+
+def apply_operator(field, band_blocks, link_blocks, link_rows):
+    dev_count = lax.axis_size("dom")
+    block_rows, band = band_blocks.shape[:2]
+    half = band // 2
+    picks = (link_rows[0][:, :, None] == jnp.arange(block_rows, dtype=jnp.int32)).astype(field.dtype)
+    padded = jnp.pad(field, ((half, half), (0, 0), (0, 0)))
+    total = pl.pallas_call(
+        plain_kernel,
+        out_shape=jax.ShapeDtypeStruct(field.shape, F32),
+        grid=(block_rows,),
+        in_specs=[
+            pl.BlockSpec(padded.shape, lambda r: (0, 0, 0)),
+            pl.BlockSpec((1, *band_blocks.shape[1:]), lambda r: (r, 0, 0, 0)),
+        ],
+        out_specs=pl.BlockSpec((1, *field.shape[1:]), lambda r: (r, 0, 0)),
+        compiler_params=params(8),
+        name="plain",
+    )(padded, band_blocks)
+    for face in range(link_rows.shape[1]):
+        by = offsets(dev_count)[face // 2] * (1 - 2 * (face % 2))
+        source = jnp.einsum("hr,rsi->hsi", picks[face ^ 1], field, precision=HIGHEST)
+        far = lax.ppermute(source, "dom", [(i, (i - by) % dev_count) for i in range(dev_count)])
+        part = jnp.einsum("hsj,hij->hsi", far, link_blocks[0, face], precision=HIGHEST)
+        total += jnp.einsum("hr,hsi->rsi", picks[face], part, precision=HIGHEST)
+    return total
+
+
+def classical(right_side, band_blocks, link_blocks, link_rows):
+    def iterate(_, state):
+        value, rest, direction, squares = state
+        image = apply_operator(direction, band_blocks, link_blocks, link_rows)
+        alpha = solve_gram(gram_matrix(direction, image), squares)
+        value = value + mix_columns(direction, alpha)
+        rest = rest - mix_columns(image, alpha)
+        fresh = gram_matrix(rest, rest)
+        direction = rest + mix_columns(direction, solve_gram(squares, fresh))
+        return value, rest, direction, fresh
+
+    start = (jnp.zeros_like(right_side), right_side, right_side, gram_matrix(right_side, right_side))
+    return lax.fori_loop(0, ITERS, iterate, start)[:2]
+
+
+def shards(*args):
+    right_side, band_blocks, link_blocks, link_rows = args
     dev_count = lax.axis_size("dom")
     block_rows, width, size = right_side.shape
     band = band_blocks.shape[1]
@@ -314,13 +439,17 @@
     right_side, band_blocks, link_blocks = (
         pltpu.with_memory_space_constraint(value, pltpu.HBM) for value in (right_side, band_blocks, link_blocks)
     )
-    slot_rows = jnp.swapaxes(link_rows, 1, 2)
+    slot_rows = pltpu.with_memory_space_constraint(jnp.swapaxes(link_rows, 1, 2), pltpu.HBM)
     messages = pl.pallas_call(
         functools.partial(first_send_kernel, dev_count),
         out_shape=[message] * count,
-        in_specs=[smem()] + hbm,
+        in_specs=hbm * 2,
         out_specs=vmem(count),
-        scratch_shapes=[pltpu.SemaphoreType.DMA((count, slots))],
+        scratch_shapes=[
+            pltpu.SMEM(slot_rows.shape, jnp.int32),
+            pltpu.VMEM(right_side.shape, F32),
+            pltpu.SemaphoreType.DMA((2,)),
+        ],
         compiler_params=params(8),
         name="first_send",
     )(slot_rows, right_side)
@@ -382,7 +511,7 @@
     )(*splits)
     split3, mine = pl.pallas_call(
         functools.partial(last_link_kernel, dev_count, half),
-        out_shape=[split, jax.ShapeDtypeStruct((dev_count, width, 128), F32)],
+        out_shape=[split, jax.ShapeDtypeStruct((dev_count, width // 2, 128), F32)],
         in_specs=[smem()] + vmem(4 + count),
         out_specs=vmem(2),
         scratch_shapes=[pltpu.VMEM(right_side.shape, F32)],
@@ -391,14 +520,21 @@
     )(slot_rows, base, links, splits[-1], moments, *far)
     splits.append(split3)
     gathered = lax.all_to_all(mine, "dom", 0, 0)
-    return pl.pallas_call(
+    value, rest, doubt = pl.pallas_call(
         functools.partial(finish_kernel, half),
-        out_shape=[field, field],
+        out_shape=[field, field, jax.ShapeDtypeStruct((8, 128), F32)],
         in_specs=vmem(1 + LEVELS),
-        out_specs=vmem(2),
+        out_specs=vmem(3),
         compiler_params=params(8),
         name="finish",
     )(gathered, *splits)
+    again = lambda state: state[0][0, 0] > 0.0
+
+    def redo(state):
+        held, flag = lax.optimization_barrier((args, state[0]))
+        return 0.0 * flag, *classical(*held)
+
+    return lax.while_loop(again, redo, (doubt, value, rest))[1:]
 
 
 def solution(mesh):

time: 70 us -> 72.1 us (1.030)
  Pallas kernels: 26.6 us -> 29.3 us
  blocking collectives: 14.2 us -> 11.9 us
  loops' own time: 0 us -> 0.88 us
    pallas_call x1, Pallas kernels: 5.86 us -> 9.04 us  [shards(): pl.pallas_call(functools.partial(finish_kernel, half), out_shape=[field,...]
    all_to_all x1, blocking collectives: 14.2 us -> 11.9 us  [shards(): gathered = lax.all_to_all(mine, 'dom', 0, 0)]
    slice x0 -> x1, local copies, waits for them, and re-layouts: none -> 1.27 us  [shards(): again = lambda state: state[0][0, 0] > 0.0]
    pallas_call x1, Pallas kernels: 1.97 us -> 1 us  [shards(): pl.pallas_call(functools.partial(first_send_kernel, dev_count), out_shape...]
    another operation x0 -> x1, loops' own time: none -> 0.88 us  [shards(): return lax.while_loop(again, redo, (doubt, value, rest))[1:]]
where the time goes in v2:
time: 72.1 us; the launch traced here: 71.8 us
  Pallas kernels  29.3 us (41%)
  starting transfers between devices  24 us (33%)
  blocking collectives  11.9 us (17%)
  waiting for transfers between devices  3.52 us (5%)
  local copies, waits for them, and re-layouts  1.29 us (2%)
  between operations  0.93 us (1%)
  loops' own time  0.88 us (1%)
    ppermute x18, starting transfers between devices, exchange(): lax.ppermute(messages[index], 'dom', matching_pairs(dev_count, pair, phase))  24 us
    all_to_all x1, blocking collectives, shards(): gathered = lax.all_to_all(mine, 'dom', 0, 0)  11.9 us
    pallas_call x1, Pallas kernels, shards(): pl.pallas_call(functools.partial(finish_kernel, half), out_shape=[field,...  9.04 us
    pallas_call x1, Pallas kernels, shards(): pl.pallas_call(functools.partial(prepare_kernel, half), out_shape=[pltpu....  8.16 us
    pallas_call x2, Pallas kernels, shards(): pl.pallas_call(band_kernel, out_shape=field, in_specs=vmem(2), out_specs=...  4.89 us
    ppermute x18, waiting for transfers between devices, exchange(): lax.ppermute(messages[index], 'dom', matching_pairs(dev_count, pair, phase))  3.52 us
    pallas_call x2, Pallas kernels, shards(): pl.pallas_call(functools.partial(link_kernel, dev_count, half), out_shape...  2.37 us
    pallas_call x1, Pallas kernels, shards(): pl.pallas_call(functools.partial(last_link_kernel, dev_count, half), out_...  1.99 us
  transfers between devices with their start and end apart: 18, of which 5 were waited for; matrix products, arithmetic and copies ran while one was open for 0% of the time, Pallas kernels for 21%

profile of v2, /device:TPU:0, one launch (start us, length us, event | category | flops | bytes accessed | tf_op | source)
XLA Modules:
  0.0 71.8 jit_solution(5535712991549490242)
XLA Ops:
  0.6 1.0 %first_send.1 = (f32[4,16,128]{2,1,0:T(8,128)S(1)}, f32[4,16,128]{2,1,0:T(8,128)S(1)}, f32[4,16,128]{2,1,0:T(8,128)S(1)}, f32[4,16,128]{2,1,0:T(8,128)S(1)}, f32...) custom-call(s32[1,4,6]{2,1,0:T(4,128)} %bitcast.247, f32[32,16,128]{2,1,0:T(8,128)} %field_hbm.3), custom_call_target="tpu_custom_call" | custom-call | tf_op jit(solution)/shard_map/first_send/pallas_call | solution.py:443
  1.6 6.5 %collective-permute-start.6 = (f32[4,16,128]{2,1,0:T(8,128)S(1)}, f32[4,16,128]{2,1,0:T(8,128)S(1)}, u32[]{:S(2)}, u32[]{:S(2)}) collective-permute-start(f32[4,16,128]{2,1,0:T(8,128)S(1)} %get-tuple-element.274), channel_id=1, source_target_pairs={{0,31},{1,2},{2,1},{3,4},{4,3},{5,6},{6,5},{7,8},{8,7},{9,10},{10,... | collective-permute-start | bytes 98312 | tf_op jit(solution)/shard_map/ppermute | solution.py:435
  8.1 0.6 collective-permute-start.7
  8.7 0.4 collective-permute-start.8
  9.2 0.0 collective-permute-start.9
  9.2 1.4 %collective-permute-start.10 = (f32[4,16,128]{2,1,0:T(8,128)S(1)}, f32[4,16,128]{2,1,0:T(8,128)S(1)}, u32[]{:S(2)}, u32[]{:S(2)}) collective-permute-start(f32[4,16,128]{2,1,0:T(8,128)S(1)} %get-tuple-element.278), channel_id=1, source_target_pairs={{0,2},{1,3},{2,0},{3,1},{4,6},{5,7},{6,4},{7,5},{8,10},{9,11},{10,... | collective-permute-start | bytes 98312 | tf_op jit(solution)/shard_map/ppermute | solution.py:435
  10.6 0.0 collective-permute-done.6.refs_0_
  10.6 0.0 collective-permute-start.11
  10.6 8.2 %prepare.1 = (bf16[18,12,128,256]{3,2,1,0:T(8,128)(2,1)S(1)}, bf16[6,2,256,256]{3,2,1,0:T(8,128)(2,1)S(1)}, bf16[48,4608]{1,0:T(8,128)(2,1)S(1)}, f32[32,16,128]{2,1,0:T(8,128)S(1)}) custom-call(f32[32,16,128]{2,1,0:T(8,128)} %field_hbm.3, f32[32,5,128,128]{3,2,1,0:T(8,128)} %band_hbm.1, f32[1,6,4,128,128]{4,3,2,1,0:T(8,128)} %link_hbm.1), custom_call_target="tpu_custom_call" | custom-call | flops 1000000000 | bytes 12000000 | tf_op jit(solution)/shard_map/prepare/pallas_call | solution.py:457
  18.8 0.0 collective-permute-done.7.refs_1_
  18.8 0.0 collective-permute-done.8.refs_2_
  18.8 0.0 collective-permute-done.9.refs_3_
  18.8 0.0 collective-permute-done.10.refs_4_
  18.9 0.0 collective-permute-done.11.refs_5_
  18.9 1.2 %link.2 = (bf16[48,4608]{1,0:T(8,128)(2,1)S(1)}, f32[4,16,128]{2,1,0:T(8,128)S(1)}, f32[4,16,128]{2,1,0:T(8,128)S(1)}, f32[4,16,128]{2,1,0:T(8,128)S(1)}, f32[4,...) custom-call(s32[1,4,6]{2,1,0:T(4,128)} %bitcast.248, ...), custom_call_target="tpu_custom_call" | custom-call | tf_op jit(solution)/shard_map/link/pallas_call | solution.py:491
  20.1 4.5 %collective-permute-start.12 = (f32[4,16,128]{2,1,0:T(8,128)S(1)}, f32[4,16,128]{2,1,0:T(8,128)S(1)}, u32[]{:S(2)}, u32[]{:S(2)}) collective-permute-start(f32[4,16,128]{2,1,0:T(8,128)S(1)} %get-tuple-element.281), channel_id=1, source_target_pairs={{0,31},{1,2},{2,1},{3,4},{4,3},{5,6},{6,5},{7,8},{8,7},{9,10},{10,... | collective-permute-start | bytes 98312 | tf_op jit(solution)/shard_map/ppermute | solution.py:435
  24.6 0.8 %collective-permute-start.13 = (f32[4,16,128]{2,1,0:T(8,128)S(1)}, f32[4,16,128]{2,1,0:T(8,128)S(1)}, u32[]{:S(2)}, u32[]{:S(2)}) collective-permute-start(f32[4,16,128]{2,1,0:T(8,128)S(1)} %get-tuple-element.282), channel_id=1, source_target_pairs={{0,30},{1,31},{2,4},{3,5},{4,2},{5,3},{6,8},{7,9},{8,6},{9,7},{10,... | collective-permute-start | bytes 98312 | tf_op jit(solution)/shard_map/ppermute | solution.py:435
  25.4 2.0 %collective-permute-start.14 = (f32[4,16,128]{2,1,0:T(8,128)S(1)}, f32[4,16,128]{2,1,0:T(8,128)S(1)}, u32[]{:S(2)}, u32[]{:S(2)}) collective-permute-start(f32[4,16,128]{2,1,0:T(8,128)S(1)} %get-tuple-element.283), channel_id=1, source_target_pairs={{0,24},{1,25},{2,26},{3,27},{4,28},{5,29},{6,30},{7,31},{8,16},{9,... | collective-permute-start | bytes 98312 | tf_op jit(solution)/shard_map/ppermute | solution.py:435
  27.4 1.9 %collective-permute-start.15 = (f32[4,16,128]{2,1,0:T(8,128)S(1)}, f32[4,16,128]{2,1,0:T(8,128)S(1)}, u32[]{:S(2)}, u32[]{:S(2)}) collective-permute-start(f32[4,16,128]{2,1,0:T(8,128)S(1)} %get-tuple-element.284), channel_id=1, source_target_pairs={{0,8},{1,9},{2,10},{3,11},{4,12},{5,13},{6,14},{7,15},{8,0},{9,1},... | collective-permute-start | bytes 98312 | tf_op jit(solution)/shard_map/ppermute | solution.py:435
  29.4 0.0 collective-permute-start.16
  29.4 0.0 collective-permute-done.12.refs_0_
  29.4 0.0 collective-permute-start.17
  29.4 2.4 %band.2.base_ref = f32[32,16,128]{2,1,0:T(8,128)S(1)} custom-call(bf16[18,12,128,256]{3,2,1,0:T(8,128)(2,1)S(1)} %get-tuple-element.271.weights_ref, bf16[48,4608]{1,0:T(8,128)(2,1)S(1)} %get-tuple-element.280.split_ref.split1), custom_call_target="tpu_custom_call" | custom-call | flops 1000000000 | bytes 12000000 | tf_op jit(solution)/shard_map/band/pallas_call | solution.py:481
  31.8 0.3 collective-permute-done.13.refs_1_
  32.1 0.0 collective-permute-done.15.refs_3_
  32.1 1.2 %collective-permute-done.16.refs_4_ = f32[4,16,128]{2,1,0:T(8,128)S(1)} collective-permute-done((f32[4,16,128]{2,1,0:T(8,128)S(1)}, f32[4,16,128]{2,1,0:T(8,128)S(1)}, u32[]{:S(2)}, u32[]{:S(2)}) %collective-permute-start.16) | collective-permute-done | bytes 32800 | tf_op jit(solution)/shard_map/ppermute | solution.py:435
  33.3 0.0 collective-permute-done.17.refs_5_
  33.3 1.2 %link.3 = (bf16[48,4608]{1,0:T(8,128)(2,1)S(1)}, f32[4,16,128]{2,1,0:T(8,128)S(1)}, f32[4,16,128]{2,1,0:T(8,128)S(1)}, f32[4,16,128]{2,1,0:T(8,128)S(1)}, f32[4,...) custom-call(s32[1,4,6]{2,1,0:T(4,128)} %bitcast.249, f32[32,16,128]{2,1,0:T(8,128)S(1)} %band.2.base_ref, ...), custom_call_target="tpu_custom_call" | custom-call | tf_op jit(solution)/shard_map/link/pallas_call | solution.py:491
  34.5 1.5 %collective-permute-start.18 = (f32[4,16,128]{2,1,0:T(8,128)S(1)}, f32[4,16,128]{2,1,0:T(8,128)S(1)}, u32[]{:S(2)}, u32[]{:S(2)}) collective-permute-start(f32[4,16,128]{2,1,0:T(8,128)S(1)} %get-tuple-element.289), channel_id=1, source_target_pairs={{0,31},{1,2},{2,1},{3,4},{4,3},{5,6},{6,5},{7,8},{8,7},{9,10},{10,... | collective-permute-start | bytes 98312 | tf_op jit(solution)/shard_map/ppermute | solution.py:435
  36.0 2.4 %band.3.base_ref = f32[32,16,128]{2,1,0:T(8,128)S(1)} custom-call(bf16[18,12,128,256]{3,2,1,0:T(8,128)(2,1)S(1)} %get-tuple-element.271.weights_ref, bf16[48,4608]{1,0:T(8,128)(2,1)S(1)} %get-tuple-element.287.split_ref.split2), custom_call_target="tpu_custom_call" | custom-call | flops 1000000000 | bytes 12000000 | tf_op jit(solution)/shard_map/band/pallas_call | solution.py:481
  38.4 2.0 %collective-permute-start.19 = (f32[4,16,128]{2,1,0:T(8,128)S(1)}, f32[4,16,128]{2,1,0:T(8,128)S(1)}, u32[]{:S(2)}, u32[]{:S(2)}) collective-permute-start(f32[4,16,128]{2,1,0:T(8,128)S(1)} %get-tuple-element.290), channel_id=1, source_target_pairs={{0,30},{1,31},{2,4},{3,5},{4,2},{5,3},{6,8},{7,9},{8,6},{9,7},{10,... | collective-permute-start | bytes 98312 | tf_op jit(solution)/shard_map/ppermute | solution.py:435
  40.5 1.0 %collective-permute-start.20 = (f32[4,16,128]{2,1,0:T(8,128)S(1)}, f32[4,16,128]{2,1,0:T(8,128)S(1)}, u32[]{:S(2)}, u32[]{:S(2)}) collective-permute-start(f32[4,16,128]{2,1,0:T(8,128)S(1)} %get-tuple-element.291), channel_id=1, source_target_pairs={{0,24},{1,25},{2,26},{3,27},{4,28},{5,29},{6,30},{7,31},{8,16},{9,... | collective-permute-start | bytes 98312 | tf_op jit(solution)/shard_map/ppermute | solution.py:435
  41.4 1.1 %collective-permute-start.21 = (f32[4,16,128]{2,1,0:T(8,128)S(1)}, f32[4,16,128]{2,1,0:T(8,128)S(1)}, u32[]{:S(2)}, u32[]{:S(2)}) collective-permute-start(f32[4,16,128]{2,1,0:T(8,128)S(1)} %get-tuple-element.292), channel_id=1, source_target_pairs={{0,8},{1,9},{2,10},{3,11},{4,12},{5,13},{6,14},{7,15},{8,0},{9,1},... | collective-permute-start | bytes 98312 | tf_op jit(solution)/shard_map/ppermute | solution.py:435
  42.6 0.0 collective-permute-start.22
  42.6 0.0 collective-permute-done.18.refs_0_
  42.6 0.0 collective-permute-start.23
  42.6 1.9 %gram.1.moments_ref = f32[16,128]{1,0:T(8,128)S(1)} custom-call(bf16[48,4608]{1,0:T(8,128)(2,1)S(1)} %get-tuple-element.288.split0, bf16[48,4608]{1,0:T(8,128)(2,1)S(1)} %get-tuple-element.280.split_ref.split1, bf16[48,4608]{1,0:T(8,128)(2,1)S(1)} %get-tuple-element.287.split_ref.split2), custom_call_target="tpu_custom_call" | custom-call | flops 1000000000 | bytes 4000000 | tf_op jit(solution)/shard_map/gram/pallas_call | solution.py:502
  44.5 1.6 %collective-permute-done.19.refs_1_ = f32[4,16,128]{2,1,0:T(8,128)S(1)} collective-permute-done((f32[4,16,128]{2,1,0:T(8,128)S(1)}, f32[4,16,128]{2,1,0:T(8,128)S(1)}, u32[]{:S(2)}, u32[]{:S(2)}) %collective-permute-start.19) | collective-permute-done | bytes 32800 | tf_op jit(solution)/shard_map/ppermute | solution.py:435
  46.1 0.1 collective-permute-done.20.refs_2_
  46.2 0.3 collective-permute-done.22.refs_4_
  46.5 2.0 %last_link.1 = (bf16[48,4608]{1,0:T(8,128)(2,1)S(1)}, f32[32,8,128]{2,1,0:T(8,128)S(1)}) custom-call(s32[1,4,6]{2,1,0:T(4,128)} %bitcast.250, f32[32,16,128]{2,1,0:T(8,128)S(1)} %band.3.base_ref, bf16[6,2,256,256]{3,2,1,0:T(8,128)(2,1)S(1)} %get-tuple-element.273.links_ref, bf16[48,4608]{1,0:T(8,128)(2,1)S(1)} %get-tuple-element.287.split_ref.split2, ...), custom_call_target="tpu_custom_call" | custom-call | tf_op jit(solution)/shard_map/last_link/pallas_call | solution.py:512
  48.5 0.0 copy-start.1
  48.5 0.0 copy-start.3
  48.5 0.0 copy-start.4
  48.5 11.9 %all_to_all.5.gathered_ref = f32[32,8,128]{2,1,0:T(8,128)S(1)} all-to-all(f32[32,8,128]{2,1,0:T(8,128)S(1)} %get-tuple-element.295), channel_id=1, replica_groups=mesh['dom'=32] {'dom'}, dimensions={0} | all-to-all | bytes 262144 | tf_op jit(solution)/shard_map/all_to_all | solution.py:522
  60.4 9.0 %finish.1 = (f32[32,16,128]{2,1,0:T(8,128)}, f32[32,16,128]{2,1,0:T(8,128)}, f32[8,128]{1,0:T(8,128)}) custom-call(f32[32,8,128]{2,1,0:T(8,128)S(1)} %all_to_all.5.gathered_ref, bf16[48,4608]{1,0:T(8,128)(2,1)S(1)} %get-tuple-element.288.split0, bf16[48,4608]{1,0:T(8,128)(2,1)S(1)} %get-tuple-element.280.split_ref.split1, ...), custom_call_target="tpu_custom_call" | custom-call | tf_op jit(solution)/shard_map/finish/pallas_call | solution.py:523
  69.5 2.2 %while.41 = (f32[8,128]{1,0:T(8,128)}, f32[32,16,128]{2,1,0:T(8,128)}, f32[32,16,128]{2,1,0:T(8,128)}, f32[32,16,128]{2,1,0:T(8,128)S(1)}, f32[32,5,128,128]{3,2...) while((f32[8,128]{1,0:T(8,128)}, ...), condition=%wide.region_8.11_spmd, body=%wide.region_0.10_spmd.sunk | while | flops 189603872 | bytes 16484256 | solution.py:537
  69.5 1.3 %slice.167 = f32[1,1]{1,0:T(1,128)} slice(f32[8,128]{1,0:T(8,128)} %get-tuple-element.407), slice={[0:1], [0:1]} | slice | bytes 8 | tf_op jit(solution)/shard_map/while/cond/slice | solution.py:531
  (6 shorter events, 0.0 us)
Async XLA Ops:
  1.6 9.0 %collective-permute-start.6 = (f32[4,16,128]{2,1,0:T(8,128)S(1)}, f32[4,16,128]{2,1,0:T(8,128)S(1)}, u32[]{:S(2)}, u32[]{:S(2)}) collective-permute-start(f32[4,16,128]{2,1,0:T(8,128)S(1)} %get-tuple-element.274), channel_id=1, source_target_pairs={{0,31},{1,2},{2,1},{3,4},{4,3},{5,6},{6,5},{7,8},{8,7},{9,10},{10,... | collective-permute-start | bytes 98312 | tf_op jit(solution)/shard_map/ppermute | solution.py:435
  8.1 10.7 %collective-permute-start.7 = (f32[4,16,128]{2,1,0:T(8,128)S(1)}, f32[4,16,128]{2,1,0:T(8,128)S(1)}, u32[]{:S(2)}, u32[]{:S(2)}) collective-permute-start(f32[4,16,128]{2,1,0:T(8,128)S(1)} %get-tuple-element.275), channel_id=1, source_target_pairs={{0,30},{1,31},{2,4},{3,5},{4,2},{5,3},{6,8},{7,9},{8,6},{9,7},{10,... | collective-permute-start | bytes 98312 | tf_op jit(solution)/shard_map/ppermute | solution.py:435
  8.7 10.1 %collective-permute-start.8 = (f32[4,16,128]{2,1,0:T(8,128)S(1)}, f32[4,16,128]{2,1,0:T(8,128)S(1)}, u32[]{:S(2)}, u32[]{:S(2)}) collective-permute-start(f32[4,16,128]{2,1,0:T(8,128)S(1)} %get-tuple-element.276), channel_id=1, source_target_pairs={{0,24},{1,25},{2,26},{3,27},{4,28},{5,29},{6,30},{7,31},{8,16},{9,... | collective-permute-start | bytes 98312 | tf_op jit(solution)/shard_map/ppermute | solution.py:435
  9.2 9.6 %collective-permute-start.9 = (f32[4,16,128]{2,1,0:T(8,128)S(1)}, f32[4,16,128]{2,1,0:T(8,128)S(1)}, u32[]{:S(2)}, u32[]{:S(2)}) collective-permute-start(f32[4,16,128]{2,1,0:T(8,128)S(1)} %get-tuple-element.277), channel_id=1, source_target_pairs={{0,8},{1,9},{2,10},{3,11},{4,12},{5,13},{6,14},{7,15},{8,0},{9,1},... | collective-permute-start | bytes 98312 | tf_op jit(solution)/shard_map/ppermute | solution.py:435
  9.2 9.7 %collective-permute-start.10 = (f32[4,16,128]{2,1,0:T(8,128)S(1)}, f32[4,16,128]{2,1,0:T(8,128)S(1)}, u32[]{:S(2)}, u32[]{:S(2)}) collective-permute-start(f32[4,16,128]{2,1,0:T(8,128)S(1)} %get-tuple-element.278), channel_id=1, source_target_pairs={{0,2},{1,3},{2,0},{3,1},{4,6},{5,7},{6,4},{7,5},{8,10},{9,11},{10,... | collective-permute-start | bytes 98312 | tf_op jit(solution)/shard_map/ppermute | solution.py:435
  10.6 8.2 %collective-permute-start.11 = (f32[4,16,128]{2,1,0:T(8,128)S(1)}, f32[4,16,128]{2,1,0:T(8,128)S(1)}, u32[]{:S(2)}, u32[]{:S(2)}) collective-permute-start(f32[4,16,128]{2,1,0:T(8,128)S(1)} %get-tuple-element.279), channel_id=1, source_target_pairs={{0,1},{1,0},{2,3},{3,2},{4,5},{5,4},{6,7},{7,6},{8,9},{9,8},{10,11... | collective-permute-start | bytes 98312 | tf_op jit(solution)/shard_map/ppermute | solution.py:435
  20.1 9.3 %collective-permute-start.12 = (f32[4,16,128]{2,1,0:T(8,128)S(1)}, f32[4,16,128]{2,1,0:T(8,128)S(1)}, u32[]{:S(2)}, u32[]{:S(2)}) collective-permute-start(f32[4,16,128]{2,1,0:T(8,128)S(1)} %get-tuple-element.281), channel_id=1, source_target_pairs={{0,31},{1,2},{2,1},{3,4},{4,3},{5,6},{6,5},{7,8},{8,7},{9,10},{10,... | collective-permute-start | bytes 98312 | tf_op jit(solution)/shard_map/ppermute | solution.py:435
  24.6 7.5 %collective-permute-start.13 = (f32[4,16,128]{2,1,0:T(8,128)S(1)}, f32[4,16,128]{2,1,0:T(8,128)S(1)}, u32[]{:S(2)}, u32[]{:S(2)}) collective-permute-start(f32[4,16,128]{2,1,0:T(8,128)S(1)} %get-tuple-element.282), channel_id=1, source_target_pairs={{0,30},{1,31},{2,4},{3,5},{4,2},{5,3},{6,8},{7,9},{8,6},{9,7},{10,... | collective-permute-start | bytes 98312 | tf_op jit(solution)/shard_map/ppermute | solution.py:435
  25.4 6.7 %collective-permute-start.14 = (f32[4,16,128]{2,1,0:T(8,128)S(1)}, f32[4,16,128]{2,1,0:T(8,128)S(1)}, u32[]{:S(2)}, u32[]{:S(2)}) collective-permute-start(f32[4,16,128]{2,1,0:T(8,128)S(1)} %get-tuple-element.283), channel_id=1, source_target_pairs={{0,24},{1,25},{2,26},{3,27},{4,28},{5,29},{6,30},{7,31},{8,16},{9,... | collective-permute-start | bytes 98312 | tf_op jit(solution)/shard_map/ppermute | solution.py:435
  27.4 4.7 %collective-permute-start.15 = (f32[4,16,128]{2,1,0:T(8,128)S(1)}, f32[4,16,128]{2,1,0:T(8,128)S(1)}, u32[]{:S(2)}, u32[]{:S(2)}) collective-permute-start(f32[4,16,128]{2,1,0:T(8,128)S(1)} %get-tuple-element.284), channel_id=1, source_target_pairs={{0,8},{1,9},{2,10},{3,11},{4,12},{5,13},{6,14},{7,15},{8,0},{9,1},... | collective-permute-start | bytes 98312 | tf_op jit(solution)/shard_map/ppermute | solution.py:435
  29.4 3.9 %collective-permute-start.16 = (f32[4,16,128]{2,1,0:T(8,128)S(1)}, f32[4,16,128]{2,1,0:T(8,128)S(1)}, u32[]{:S(2)}, u32[]{:S(2)}) collective-permute-start(f32[4,16,128]{2,1,0:T(8,128)S(1)} %get-tuple-element.285), channel_id=1, source_target_pairs={{0,2},{1,3},{2,0},{3,1},{4,6},{5,7},{6,4},{7,5},{8,10},{9,11},{10,... | collective-permute-start | bytes 98312 | tf_op jit(solution)/shard_map/ppermute | solution.py:435
  29.4 3.9 %collective-permute-start.17 = (f32[4,16,128]{2,1,0:T(8,128)S(1)}, f32[4,16,128]{2,1,0:T(8,128)S(1)}, u32[]{:S(2)}, u32[]{:S(2)}) collective-permute-start(f32[4,16,128]{2,1,0:T(8,128)S(1)} %get-tuple-element.286), channel_id=1, source_target_pairs={{0,1},{1,0},{2,3},{3,2},{4,5},{5,4},{6,7},{7,6},{8,9},{9,8},{10,11... | collective-permute-start | bytes 98312 | tf_op jit(solution)/shard_map/ppermute | solution.py:435
  34.5 8.1 %collective-permute-start.18 = (f32[4,16,128]{2,1,0:T(8,128)S(1)}, f32[4,16,128]{2,1,0:T(8,128)S(1)}, u32[]{:S(2)}, u32[]{:S(2)}) collective-permute-start(f32[4,16,128]{2,1,0:T(8,128)S(1)} %get-tuple-element.289), channel_id=1, source_target_pairs={{0,31},{1,2},{2,1},{3,4},{4,3},{5,6},{6,5},{7,8},{8,7},{9,10},{10,... | collective-permute-start | bytes 98312 | tf_op jit(solution)/shard_map/ppermute | solution.py:435
  38.4 7.6 %collective-permute-start.19 = (f32[4,16,128]{2,1,0:T(8,128)S(1)}, f32[4,16,128]{2,1,0:T(8,128)S(1)}, u32[]{:S(2)}, u32[]{:S(2)}) collective-permute-start(f32[4,16,128]{2,1,0:T(8,128)S(1)} %get-tuple-element.290), channel_id=1, source_target_pairs={{0,30},{1,31},{2,4},{3,5},{4,2},{5,3},{6,8},{7,9},{8,6},{9,7},{10,... | collective-permute-start | bytes 98312 | tf_op jit(solution)/shard_map/ppermute | solution.py:435
  40.5 5.7 %collective-permute-start.20 = (f32[4,16,128]{2,1,0:T(8,128)S(1)}, f32[4,16,128]{2,1,0:T(8,128)S(1)}, u32[]{:S(2)}, u32[]{:S(2)}) collective-permute-start(f32[4,16,128]{2,1,0:T(8,128)S(1)} %get-tuple-element.291), channel_id=1, source_target_pairs={{0,24},{1,25},{2,26},{3,27},{4,28},{5,29},{6,30},{7,31},{8,16},{9,... | collective-permute-start | bytes 98312 | tf_op jit(solution)/shard_map/ppermute | solution.py:435
  41.4 4.7 %collective-permute-start.21 = (f32[4,16,128]{2,1,0:T(8,128)S(1)}, f32[4,16,128]{2,1,0:T(8,128)S(1)}, u32[]{:S(2)}, u32[]{:S(2)}) collective-permute-start(f32[4,16,128]{2,1,0:T(8,128)S(1)} %get-tuple-element.292), channel_id=1, source_target_pairs={{0,8},{1,9},{2,10},{3,11},{4,12},{5,13},{6,14},{7,15},{8,0},{9,1},... | collective-permute-start | bytes 98312 | tf_op jit(solution)/shard_map/ppermute | solution.py:435
  42.6 3.9 %collective-permute-start.22 = (f32[4,16,128]{2,1,0:T(8,128)S(1)}, f32[4,16,128]{2,1,0:T(8,128)S(1)}, u32[]{:S(2)}, u32[]{:S(2)}) collective-permute-start(f32[4,16,128]{2,1,0:T(8,128)S(1)} %get-tuple-element.293), channel_id=1, source_target_pairs={{0,2},{1,3},{2,0},{3,1},{4,6},{5,7},{6,4},{7,5},{8,10},{9,11},{10,... | collective-permute-start | bytes 98312 | tf_op jit(solution)/shard_map/ppermute | solution.py:435
  42.6 3.9 %collective-permute-start.23 = (f32[4,16,128]{2,1,0:T(8,128)S(1)}, f32[4,16,128]{2,1,0:T(8,128)S(1)}, u32[]{:S(2)}, u32[]{:S(2)}) collective-permute-start(f32[4,16,128]{2,1,0:T(8,128)S(1)} %get-tuple-element.294), channel_id=1, source_target_pairs={{0,1},{1,0},{2,3},{3,2},{4,5},{5,4},{6,7},{7,6},{8,9},{9,8},{10,11... | collective-permute-start | bytes 98312 | tf_op jit(solution)/shard_map/ppermute | solution.py:435
  48.5 21.0 %copy-start.1 = (f32[1,6,4,128,128]{4,3,2,1,0:T(8,128)S(1)}, f32[1,6,4,128,128]{4,3,2,1,0:T(8,128)}, u32[]{:S(2)}) copy-start(f32[1,6,4,128,128]{4,3,2,1,0:T(8,128)} %link_hbm.1) | copy-start | bytes 4718596
  48.5 21.0 %copy-start.3 = (f32[32,16,128]{2,1,0:T(8,128)S(1)}, f32[32,16,128]{2,1,0:T(8,128)}, u32[]{:S(2)}) copy-start(f32[32,16,128]{2,1,0:T(8,128)} %field_hbm.3) | copy-start | bytes 786436
  48.5 21.0 %copy-start.4 = (s32[1,6,4]{1,2,0:T(4,128)S(1)}, s32[1,6,4]{1,2,0:T(4,128)}, u32[]{:S(2)}) copy-start(s32[1,6,4]{1,2,0:T(4,128)} %param.14) | copy-start | bytes 292

commit v3 on v2

--- a/solution.py
+++ b/solution.py
@@ -10,6 +10,7 @@
 
 ITERS = 3
 TRUSTED_PIVOT = 0.008
+AHEAD = 3
 HIGHEST = lax.Precision.HIGHEST
 LEVELS = ITERS + 1
 PIECES = 3
@@ -107,7 +108,9 @@
     out_ref[2 * pair + 1] = total[:, size:]
 
 
-def band_kernel(weights_ref, split_ref, out_ref):
+def band_kernel(pad, weights_ref, field_ref, out_ref, split_ref):
+    split_field(field_ref, split_ref, pad)
+
     def body(pair, carry):
         pair_product(weights_ref, split_ref, out_ref, pair)
         return carry
@@ -144,6 +147,7 @@
     def convert(step, carry):
         here = pl.ds(2 * step, 2)
         pltpu.make_async_copy(band_hbm.at[here], band_ref.at[here], sems.at[step]).wait()
+        pair_product(weights_ref, split_ref, out_ref, jnp.maximum(step - 2, 0))
         for even in range(2):
             for k in range(band):
                 shift = (even + k - half) // 2
@@ -155,10 +159,10 @@
                 cols = slice(col * size, (col + 1) * size)
                 weights_ref[step + shift + 1, place, :, cols] = high
                 weights_ref[step + shift + 1, span + place, :, cols] = low
-        pair_product(weights_ref, split_ref, out_ref, jnp.maximum(step - 1, 0))
         return carry
 
     lax.fori_loop(0, pairs, convert, 0)
+    pair_product(weights_ref, split_ref, out_ref, pairs - 2)
     pair_product(weights_ref, split_ref, out_ref, pairs - 1)
     copies[-1].wait()
 
@@ -193,50 +197,47 @@
                 field_ref[row] = field_ref[row] + fold(part, width)
 
 
-def link_kernel(dev_count, pad, rows_ref, base_ref, links_ref, *refs):
+def link_kernel(dev_count, rows_ref, base_ref, links_ref, *refs):
     count = len(MATCHINGS)
-    far_refs, split_ref, out_refs, field_ref = refs[:count], refs[count], refs[count + 1 : -1], refs[-1]
+    far_refs, field_ref, out_refs = refs[:count], refs[count], refs[count + 1 :]
     add_links(dev_count, rows_ref, base_ref, links_ref, far_refs, field_ref)
     send_rows(dev_count, rows_ref, field_ref, out_refs)
-    split_field(field_ref, split_ref, pad)
-
-
-def gram_rows(left, split_refs, cols):
-    width = split_refs[0].shape[0] // PIECES
-    right = [ref[piece * width : (piece + 1) * width, cols] for piece in range(PIECES) for ref in split_refs]
-    fill = [jnp.zeros_like(right[0])] * (2 * 128 // width - len(right))
-    return lax.dot_general(
-        left, jnp.concatenate(right + fill, axis=0), (((1,), (1,)), ((), ())), preferred_element_type=F32
-    )
-
-
-def fold_lanes(value):
-    first = value[:, :128]
-    return value[:, 128:] + (first + pltpu.roll(first, 64, 1))
-
-
-def gram_kernel(pad, split0, split1, split2, out_ref, total):
-    rows, lanes = split0.shape
+
+
+def gram(pad, left_refs, right_refs):
+    rows, lanes = left_refs[0].shape
     width = rows // PIECES
-    refs = (split0, split1, split2, split2)
-    inner = lanes - 2 * pad * 128
-    chunk = inner // 8
-    total[...] = jnp.zeros_like(total)
-
-    def body(step, carry):
-        cols = pl.ds(pl.multiple_of(pad * 128 + step * chunk, 128), chunk)
-        left = jnp.concatenate([ref[:, cols] for ref in refs[:3]], axis=0)
-        total[...] += gram_rows(left, refs, cols)
-        return carry
-
-    lax.fori_loop(0, 8, body, 0)
-    z = [fold_lanes(fold(total[rows * k : rows * (k + 1)], width)) for k in range(3)]
-    lane = lax.broadcasted_iota(jnp.int32, z[0].shape, 1)
-    out_ref[...] = jnp.where(
-        lane < 2 * width,
-        z[0],
-        jnp.where(lane < 4 * width, pltpu.roll(z[1], width, 1), pltpu.roll(z[2], 2 * width, 1)),
-    )
+    cols = slice(pad * 128, lanes - pad * 128)
+    left = jnp.concatenate([ref[:, cols] for ref in left_refs], axis=0)
+    right = [ref[piece * width : (piece + 1) * width, cols] for piece in range(PIECES) for ref in right_refs]
+    right += [jnp.zeros_like(right[0])] * (128 // width - len(right))
+    dims = (((1,), (1,)), ((), ()))
+    product = lax.dot_general(left, jnp.concatenate(right, axis=0), dims, preferred_element_type=F32)
+    step = len(right_refs) * width
+    sums = []
+    for k in range(len(left_refs)):
+        part = fold(product[rows * k : rows * (k + 1)], width)
+        total = part
+        for piece in range(1, PIECES):
+            total = total + pltpu.roll(part, 128 - piece * step, 1)
+        sums.append(total)
+    return sums
+
+
+def lane_of(value):
+    return lax.broadcasted_iota(jnp.int32, value.shape, 1)
+
+
+def early_gram_kernel(pad, split0, split1, out_ref):
+    width = out_ref.shape[0]
+    first, second = gram(pad, (split0, split1), (split0, split1))
+    out_ref[...] = jnp.where(lane_of(first) < 2 * width, first, pltpu.roll(second, width, 1))
+
+
+def late_gram_kernel(pad, split1, split2, early_ref, out_ref):
+    width = out_ref.shape[0]
+    (late,) = gram(pad, (split2,), (split1, split2))
+    out_ref[...] = jnp.where(lane_of(late) < 3 * width, early_ref[...], pltpu.roll(late, 3 * width, 1))
 
 
 def places(width, lanes):
@@ -285,12 +286,9 @@
     far_refs, split_ref, out_ref, field_ref = refs[:count], refs[count], refs[count + 1], refs[-1]
     add_links(dev_count, rows_ref, base_ref, links_ref, far_refs, field_ref)
     split_field(field_ref, split_ref, pad)
-    rows, lanes = split2.shape
-    width = rows // PIECES
-    cols = slice(pad * 128, lanes - pad * 128)
-    z = fold_lanes(fold(gram_rows(split2[:, cols], (split2, split2, split2, split_ref), cols), width))
-    lane = lax.broadcasted_iota(jnp.int32, z.shape, 1)
-    mine = jnp.where(lane < 5 * width, moments_ref[...], pltpu.roll(z, 2 * width, 1))
+    width = moments_ref.shape[0]
+    (last,) = gram(pad, (split2,), (split_ref,))
+    mine = jnp.where(lane_of(last) < 5 * width, moments_ref[...], pltpu.roll(last, 5 * width, 1))
     mine = pack(mine)
     for peer in range(out_ref.shape[0]):
         out_ref[peer] = mine
@@ -310,24 +308,29 @@
     across = lax.broadcasted_iota(jnp.int32, table.shape, 1) == lax.broadcasted_iota(jnp.int32, table.shape, 0)
     diagonal = jnp.sum(jnp.where(across, table, 0.0), axis=0, keepdims=True)
     pivots = jnp.zeros((1, lanes), F32)
+    column = lambda k: jnp.broadcast_to(table[:, k : k + 1], table.shape)
+    ahead = {k: (column(k), column(k + 1)) for k in range(0, 2 * AHEAD, 2)}
     for k in range(0, ITERS * width, 2):
         if k and k % 8 == 0:
             table = table[8:]
+            ahead = {key: (one[8:], two[8:]) for key, (one, two) in ahead.items()}
+        if k + 2 * AHEAD < ITERS * width:
+            ahead[k + 2 * AHEAD] = (column(k + 2 * AHEAD), column(k + 2 * AHEAD + 1))
         at = k % 8
-        first, second = table[at : at + 1], table[at + 1 : at + 2]
-        left, right = table[:, k : k + 1], table[:, k + 1 : k + 2]
+        left, right = ahead.pop(k)
         p11, p12 = left[at : at + 1], right[at : at + 1]
         p21, p22 = left[at + 1 : at + 2], right[at + 1 : at + 2]
         det = p11 * p22 - p12 * p21
         inverse = 1.0 / det
         pivots = jnp.where(lane == k, p11, jnp.where(lane == k + 1, det / p11, pivots))
         left, right = (left * p22 - right * p21) * inverse, (right * p11 - left * p12) * inverse
-        rest = table - left * first - right * second
-        table = jnp.where(lane == k, left, jnp.where(lane == k + 1, right, rest))
+        clear = lambda value: value - left * value[at : at + 1] - right * value[at + 1 : at + 2]
+        ahead = {key: (clear(one), clear(two)) for key, (one, two) in ahead.items()}
+        table = jnp.where(lane == k, left, jnp.where(lane == k + 1, right, clear(table)))
     trusted = (pivots > TRUSTED_PIVOT * diagonal) & (pivots < jnp.inf)
     used = lane < ITERS * width
     doubt = jnp.where(used & jnp.logical_not(trusted), 1.0, 0.0)
-    doubt_ref[...] = jnp.broadcast_to(jnp.max(doubt, axis=1, keepdims=True), doubt_ref.shape)
+    doubt_ref[0] = jnp.max(doubt).astype(jnp.int32)
     coeffs = table[-width:]
     lane = lax.broadcasted_iota(jnp.int32, coeffs.shape, 1)
     unit = (lane == lax.broadcasted_iota(jnp.int32, coeffs.shape, 0)).astype(F32)
@@ -476,39 +479,39 @@
     )(right_side, band_blocks, link_blocks)
 
     splits = [split0]
+    moments = None
     for level in range(ITERS):
         if level > 0:
-            base = pl.pallas_call(
-                band_kernel,
-                out_shape=field,
+            base, latest = pl.pallas_call(
+                functools.partial(band_kernel, half),
+                out_shape=[field, split],
                 in_specs=vmem(2),
-                out_specs=vmem(1)[0],
+                out_specs=vmem(2),
                 compiler_params=params(8),
                 cost_estimate=pl.CostEstimate(flops=10**9, bytes_accessed=12 * 10**6, transcendentals=0),
                 name="band",
-            )(weights, splits[-1])
+            )(weights, values)
+            splits.append(latest)
+            late = level == ITERS - 1
+            moments = pl.pallas_call(
+                functools.partial(late_gram_kernel if late else early_gram_kernel, half),
+                out_shape=jax.ShapeDtypeStruct((width, 128), F32),
+                in_specs=vmem(2 + late),
+                out_specs=vmem(1)[0],
+                compiler_params=params(8),
+                cost_estimate=pl.CostEstimate(flops=10**9, bytes_accessed=4 * 10**6, transcendentals=0),
+                name="gram",
+            )(*splits[-2:], *([moments] if late else []))
         if level + 1 < ITERS:
-            outs = pl.pallas_call(
-                functools.partial(link_kernel, dev_count, half),
-                out_shape=[split] + [message] * count,
+            values, *messages = pl.pallas_call(
+                functools.partial(link_kernel, dev_count),
+                out_shape=[field] + [message] * count,
                 in_specs=[smem()] + vmem(2 + count),
                 out_specs=vmem(1 + count),
-                scratch_shapes=[pltpu.VMEM(right_side.shape, F32)],
                 compiler_params=params(8),
                 name="link",
             )(slot_rows, base, links, *far)
-            splits.append(outs[0])
-            far = exchange(outs[1:])
-    moments = pl.pallas_call(
-        functools.partial(gram_kernel, half),
-        out_shape=jax.ShapeDtypeStruct((width, 128), F32),
-        in_specs=vmem(ITERS),
-        out_specs=vmem(1)[0],
-        scratch_shapes=[pltpu.VMEM((ITERS * PIECES * width, 256), F32)],
-        compiler_params=params(8),
-        cost_estimate=pl.CostEstimate(flops=10**9, bytes_accessed=4 * 10**6, transcendentals=0),
-        name="gram",
-    )(*splits)
+            far = exchange(messages)
     split3, mine = pl.pallas_call(
         functools.partial(last_link_kernel, dev_count, half),
         out_shape=[split, jax.ShapeDtypeStruct((dev_count, width // 2, 128), F32)],
@@ -522,17 +525,17 @@
     gathered = lax.all_to_all(mine, "dom", 0, 0)
     value, rest, doubt = pl.pallas_call(
         functools.partial(finish_kernel, half),
-        out_shape=[field, field, jax.ShapeDtypeStruct((8, 128), F32)],
+        out_shape=[field, field, jax.ShapeDtypeStruct((1,), jnp.int32)],
         in_specs=vmem(1 + LEVELS),
-        out_specs=vmem(3),
+        out_specs=vmem(2) + [smem()],
         compiler_params=params(8),
         name="finish",
     )(gathered, *splits)
-    again = lambda state: state[0][0, 0] > 0.0
+    again = lambda state: state[0][0] > 0
 
     def redo(state):
         held, flag = lax.optimization_barrier((args, state[0]))
-        return 0.0 * flag, *classical(*held)
+        return 0 * flag, *classical(*held)
 
     return lax.while_loop(again, redo, (doubt, value, rest))[1:]
 

time: 72.1 us -> 66.5 us (0.922)
  Pallas kernels: 29.3 us -> 22.6 us
  waiting for transfers between devices: 3.52 us -> 6.03 us
  local copies, waits for them, and re-layouts: 1.29 us -> 0.02 us
    pallas_call x1, Pallas kernels: 9.04 us -> 3.28 us  [shards(): pl.pallas_call(functools.partial(finish_kernel, half), out_shape=[field,...]
    ppermute x18, waiting for transfers between devices: 3.52 us -> 6.03 us  [exchange(): lax.ppermute(messages[index], 'dom', matching_pairs(dev_count, pair, phase))]
    slice x1 -> x0, local copies, waits for them, and re-layouts: 1.27 us -> none  [shards(): again = lambda state: state[0][0, 0] > 0.0]
    pallas_call x5 -> x6, Pallas kernels: 9.12 us -> 8.24 us  [the longest x2 5.03 us: shards(): pl.pallas_call(functools.partial(band_kernel, half), out_shape=[field, sp...]
  transfers between devices with their start and end apart: 18 -> 18, of which waited for: 5 -> 4; matrix products, arithmetic and copies ran while one was open for 0% -> 0% of each run, Pallas kernels for 21% -> 21%
where the time goes in v3:
time: 66.5 us; the launch traced here: 66.2 us
  starting transfers between devices  24 us (36%)
  Pallas kernels  22.6 us (34%)
  blocking collectives  11.6 us (17%)
  waiting for transfers between devices  6.03 us (9%)
  between operations  1.02 us (2%)
  loops' own time  0.88 us (1%)
    ppermute x18, starting transfers between devices, exchange(): lax.ppermute(messages[index], 'dom', matching_pairs(dev_count, pair, phase))  24 us
    all_to_all x1, blocking collectives, shards(): gathered = lax.all_to_all(mine, 'dom', 0, 0)  11.6 us
    pallas_call x1, Pallas kernels, shards(): pl.pallas_call(functools.partial(prepare_kernel, half), out_shape=[pltpu....  8.17 us
    ppermute x18, waiting for transfers between devices, exchange(): lax.ppermute(messages[index], 'dom', matching_pairs(dev_count, pair, phase))  6.03 us
    pallas_call x2, Pallas kernels, shards(): pl.pallas_call(functools.partial(band_kernel, half), out_shape=[field, sp...  5.03 us
    pallas_call x1, Pallas kernels, shards(): pl.pallas_call(functools.partial(finish_kernel, half), out_shape=[field,...  3.28 us
    pallas_call x2, Pallas kernels, shards(): pl.pallas_call(functools.partial(link_kernel, dev_count), out_shape=[fiel...  2.23 us
    pallas_call x1, Pallas kernels, shards(): pl.pallas_call(functools.partial(last_link_kernel, dev_count, half), out_...  1.92 us
  transfers between devices with their start and end apart: 18, of which 4 were waited for; matrix products, arithmetic and copies ran while one was open for 0% of the time, Pallas kernels for 21%

profile of v3, /device:TPU:0, one launch (start us, length us, event | category | flops | bytes accessed | tf_op | source)
XLA Modules:
  0.0 66.2 jit_solution(8600418409107312766)
XLA Ops:
  0.6 1.0 %first_send.1 = (f32[4,16,128]{2,1,0:T(8,128)S(1)}, f32[4,16,128]{2,1,0:T(8,128)S(1)}, f32[4,16,128]{2,1,0:T(8,128)S(1)}, f32[4,16,128]{2,1,0:T(8,128)S(1)}, f32...) custom-call(s32[1,4,6]{2,1,0:T(4,128)} %bitcast.240, f32[32,16,128]{2,1,0:T(8,128)} %field_hbm.3), custom_call_target="tpu_custom_call" | custom-call | tf_op jit(solution)/shard_map/first_send/pallas_call | solution.py:446
  1.6 6.5 %collective-permute-start.6 = (f32[4,16,128]{2,1,0:T(8,128)S(1)}, f32[4,16,128]{2,1,0:T(8,128)S(1)}, u32[]{:S(2)}, u32[]{:S(2)}) collective-permute-start(f32[4,16,128]{2,1,0:T(8,128)S(1)} %get-tuple-element.202), channel_id=1, source_target_pairs={{0,31},{1,2},{2,1},{3,4},{4,3},{5,6},{6,5},{7,8},{8,7},{9,10},{10,... | collective-permute-start | bytes 98312 | tf_op jit(solution)/shard_map/ppermute | solution.py:438
  8.1 0.6 collective-permute-start.7
  8.7 0.4 collective-permute-start.8
  9.2 0.0 collective-permute-start.9
  9.2 1.4 %collective-permute-start.10 = (f32[4,16,128]{2,1,0:T(8,128)S(1)}, f32[4,16,128]{2,1,0:T(8,128)S(1)}, u32[]{:S(2)}, u32[]{:S(2)}) collective-permute-start(f32[4,16,128]{2,1,0:T(8,128)S(1)} %get-tuple-element.206), channel_id=1, source_target_pairs={{0,2},{1,3},{2,0},{3,1},{4,6},{5,7},{6,4},{7,5},{8,10},{9,11},{10,... | collective-permute-start | bytes 98312 | tf_op jit(solution)/shard_map/ppermute | solution.py:438
  10.6 0.0 collective-permute-done.6.refs_0_
  10.6 0.0 collective-permute-start.11
  10.6 8.2 %prepare.1 = (bf16[18,12,128,256]{3,2,1,0:T(8,128)(2,1)S(1)}, bf16[6,2,256,256]{3,2,1,0:T(8,128)(2,1)S(1)}, bf16[48,4608]{1,0:T(8,128)(2,1)S(1)}, f32[32,16,128]{2,1,0:T(8,128)S(1)}) custom-call(f32[32,16,128]{2,1,0:T(8,128)} %field_hbm.3, f32[32,5,128,128]{3,2,1,0:T(8,128)} %band_hbm.1, f32[1,6,4,128,128]{4,3,2,1,0:T(8,128)} %link_hbm.1), custom_call_target="tpu_custom_call" | custom-call | flops 1000000000 | bytes 12000000 | tf_op jit(solution)/shard_map/prepare/pallas_call | solution.py:460
  18.8 0.0 collective-permute-done.7.refs_1_
  18.8 0.0 collective-permute-done.8.refs_2_
  18.8 0.0 collective-permute-done.9.refs_3_
  18.9 0.0 collective-permute-done.10.refs_4_
  18.9 0.0 collective-permute-done.11.refs_5_
  18.9 1.1 %link.2 = (f32[32,16,128]{2,1,0:T(8,128)S(1)}, f32[4,16,128]{2,1,0:T(8,128)S(1)}, f32[4,16,128]{2,1,0:T(8,128)S(1)}, f32[4,16,128]{2,1,0:T(8,128)S(1)}, f32[4,16...) custom-call(s32[1,4,6]{2,1,0:T(4,128)} %bitcast.241, ...), custom_call_target="tpu_custom_call" | custom-call | tf_op jit(solution)/shard_map/link/pallas_call | solution.py:506
  20.0 4.5 %collective-permute-start.12 = (f32[4,16,128]{2,1,0:T(8,128)S(1)}, f32[4,16,128]{2,1,0:T(8,128)S(1)}, u32[]{:S(2)}, u32[]{:S(2)}) collective-permute-start(f32[4,16,128]{2,1,0:T(8,128)S(1)} %get-tuple-element.210), channel_id=1, source_target_pairs={{0,31},{1,2},{2,1},{3,4},{4,3},{5,6},{6,5},{7,8},{8,7},{9,10},{10,... | collective-permute-start | bytes 98312 | tf_op jit(solution)/shard_map/ppermute | solution.py:438
  24.5 0.8 %collective-permute-start.13 = (f32[4,16,128]{2,1,0:T(8,128)S(1)}, f32[4,16,128]{2,1,0:T(8,128)S(1)}, u32[]{:S(2)}, u32[]{:S(2)}) collective-permute-start(f32[4,16,128]{2,1,0:T(8,128)S(1)} %get-tuple-element.211), channel_id=1, source_target_pairs={{0,30},{1,31},{2,4},{3,5},{4,2},{5,3},{6,8},{7,9},{8,6},{9,7},{10,... | collective-permute-start | bytes 98312 | tf_op jit(solution)/shard_map/ppermute | solution.py:438
  25.3 2.0 %collective-permute-start.14 = (f32[4,16,128]{2,1,0:T(8,128)S(1)}, f32[4,16,128]{2,1,0:T(8,128)S(1)}, u32[]{:S(2)}, u32[]{:S(2)}) collective-permute-start(f32[4,16,128]{2,1,0:T(8,128)S(1)} %get-tuple-element.212), channel_id=1, source_target_pairs={{0,24},{1,25},{2,26},{3,27},{4,28},{5,29},{6,30},{7,31},{8,16},{9,... | collective-permute-start | bytes 98312 | tf_op jit(solution)/shard_map/ppermute | solution.py:438
  27.3 2.0 %collective-permute-start.15 = (f32[4,16,128]{2,1,0:T(8,128)S(1)}, f32[4,16,128]{2,1,0:T(8,128)S(1)}, u32[]{:S(2)}, u32[]{:S(2)}) collective-permute-start(f32[4,16,128]{2,1,0:T(8,128)S(1)} %get-tuple-element.213), channel_id=1, source_target_pairs={{0,8},{1,9},{2,10},{3,11},{4,12},{5,13},{6,14},{7,15},{8,0},{9,1},... | collective-permute-start | bytes 98312 | tf_op jit(solution)/shard_map/ppermute | solution.py:438
  29.3 2.5 %band.2 = (f32[32,16,128]{2,1,0:T(8,128)S(1)}, bf16[48,4608]{1,0:T(8,128)(2,1)S(1)}) custom-call(bf16[18,12,128,256]{3,2,1,0:T(8,128)(2,1)S(1)} %get-tuple-element.199.weights_ref, f32[32,16,128]{2,1,0:T(8,128)S(1)} %get-tuple-element.208.field_ref), custom_call_target="tpu_custom_call" | custom-call | flops 1000000000 | bytes 12000000 | tf_op jit(solution)/shard_map/band/pallas_call | solution.py:485
  31.9 0.0 collective-permute-start.16
  31.9 0.0 collective-permute-done.12.refs_0_
  31.9 0.1 collective-permute-start.17
  32.0 0.5 gram.2.early_ref
  32.5 0.0 collective-permute-done.13.refs_1_
  32.5 0.0 collective-permute-done.14.refs_2_
  32.5 0.0 collective-permute-done.15.refs_3_
  32.5 3.2 %collective-permute-done.16.refs_4_ = f32[4,16,128]{2,1,0:T(8,128)S(1)} collective-permute-done((f32[4,16,128]{2,1,0:T(8,128)S(1)}, f32[4,16,128]{2,1,0:T(8,128)S(1)}, u32[]{:S(2)}, u32[]{:S(2)}) %collective-permute-start.16) | collective-permute-done | bytes 32800 | tf_op jit(solution)/shard_map/ppermute | solution.py:438
  35.8 0.0 collective-permute-done.17.refs_5_
  35.8 1.1 %link.3 = (f32[32,16,128]{2,1,0:T(8,128)S(1)}, f32[4,16,128]{2,1,0:T(8,128)S(1)}, f32[4,16,128]{2,1,0:T(8,128)S(1)}, f32[4,16,128]{2,1,0:T(8,128)S(1)}, f32[4,16...) custom-call(s32[1,4,6]{2,1,0:T(4,128)} %bitcast.242, ...), custom_call_target="tpu_custom_call" | custom-call | tf_op jit(solution)/shard_map/link/pallas_call | solution.py:506
  36.9 0.1 collective-permute-start.18
  37.0 2.5 %band.3 = (f32[32,16,128]{2,1,0:T(8,128)S(1)}, bf16[48,4608]{1,0:T(8,128)(2,1)S(1)}) custom-call(bf16[18,12,128,256]{3,2,1,0:T(8,128)(2,1)S(1)} %get-tuple-element.199.weights_ref, f32[32,16,128]{2,1,0:T(8,128)S(1)} %get-tuple-element.216.field_ref), custom_call_target="tpu_custom_call" | custom-call | flops 1000000000 | bytes 12000000 | tf_op jit(solution)/shard_map/band/pallas_call | solution.py:485
  39.5 2.7 %collective-permute-start.19 = (f32[4,16,128]{2,1,0:T(8,128)S(1)}, f32[4,16,128]{2,1,0:T(8,128)S(1)}, u32[]{:S(2)}, u32[]{:S(2)}) collective-permute-start(f32[4,16,128]{2,1,0:T(8,128)S(1)} %get-tuple-element.222), channel_id=1, source_target_pairs={{0,30},{1,31},{2,4},{3,5},{4,2},{5,3},{6,8},{7,9},{8,6},{9,7},{10,... | collective-permute-start | bytes 98312 | tf_op jit(solution)/shard_map/ppermute | solution.py:438
  42.2 1.0 %collective-permute-start.20 = (f32[4,16,128]{2,1,0:T(8,128)S(1)}, f32[4,16,128]{2,1,0:T(8,128)S(1)}, u32[]{:S(2)}, u32[]{:S(2)}) collective-permute-start(f32[4,16,128]{2,1,0:T(8,128)S(1)} %get-tuple-element.223), channel_id=1, source_target_pairs={{0,24},{1,25},{2,26},{3,27},{4,28},{5,29},{6,30},{7,31},{8,16},{9,... | collective-permute-start | bytes 98312 | tf_op jit(solution)/shard_map/ppermute | solution.py:438
  43.2 1.1 %collective-permute-start.21 = (f32[4,16,128]{2,1,0:T(8,128)S(1)}, f32[4,16,128]{2,1,0:T(8,128)S(1)}, u32[]{:S(2)}, u32[]{:S(2)}) collective-permute-start(f32[4,16,128]{2,1,0:T(8,128)S(1)} %get-tuple-element.224), channel_id=1, source_target_pairs={{0,8},{1,9},{2,10},{3,11},{4,12},{5,13},{6,14},{7,15},{8,0},{9,1},... | collective-permute-start | bytes 98312 | tf_op jit(solution)/shard_map/ppermute | solution.py:438
  44.4 0.0 collective-permute-start.22
  44.4 0.7 %collective-permute-start.23 = (f32[4,16,128]{2,1,0:T(8,128)S(1)}, f32[4,16,128]{2,1,0:T(8,128)S(1)}, u32[]{:S(2)}, u32[]{:S(2)}) collective-permute-start(f32[4,16,128]{2,1,0:T(8,128)S(1)} %get-tuple-element.226), channel_id=1, source_target_pairs={{0,1},{1,0},{2,3},{3,2},{4,5},{5,4},{6,7},{7,6},{8,9},{9,8},{10,11... | collective-permute-start | bytes 98312 | tf_op jit(solution)/shard_map/ppermute | solution.py:438
  45.1 0.5 gram.3.moments_ref
  45.5 1.9 %collective-permute-done.19.refs_1_ = f32[4,16,128]{2,1,0:T(8,128)S(1)} collective-permute-done((f32[4,16,128]{2,1,0:T(8,128)S(1)}, f32[4,16,128]{2,1,0:T(8,128)S(1)}, u32[]{:S(2)}, u32[]{:S(2)}) %collective-permute-start.19) | collective-permute-done | bytes 32800 | tf_op jit(solution)/shard_map/ppermute | solution.py:438
  47.4 0.5 collective-permute-done.20.refs_2_
  47.9 0.3 collective-permute-done.22.refs_4_
  48.3 1.9 %last_link.1 = (bf16[48,4608]{1,0:T(8,128)(2,1)S(1)}, f32[32,8,128]{2,1,0:T(8,128)S(1)}) custom-call(s32[1,4,6]{2,1,0:T(4,128)} %bitcast.243, f32[32,16,128]{2,1,0:T(8,128)S(1)} %get-tuple-element.217.base_ref, bf16[6,2,256,256]{3,2,1,0:T(8,128)(2,1)S(1)} %get-tuple-element.201.links_ref, bf16[48,4608]{1,0:T(8,128)(2,1)S(1)} %get-tuple-element.218.split2, ...), custom_call_target="tpu_custom_call" | custom-call | tf_op jit(solution)/shard_map/last_link/pallas_call | solution.py:515
  50.2 0.0 copy-start.1
  50.2 0.0 copy-start.3
  50.2 0.0 copy-start.4
  50.2 11.6 %all_to_all.5.gathered_ref = f32[32,8,128]{2,1,0:T(8,128)S(1)} all-to-all(f32[32,8,128]{2,1,0:T(8,128)S(1)} %get-tuple-element.227), channel_id=1, replica_groups=mesh['dom'=32] {'dom'}, dimensions={0} | all-to-all | bytes 262144 | tf_op jit(solution)/shard_map/all_to_all | solution.py:525
  61.8 3.3 %finish.1 = (f32[32,16,128]{2,1,0:T(8,128)}, f32[32,16,128]{2,1,0:T(8,128)}, s32[1]{0:T(128)}) custom-call(f32[32,8,128]{2,1,0:T(8,128)S(1)} %all_to_all.5.gathered_ref, bf16[48,4608]{1,0:T(8,128)(2,1)S(1)} %get-tuple-element.220.split0, bf16[48,4608]{1,0:T(8,128)(2,1)S(1)} %get-tuple-element.219.split1, bf16[48,4608]{1,0:T(8,128)(2,1)S(1)} %get-tuple-element.218.split2, ...), custom_call_target="tpu_custom_call" | custom-call | tf_op jit(solution)/shard_map/finish/pallas_call | solution.py:526
  65.2 0.9 %while.30 = (s32[1]{0:T(128)}, f32[32,16,128]{2,1,0:T(8,128)}, f32[32,16,128]{2,1,0:T(8,128)}, f32[32,16,128]{2,1,0:T(8,128)S(1)}, f32[32,5,128,128]{3,2,1,0:T(8...) while((s32[1]{0:T(128)}, f32[32,16,128]{2,1,0:T(8,128)}, ...), condition=%region_8.11_spmd, body=%region_0.10_spmd | while | flops 189602848 | bytes 16476032 | solution.py:540
  (6 shorter events, 0.0 us)
Async XLA Ops:
  1.6 9.0 %collective-permute-start.6 = (f32[4,16,128]{2,1,0:T(8,128)S(1)}, f32[4,16,128]{2,1,0:T(8,128)S(1)}, u32[]{:S(2)}, u32[]{:S(2)}) collective-permute-start(f32[4,16,128]{2,1,0:T(8,128)S(1)} %get-tuple-element.202), channel_id=1, source_target_pairs={{0,31},{1,2},{2,1},{3,4},{4,3},{5,6},{6,5},{7,8},{8,7},{9,10},{10,... | collective-permute-start | bytes 98312 | tf_op jit(solution)/shard_map/ppermute | solution.py:438
  8.1 10.7 %collective-permute-start.7 = (f32[4,16,128]{2,1,0:T(8,128)S(1)}, f32[4,16,128]{2,1,0:T(8,128)S(1)}, u32[]{:S(2)}, u32[]{:S(2)}) collective-permute-start(f32[4,16,128]{2,1,0:T(8,128)S(1)} %get-tuple-element.203), channel_id=1, source_target_pairs={{0,30},{1,31},{2,4},{3,5},{4,2},{5,3},{6,8},{7,9},{8,6},{9,7},{10,... | collective-permute-start | bytes 98312 | tf_op jit(solution)/shard_map/ppermute | solution.py:438
  8.7 10.1 %collective-permute-start.8 = (f32[4,16,128]{2,1,0:T(8,128)S(1)}, f32[4,16,128]{2,1,0:T(8,128)S(1)}, u32[]{:S(2)}, u32[]{:S(2)}) collective-permute-start(f32[4,16,128]{2,1,0:T(8,128)S(1)} %get-tuple-element.204), channel_id=1, source_target_pairs={{0,24},{1,25},{2,26},{3,27},{4,28},{5,29},{6,30},{7,31},{8,16},{9,... | collective-permute-start | bytes 98312 | tf_op jit(solution)/shard_map/ppermute | solution.py:438
  9.2 9.7 %collective-permute-start.9 = (f32[4,16,128]{2,1,0:T(8,128)S(1)}, f32[4,16,128]{2,1,0:T(8,128)S(1)}, u32[]{:S(2)}, u32[]{:S(2)}) collective-permute-start(f32[4,16,128]{2,1,0:T(8,128)S(1)} %get-tuple-element.205), channel_id=1, source_target_pairs={{0,8},{1,9},{2,10},{3,11},{4,12},{5,13},{6,14},{7,15},{8,0},{9,1},... | collective-permute-start | bytes 98312 | tf_op jit(solution)/shard_map/ppermute | solution.py:438
  9.2 9.7 %collective-permute-start.10 = (f32[4,16,128]{2,1,0:T(8,128)S(1)}, f32[4,16,128]{2,1,0:T(8,128)S(1)}, u32[]{:S(2)}, u32[]{:S(2)}) collective-permute-start(f32[4,16,128]{2,1,0:T(8,128)S(1)} %get-tuple-element.206), channel_id=1, source_target_pairs={{0,2},{1,3},{2,0},{3,1},{4,6},{5,7},{6,4},{7,5},{8,10},{9,11},{10,... | collective-permute-start | bytes 98312 | tf_op jit(solution)/shard_map/ppermute | solution.py:438
  10.6 8.2 %collective-permute-start.11 = (f32[4,16,128]{2,1,0:T(8,128)S(1)}, f32[4,16,128]{2,1,0:T(8,128)S(1)}, u32[]{:S(2)}, u32[]{:S(2)}) collective-permute-start(f32[4,16,128]{2,1,0:T(8,128)S(1)} %get-tuple-element.207), channel_id=1, source_target_pairs={{0,1},{1,0},{2,3},{3,2},{4,5},{5,4},{6,7},{7,6},{8,9},{9,8},{10,11... | collective-permute-start | bytes 98312 | tf_op jit(solution)/shard_map/ppermute | solution.py:438
  20.0 11.9 %collective-permute-start.12 = (f32[4,16,128]{2,1,0:T(8,128)S(1)}, f32[4,16,128]{2,1,0:T(8,128)S(1)}, u32[]{:S(2)}, u32[]{:S(2)}) collective-permute-start(f32[4,16,128]{2,1,0:T(8,128)S(1)} %get-tuple-element.210), channel_id=1, source_target_pairs={{0,31},{1,2},{2,1},{3,4},{4,3},{5,6},{6,5},{7,8},{8,7},{9,10},{10,... | collective-permute-start | bytes 98312 | tf_op jit(solution)/shard_map/ppermute | solution.py:438
  24.5 8.0 %collective-permute-start.13 = (f32[4,16,128]{2,1,0:T(8,128)S(1)}, f32[4,16,128]{2,1,0:T(8,128)S(1)}, u32[]{:S(2)}, u32[]{:S(2)}) collective-permute-start(f32[4,16,128]{2,1,0:T(8,128)S(1)} %get-tuple-element.211), channel_id=1, source_target_pairs={{0,30},{1,31},{2,4},{3,5},{4,2},{5,3},{6,8},{7,9},{8,6},{9,7},{10,... | collective-permute-start | bytes 98312 | tf_op jit(solution)/shard_map/ppermute | solution.py:438
  25.3 7.2 %collective-permute-start.14 = (f32[4,16,128]{2,1,0:T(8,128)S(1)}, f32[4,16,128]{2,1,0:T(8,128)S(1)}, u32[]{:S(2)}, u32[]{:S(2)}) collective-permute-start(f32[4,16,128]{2,1,0:T(8,128)S(1)} %get-tuple-element.212), channel_id=1, source_target_pairs={{0,24},{1,25},{2,26},{3,27},{4,28},{5,29},{6,30},{7,31},{8,16},{9,... | collective-permute-start | bytes 98312 | tf_op jit(solution)/shard_map/ppermute | solution.py:438
  27.3 5.2 %collective-permute-start.15 = (f32[4,16,128]{2,1,0:T(8,128)S(1)}, f32[4,16,128]{2,1,0:T(8,128)S(1)}, u32[]{:S(2)}, u32[]{:S(2)}) collective-permute-start(f32[4,16,128]{2,1,0:T(8,128)S(1)} %get-tuple-element.213), channel_id=1, source_target_pairs={{0,8},{1,9},{2,10},{3,11},{4,12},{5,13},{6,14},{7,15},{8,0},{9,1},... | collective-permute-start | bytes 98312 | tf_op jit(solution)/shard_map/ppermute | solution.py:438
  31.9 3.9 %collective-permute-start.16 = (f32[4,16,128]{2,1,0:T(8,128)S(1)}, f32[4,16,128]{2,1,0:T(8,128)S(1)}, u32[]{:S(2)}, u32[]{:S(2)}) collective-permute-start(f32[4,16,128]{2,1,0:T(8,128)S(1)} %get-tuple-element.214), channel_id=1, source_target_pairs={{0,2},{1,3},{2,0},{3,1},{4,6},{5,7},{6,4},{7,5},{8,10},{9,11},{10,... | collective-permute-start | bytes 98312 | tf_op jit(solution)/shard_map/ppermute | solution.py:438
  31.9 3.9 %collective-permute-start.17 = (f32[4,16,128]{2,1,0:T(8,128)S(1)}, f32[4,16,128]{2,1,0:T(8,128)S(1)}, u32[]{:S(2)}, u32[]{:S(2)}) collective-permute-start(f32[4,16,128]{2,1,0:T(8,128)S(1)} %get-tuple-element.215), channel_id=1, source_target_pairs={{0,1},{1,0},{2,3},{3,2},{4,5},{5,4},{6,7},{7,6},{8,9},{9,8},{10,11... | collective-permute-start | bytes 98312 | tf_op jit(solution)/shard_map/ppermute | solution.py:438
  36.9 7.4 %collective-permute-start.18 = (f32[4,16,128]{2,1,0:T(8,128)S(1)}, f32[4,16,128]{2,1,0:T(8,128)S(1)}, u32[]{:S(2)}, u32[]{:S(2)}) collective-permute-start(f32[4,16,128]{2,1,0:T(8,128)S(1)} %get-tuple-element.221), channel_id=1, source_target_pairs={{0,31},{1,2},{2,1},{3,4},{4,3},{5,6},{6,5},{7,8},{8,7},{9,10},{10,... | collective-permute-start | bytes 98312 | tf_op jit(solution)/shard_map/ppermute | solution.py:438
  39.5 7.9 %collective-permute-start.19 = (f32[4,16,128]{2,1,0:T(8,128)S(1)}, f32[4,16,128]{2,1,0:T(8,128)S(1)}, u32[]{:S(2)}, u32[]{:S(2)}) collective-permute-start(f32[4,16,128]{2,1,0:T(8,128)S(1)} %get-tuple-element.222), channel_id=1, source_target_pairs={{0,30},{1,31},{2,4},{3,5},{4,2},{5,3},{6,8},{7,9},{8,6},{9,7},{10,... | collective-permute-start | bytes 98312 | tf_op jit(solution)/shard_map/ppermute | solution.py:438
  42.2 5.7 %collective-permute-start.20 = (f32[4,16,128]{2,1,0:T(8,128)S(1)}, f32[4,16,128]{2,1,0:T(8,128)S(1)}, u32[]{:S(2)}, u32[]{:S(2)}) collective-permute-start(f32[4,16,128]{2,1,0:T(8,128)S(1)} %get-tuple-element.223), channel_id=1, source_target_pairs={{0,24},{1,25},{2,26},{3,27},{4,28},{5,29},{6,30},{7,31},{8,16},{9,... | collective-permute-start | bytes 98312 | tf_op jit(solution)/shard_map/ppermute | solution.py:438
  43.2 4.7 %collective-permute-start.21 = (f32[4,16,128]{2,1,0:T(8,128)S(1)}, f32[4,16,128]{2,1,0:T(8,128)S(1)}, u32[]{:S(2)}, u32[]{:S(2)}) collective-permute-start(f32[4,16,128]{2,1,0:T(8,128)S(1)} %get-tuple-element.224), channel_id=1, source_target_pairs={{0,8},{1,9},{2,10},{3,11},{4,12},{5,13},{6,14},{7,15},{8,0},{9,1},... | collective-permute-start | bytes 98312 | tf_op jit(solution)/shard_map/ppermute | solution.py:438
  44.4 3.9 %collective-permute-start.22 = (f32[4,16,128]{2,1,0:T(8,128)S(1)}, f32[4,16,128]{2,1,0:T(8,128)S(1)}, u32[]{:S(2)}, u32[]{:S(2)}) collective-permute-start(f32[4,16,128]{2,1,0:T(8,128)S(1)} %get-tuple-element.225), channel_id=1, source_target_pairs={{0,2},{1,3},{2,0},{3,1},{4,6},{5,7},{6,4},{7,5},{8,10},{9,11},{10,... | collective-permute-start | bytes 98312 | tf_op jit(solution)/shard_map/ppermute | solution.py:438
  44.4 3.9 %collective-permute-start.23 = (f32[4,16,128]{2,1,0:T(8,128)S(1)}, f32[4,16,128]{2,1,0:T(8,128)S(1)}, u32[]{:S(2)}, u32[]{:S(2)}) collective-permute-start(f32[4,16,128]{2,1,0:T(8,128)S(1)} %get-tuple-element.226), channel_id=1, source_target_pairs={{0,1},{1,0},{2,3},{3,2},{4,5},{5,4},{6,7},{7,6},{8,9},{9,8},{10,11... | collective-permute-start | bytes 98312 | tf_op jit(solution)/shard_map/ppermute | solution.py:438
  50.2 14.9 %copy-start.1 = (f32[1,6,4,128,128]{4,3,2,1,0:T(8,128)S(1)}, f32[1,6,4,128,128]{4,3,2,1,0:T(8,128)}, u32[]{:S(2)}) copy-start(f32[1,6,4,128,128]{4,3,2,1,0:T(8,128)} %link_hbm.1) | copy-start | bytes 4718596
  50.2 14.9 %copy-start.3 = (f32[32,16,128]{2,1,0:T(8,128)S(1)}, f32[32,16,128]{2,1,0:T(8,128)}, u32[]{:S(2)}) copy-start(f32[32,16,128]{2,1,0:T(8,128)} %field_hbm.3) | copy-start | bytes 786436
  50.2 14.9 %copy-start.4 = (s32[1,6,4]{1,2,0:T(4,128)S(1)}, s32[1,6,4]{1,2,0:T(4,128)}, u32[]{:S(2)}) copy-start(s32[1,6,4]{1,2,0:T(4,128)} %param.14) | copy-start | bytes 292

commit v4 on v3

--- a/solution.py
+++ b/solution.py
@@ -119,7 +119,7 @@
 
 
 def prepare_kernel(
-    half, field_hbm, band_hbm, link_hbm, weights_ref, links_ref, split_ref, out_ref, field_ref, band_ref, link_ref, sems
+    half, field_hbm, band_hbm, link_hbm, weights_ref, links_ref, split_ref, out_ref, field_ref, band_ref, link_ref, total_ref, sems
 ):
     block_rows, band, size, _ = band_ref.shape
     faces, count = link_ref.shape[:2]
@@ -141,14 +141,16 @@
         for pair in range(1, pairs + 1):
             weights_ref[pair, copy * span, :, size:] = wide[:, :size]
             weights_ref[pair, copy * span + span - 1, :, :size] = wide[:, :size]
+    total_ref[...] = jnp.zeros_like(total_ref)
     copies[0].wait()
     split_field(field_ref, split_ref, half)
 
     def convert(step, carry):
         here = pl.ds(2 * step, 2)
         pltpu.make_async_copy(band_hbm.at[here], band_ref.at[here], sems.at[step]).wait()
-        pair_product(weights_ref, split_ref, out_ref, jnp.maximum(step - 2, 0))
         for even in range(2):
+            rows = split_ref[:, pl.ds(pl.multiple_of((half + 2 * step + even) * size, size), size)]
+            both = jnp.concatenate([rows, rows], axis=1)
             for k in range(band):
                 shift = (even + k - half) // 2
                 col = (even + k - half) % 2
@@ -159,11 +161,12 @@
                 cols = slice(col * size, (col + 1) * size)
                 weights_ref[step + shift + 1, place, :, cols] = high
                 weights_ref[step + shift + 1, span + place, :, cols] = low
+                product = jnp.dot(both, jnp.concatenate([high, low], axis=0), preferred_element_type=F32)
+                total_ref[2 * step + even + k] += fold(product, field_ref.shape[1])
         return carry
 
     lax.fori_loop(0, pairs, convert, 0)
-    pair_product(weights_ref, split_ref, out_ref, pairs - 2)
-    pair_product(weights_ref, split_ref, out_ref, pairs - 1)
+    out_ref[...] = total_ref[pl.ds(half, block_rows)]
     copies[-1].wait()
 
     def convert_links(face, carry):
@@ -471,6 +474,7 @@
             pltpu.VMEM(right_side.shape, F32),
             pltpu.VMEM(band_blocks.shape, F32),
             pltpu.VMEM(link_blocks.shape[1:], F32),
+            pltpu.VMEM((block_rows + 2 * half, width, size), F32),
             pltpu.SemaphoreType.DMA((pairs + 2,)),
         ],
         compiler_params=params(18),

time: 66.5 us -> 65.1 us (0.979)
  Pallas kernels: 22.6 us -> 21.3 us
    pallas_call x1, Pallas kernels: 8.17 us -> 6.84 us  [shards(): pl.pallas_call(functools.partial(prepare_kernel, half), out_shape=[pltpu....]
  transfers between devices with their start and end apart: 18 -> 18, of which waited for: 4 -> 4; matrix products, arithmetic and copies ran while one was open for 0% -> 0% of each run, Pallas kernels for 21% -> 20%
where the time goes in v4:
time: 65.1 us; the launch traced here: 64.9 us
  starting transfers between devices  24 us (37%)
  Pallas kernels  21.3 us (33%)
  blocking collectives  11.6 us (18%)
  waiting for transfers between devices  6.03 us (9%)
  between operations  1.02 us (2%)
  loops' own time  0.88 us (1%)
    ppermute x18, starting transfers between devices, exchange(): lax.ppermute(messages[index], 'dom', matching_pairs(dev_count, pair, phase))  24 us
    all_to_all x1, blocking collectives, shards(): gathered = lax.all_to_all(mine, 'dom', 0, 0)  11.6 us
    pallas_call x1, Pallas kernels, shards(): pl.pallas_call(functools.partial(prepare_kernel, half), out_shape=[pltpu....  6.84 us
    ppermute x18, waiting for transfers between devices, exchange(): lax.ppermute(messages[index], 'dom', matching_pairs(dev_count, pair, phase))  6.03 us
    pallas_call x2, Pallas kernels, shards(): pl.pallas_call(functools.partial(band_kernel, half), out_shape=[field, sp...  5.02 us
    pallas_call x1, Pallas kernels, shards(): pl.pallas_call(functools.partial(finish_kernel, half), out_shape=[field,...  3.28 us
    pallas_call x2, Pallas kernels, shards(): pl.pallas_call(functools.partial(link_kernel, dev_count), out_shape=[fiel...  2.23 us
    pallas_call x1, Pallas kernels, shards(): pl.pallas_call(functools.partial(last_link_kernel, dev_count, half), out_...  1.92 us
  transfers between devices with their start and end apart: 18, of which 4 were waited for; matrix products, arithmetic and copies ran while one was open for 0% of the time, Pallas kernels for 20%

profile of v4, /device:TPU:0, one launch (start us, length us, event | category | flops | bytes accessed | tf_op | source)
XLA Modules:
  0.0 64.9 jit_solution(585783611625928093)
XLA Ops:
  0.6 1.0 %first_send.1 = (f32[4,16,128]{2,1,0:T(8,128)S(1)}, f32[4,16,128]{2,1,0:T(8,128)S(1)}, f32[4,16,128]{2,1,0:T(8,128)S(1)}, f32[4,16,128]{2,1,0:T(8,128)S(1)}, f32...) custom-call(s32[1,4,6]{2,1,0:T(4,128)} %bitcast.240, f32[32,16,128]{2,1,0:T(8,128)} %field_hbm.3), custom_call_target="tpu_custom_call" | custom-call | tf_op jit(solution)/shard_map/first_send/pallas_call | solution.py:449
  1.6 6.5 %collective-permute-start.6 = (f32[4,16,128]{2,1,0:T(8,128)S(1)}, f32[4,16,128]{2,1,0:T(8,128)S(1)}, u32[]{:S(2)}, u32[]{:S(2)}) collective-permute-start(f32[4,16,128]{2,1,0:T(8,128)S(1)} %get-tuple-element.202), channel_id=1, source_target_pairs={{0,31},{1,2},{2,1},{3,4},{4,3},{5,6},{6,5},{7,8},{8,7},{9,10},{10,... | collective-permute-start | bytes 98312 | tf_op jit(solution)/shard_map/ppermute | solution.py:441
  8.1 0.6 collective-permute-start.7
  8.7 0.4 collective-permute-start.8
  9.2 0.0 collective-permute-start.9
  9.2 1.4 %collective-permute-start.10 = (f32[4,16,128]{2,1,0:T(8,128)S(1)}, f32[4,16,128]{2,1,0:T(8,128)S(1)}, u32[]{:S(2)}, u32[]{:S(2)}) collective-permute-start(f32[4,16,128]{2,1,0:T(8,128)S(1)} %get-tuple-element.206), channel_id=1, source_target_pairs={{0,2},{1,3},{2,0},{3,1},{4,6},{5,7},{6,4},{7,5},{8,10},{9,11},{10,... | collective-permute-start | bytes 98312 | tf_op jit(solution)/shard_map/ppermute | solution.py:441
  10.6 0.0 collective-permute-done.6.refs_0_
  10.6 0.0 collective-permute-start.11
  10.6 6.8 %prepare.1 = (bf16[18,12,128,256]{3,2,1,0:T(8,128)(2,1)S(1)}, bf16[6,2,256,256]{3,2,1,0:T(8,128)(2,1)S(1)}, bf16[48,4608]{1,0:T(8,128)(2,1)S(1)}, f32[32,16,128]{2,1,0:T(8,128)S(1)}) custom-call(f32[32,16,128]{2,1,0:T(8,128)} %field_hbm.3, f32[32,5,128,128]{3,2,1,0:T(8,128)} %band_hbm.1, f32[1,6,4,128,128]{4,3,2,1,0:T(8,128)} %link_hbm.1), custom_call_target="tpu_custom_call" | custom-call | flops 1000000000 | bytes 12000000 | tf_op jit(solution)/shard_map/prepare/pallas_call | solution.py:463
  17.5 0.0 collective-permute-done.7.refs_1_
  17.5 0.0 collective-permute-done.8.refs_2_
  17.5 0.0 collective-permute-done.9.refs_3_
  17.5 0.0 collective-permute-done.10.refs_4_
  17.5 0.0 collective-permute-done.11.refs_5_
  17.5 1.1 %link.2 = (f32[32,16,128]{2,1,0:T(8,128)S(1)}, f32[4,16,128]{2,1,0:T(8,128)S(1)}, f32[4,16,128]{2,1,0:T(8,128)S(1)}, f32[4,16,128]{2,1,0:T(8,128)S(1)}, f32[4,16...) custom-call(s32[1,4,6]{2,1,0:T(4,128)} %bitcast.241, ...), custom_call_target="tpu_custom_call" | custom-call | tf_op jit(solution)/shard_map/link/pallas_call | solution.py:510
  18.7 4.5 %collective-permute-start.12 = (f32[4,16,128]{2,1,0:T(8,128)S(1)}, f32[4,16,128]{2,1,0:T(8,128)S(1)}, u32[]{:S(2)}, u32[]{:S(2)}) collective-permute-start(f32[4,16,128]{2,1,0:T(8,128)S(1)} %get-tuple-element.210), channel_id=1, source_target_pairs={{0,31},{1,2},{2,1},{3,4},{4,3},{5,6},{6,5},{7,8},{8,7},{9,10},{10,... | collective-permute-start | bytes 98312 | tf_op jit(solution)/shard_map/ppermute | solution.py:441
  23.2 0.8 %collective-permute-start.13 = (f32[4,16,128]{2,1,0:T(8,128)S(1)}, f32[4,16,128]{2,1,0:T(8,128)S(1)}, u32[]{:S(2)}, u32[]{:S(2)}) collective-permute-start(f32[4,16,128]{2,1,0:T(8,128)S(1)} %get-tuple-element.211), channel_id=1, source_target_pairs={{0,30},{1,31},{2,4},{3,5},{4,2},{5,3},{6,8},{7,9},{8,6},{9,7},{10,... | collective-permute-start | bytes 98312 | tf_op jit(solution)/shard_map/ppermute | solution.py:441
  24.0 2.0 %collective-permute-start.14 = (f32[4,16,128]{2,1,0:T(8,128)S(1)}, f32[4,16,128]{2,1,0:T(8,128)S(1)}, u32[]{:S(2)}, u32[]{:S(2)}) collective-permute-start(f32[4,16,128]{2,1,0:T(8,128)S(1)} %get-tuple-element.212), channel_id=1, source_target_pairs={{0,24},{1,25},{2,26},{3,27},{4,28},{5,29},{6,30},{7,31},{8,16},{9,... | collective-permute-start | bytes 98312 | tf_op jit(solution)/shard_map/ppermute | solution.py:441
  26.0 2.0 %collective-permute-start.15 = (f32[4,16,128]{2,1,0:T(8,128)S(1)}, f32[4,16,128]{2,1,0:T(8,128)S(1)}, u32[]{:S(2)}, u32[]{:S(2)}) collective-permute-start(f32[4,16,128]{2,1,0:T(8,128)S(1)} %get-tuple-element.213), channel_id=1, source_target_pairs={{0,8},{1,9},{2,10},{3,11},{4,12},{5,13},{6,14},{7,15},{8,0},{9,1},... | collective-permute-start | bytes 98312 | tf_op jit(solution)/shard_map/ppermute | solution.py:441
  28.0 2.5 %band.2 = (f32[32,16,128]{2,1,0:T(8,128)S(1)}, bf16[48,4608]{1,0:T(8,128)(2,1)S(1)}) custom-call(bf16[18,12,128,256]{3,2,1,0:T(8,128)(2,1)S(1)} %get-tuple-element.199.weights_ref, f32[32,16,128]{2,1,0:T(8,128)S(1)} %get-tuple-element.208.field_ref), custom_call_target="tpu_custom_call" | custom-call | flops 1000000000 | bytes 12000000 | tf_op jit(solution)/shard_map/band/pallas_call | solution.py:489
  30.5 0.0 collective-permute-start.16
  30.5 0.0 collective-permute-done.12.refs_0_
  30.5 0.1 collective-permute-start.17
  30.6 0.5 gram.2.early_ref
  31.1 0.0 collective-permute-done.13.refs_1_
  31.1 0.0 collective-permute-done.14.refs_2_
  31.2 0.0 collective-permute-done.15.refs_3_
  31.2 3.2 %collective-permute-done.16.refs_4_ = f32[4,16,128]{2,1,0:T(8,128)S(1)} collective-permute-done((f32[4,16,128]{2,1,0:T(8,128)S(1)}, f32[4,16,128]{2,1,0:T(8,128)S(1)}, u32[]{:S(2)}, u32[]{:S(2)}) %collective-permute-start.16) | collective-permute-done | bytes 32800 | tf_op jit(solution)/shard_map/ppermute | solution.py:441
  34.5 1.1 %link.3 = (f32[32,16,128]{2,1,0:T(8,128)S(1)}, f32[4,16,128]{2,1,0:T(8,128)S(1)}, f32[4,16,128]{2,1,0:T(8,128)S(1)}, f32[4,16,128]{2,1,0:T(8,128)S(1)}, f32[4,16...) custom-call(s32[1,4,6]{2,1,0:T(4,128)} %bitcast.242, ...), custom_call_target="tpu_custom_call" | custom-call | tf_op jit(solution)/shard_map/link/pallas_call | solution.py:510
  35.6 0.1 collective-permute-start.18
  35.7 2.5 %band.3 = (f32[32,16,128]{2,1,0:T(8,128)S(1)}, bf16[48,4608]{1,0:T(8,128)(2,1)S(1)}) custom-call(bf16[18,12,128,256]{3,2,1,0:T(8,128)(2,1)S(1)} %get-tuple-element.199.weights_ref, f32[32,16,128]{2,1,0:T(8,128)S(1)} %get-tuple-element.216.field_ref), custom_call_target="tpu_custom_call" | custom-call | flops 1000000000 | bytes 12000000 | tf_op jit(solution)/shard_map/band/pallas_call | solution.py:489
  38.2 2.7 %collective-permute-start.19 = (f32[4,16,128]{2,1,0:T(8,128)S(1)}, f32[4,16,128]{2,1,0:T(8,128)S(1)}, u32[]{:S(2)}, u32[]{:S(2)}) collective-permute-start(f32[4,16,128]{2,1,0:T(8,128)S(1)} %get-tuple-element.222), channel_id=1, source_target_pairs={{0,30},{1,31},{2,4},{3,5},{4,2},{5,3},{6,8},{7,9},{8,6},{9,7},{10,... | collective-permute-start | bytes 98312 | tf_op jit(solution)/shard_map/ppermute | solution.py:441
  40.9 1.0 %collective-permute-start.20 = (f32[4,16,128]{2,1,0:T(8,128)S(1)}, f32[4,16,128]{2,1,0:T(8,128)S(1)}, u32[]{:S(2)}, u32[]{:S(2)}) collective-permute-start(f32[4,16,128]{2,1,0:T(8,128)S(1)} %get-tuple-element.223), channel_id=1, source_target_pairs={{0,24},{1,25},{2,26},{3,27},{4,28},{5,29},{6,30},{7,31},{8,16},{9,... | collective-permute-start | bytes 98312 | tf_op jit(solution)/shard_map/ppermute | solution.py:441
  41.9 1.1 %collective-permute-start.21 = (f32[4,16,128]{2,1,0:T(8,128)S(1)}, f32[4,16,128]{2,1,0:T(8,128)S(1)}, u32[]{:S(2)}, u32[]{:S(2)}) collective-permute-start(f32[4,16,128]{2,1,0:T(8,128)S(1)} %get-tuple-element.224), channel_id=1, source_target_pairs={{0,8},{1,9},{2,10},{3,11},{4,12},{5,13},{6,14},{7,15},{8,0},{9,1},... | collective-permute-start | bytes 98312 | tf_op jit(solution)/shard_map/ppermute | solution.py:441
  43.0 0.7 %collective-permute-start.23 = (f32[4,16,128]{2,1,0:T(8,128)S(1)}, f32[4,16,128]{2,1,0:T(8,128)S(1)}, u32[]{:S(2)}, u32[]{:S(2)}) collective-permute-start(f32[4,16,128]{2,1,0:T(8,128)S(1)} %get-tuple-element.226), channel_id=1, source_target_pairs={{0,1},{1,0},{2,3},{3,2},{4,5},{5,4},{6,7},{7,6},{8,9},{9,8},{10,11... | collective-permute-start | bytes 98312 | tf_op jit(solution)/shard_map/ppermute | solution.py:441
  43.7 0.5 gram.3.moments_ref
  44.2 1.9 %collective-permute-done.19.refs_1_ = f32[4,16,128]{2,1,0:T(8,128)S(1)} collective-permute-done((f32[4,16,128]{2,1,0:T(8,128)S(1)}, f32[4,16,128]{2,1,0:T(8,128)S(1)}, u32[]{:S(2)}, u32[]{:S(2)}) %collective-permute-start.19) | collective-permute-done | bytes 32800 | tf_op jit(solution)/shard_map/ppermute | solution.py:441
  46.1 0.7 %collective-permute-done.20.refs_2_ = f32[4,16,128]{2,1,0:T(8,128)S(1)} collective-permute-done((f32[4,16,128]{2,1,0:T(8,128)S(1)}, f32[4,16,128]{2,1,0:T(8,128)S(1)}, u32[]{:S(2)}, u32[]{:S(2)}) %collective-permute-start.20) | collective-permute-done | bytes 32800 | tf_op jit(solution)/shard_map/ppermute | solution.py:441
  46.7 0.0 collective-permute-done.21.refs_3_
  46.7 0.2 collective-permute-done.22.refs_4_
  46.9 0.0 collective-permute-done.23.refs_5_
  46.9 1.9 %last_link.1 = (bf16[48,4608]{1,0:T(8,128)(2,1)S(1)}, f32[32,8,128]{2,1,0:T(8,128)S(1)}) custom-call(s32[1,4,6]{2,1,0:T(4,128)} %bitcast.243, f32[32,16,128]{2,1,0:T(8,128)S(1)} %get-tuple-element.217.base_ref, bf16[6,2,256,256]{3,2,1,0:T(8,128)(2,1)S(1)} %get-tuple-element.201.links_ref, bf16[48,4608]{1,0:T(8,128)(2,1)S(1)} %get-tuple-element.218.split2, ...), custom_call_target="tpu_custom_call" | custom-call | tf_op jit(solution)/shard_map/last_link/pallas_call | solution.py:519
  48.9 0.0 copy-start.1
  48.9 0.0 copy-start.3
  48.9 0.0 copy-start.4
  48.9 11.6 %all_to_all.5.gathered_ref = f32[32,8,128]{2,1,0:T(8,128)S(1)} all-to-all(f32[32,8,128]{2,1,0:T(8,128)S(1)} %get-tuple-element.227), channel_id=1, replica_groups=mesh['dom'=32] {'dom'}, dimensions={0} | all-to-all | bytes 262144 | tf_op jit(solution)/shard_map/all_to_all | solution.py:529
  60.5 3.3 %finish.1 = (f32[32,16,128]{2,1,0:T(8,128)}, f32[32,16,128]{2,1,0:T(8,128)}, s32[1]{0:T(128)}) custom-call(f32[32,8,128]{2,1,0:T(8,128)S(1)} %all_to_all.5.gathered_ref, bf16[48,4608]{1,0:T(8,128)(2,1)S(1)} %get-tuple-element.220.split0, bf16[48,4608]{1,0:T(8,128)(2,1)S(1)} %get-tuple-element.219.split1, bf16[48,4608]{1,0:T(8,128)(2,1)S(1)} %get-tuple-element.218.split2, ...), custom_call_target="tpu_custom_call" | custom-call | tf_op jit(solution)/shard_map/finish/pallas_call | solution.py:530
  63.9 0.9 %while.30 = (s32[1]{0:T(128)}, f32[32,16,128]{2,1,0:T(8,128)}, f32[32,16,128]{2,1,0:T(8,128)}, f32[32,16,128]{2,1,0:T(8,128)S(1)}, f32[32,5,128,128]{3,2,1,0:T(8...) while((s32[1]{0:T(128)}, f32[32,16,128]{2,1,0:T(8,128)}, ...), condition=%region_8.11_spmd, body=%region_0.10_spmd | while | flops 189602848 | bytes 16476032 | solution.py:544
  (6 shorter events, 0.0 us)
Async XLA Ops:
  1.6 9.0 %collective-permute-start.6 = (f32[4,16,128]{2,1,0:T(8,128)S(1)}, f32[4,16,128]{2,1,0:T(8,128)S(1)}, u32[]{:S(2)}, u32[]{:S(2)}) collective-permute-start(f32[4,16,128]{2,1,0:T(8,128)S(1)} %get-tuple-element.202), channel_id=1, source_target_pairs={{0,31},{1,2},{2,1},{3,4},{4,3},{5,6},{6,5},{7,8},{8,7},{9,10},{10,... | collective-permute-start | bytes 98312 | tf_op jit(solution)/shard_map/ppermute | solution.py:441
  8.1 9.4 %collective-permute-start.7 = (f32[4,16,128]{2,1,0:T(8,128)S(1)}, f32[4,16,128]{2,1,0:T(8,128)S(1)}, u32[]{:S(2)}, u32[]{:S(2)}) collective-permute-start(f32[4,16,128]{2,1,0:T(8,128)S(1)} %get-tuple-element.203), channel_id=1, source_target_pairs={{0,30},{1,31},{2,4},{3,5},{4,2},{5,3},{6,8},{7,9},{8,6},{9,7},{10,... | collective-permute-start | bytes 98312 | tf_op jit(solution)/shard_map/ppermute | solution.py:441
  8.7 8.8 %collective-permute-start.8 = (f32[4,16,128]{2,1,0:T(8,128)S(1)}, f32[4,16,128]{2,1,0:T(8,128)S(1)}, u32[]{:S(2)}, u32[]{:S(2)}) collective-permute-start(f32[4,16,128]{2,1,0:T(8,128)S(1)} %get-tuple-element.204), channel_id=1, source_target_pairs={{0,24},{1,25},{2,26},{3,27},{4,28},{5,29},{6,30},{7,31},{8,16},{9,... | collective-permute-start | bytes 98312 | tf_op jit(solution)/shard_map/ppermute | solution.py:441
  9.2 8.3 %collective-permute-start.9 = (f32[4,16,128]{2,1,0:T(8,128)S(1)}, f32[4,16,128]{2,1,0:T(8,128)S(1)}, u32[]{:S(2)}, u32[]{:S(2)}) collective-permute-start(f32[4,16,128]{2,1,0:T(8,128)S(1)} %get-tuple-element.205), channel_id=1, source_target_pairs={{0,8},{1,9},{2,10},{3,11},{4,12},{5,13},{6,14},{7,15},{8,0},{9,1},... | collective-permute-start | bytes 98312 | tf_op jit(solution)/shard_map/ppermute | solution.py:441
  9.2 8.3 %collective-permute-start.10 = (f32[4,16,128]{2,1,0:T(8,128)S(1)}, f32[4,16,128]{2,1,0:T(8,128)S(1)}, u32[]{:S(2)}, u32[]{:S(2)}) collective-permute-start(f32[4,16,128]{2,1,0:T(8,128)S(1)} %get-tuple-element.206), channel_id=1, source_target_pairs={{0,2},{1,3},{2,0},{3,1},{4,6},{5,7},{6,4},{7,5},{8,10},{9,11},{10,... | collective-permute-start | bytes 98312 | tf_op jit(solution)/shard_map/ppermute | solution.py:441
  10.6 6.9 %collective-permute-start.11 = (f32[4,16,128]{2,1,0:T(8,128)S(1)}, f32[4,16,128]{2,1,0:T(8,128)S(1)}, u32[]{:S(2)}, u32[]{:S(2)}) collective-permute-start(f32[4,16,128]{2,1,0:T(8,128)S(1)} %get-tuple-element.207), channel_id=1, source_target_pairs={{0,1},{1,0},{2,3},{3,2},{4,5},{5,4},{6,7},{7,6},{8,9},{9,8},{10,11... | collective-permute-start | bytes 98312 | tf_op jit(solution)/shard_map/ppermute | solution.py:441
  18.7 11.9 %collective-permute-start.12 = (f32[4,16,128]{2,1,0:T(8,128)S(1)}, f32[4,16,128]{2,1,0:T(8,128)S(1)}, u32[]{:S(2)}, u32[]{:S(2)}) collective-permute-start(f32[4,16,128]{2,1,0:T(8,128)S(1)} %get-tuple-element.210), channel_id=1, source_target_pairs={{0,31},{1,2},{2,1},{3,4},{4,3},{5,6},{6,5},{7,8},{8,7},{9,10},{10,... | collective-permute-start | bytes 98312 | tf_op jit(solution)/shard_map/ppermute | solution.py:441
  23.2 8.0 %collective-permute-start.13 = (f32[4,16,128]{2,1,0:T(8,128)S(1)}, f32[4,16,128]{2,1,0:T(8,128)S(1)}, u32[]{:S(2)}, u32[]{:S(2)}) collective-permute-start(f32[4,16,128]{2,1,0:T(8,128)S(1)} %get-tuple-element.211), channel_id=1, source_target_pairs={{0,30},{1,31},{2,4},{3,5},{4,2},{5,3},{6,8},{7,9},{8,6},{9,7},{10,... | collective-permute-start | bytes 98312 | tf_op jit(solution)/shard_map/ppermute | solution.py:441
  24.0 7.2 %collective-permute-start.14 = (f32[4,16,128]{2,1,0:T(8,128)S(1)}, f32[4,16,128]{2,1,0:T(8,128)S(1)}, u32[]{:S(2)}, u32[]{:S(2)}) collective-permute-start(f32[4,16,128]{2,1,0:T(8,128)S(1)} %get-tuple-element.212), channel_id=1, source_target_pairs={{0,24},{1,25},{2,26},{3,27},{4,28},{5,29},{6,30},{7,31},{8,16},{9,... | collective-permute-start | bytes 98312 | tf_op jit(solution)/shard_map/ppermute | solution.py:441
  26.0 5.2 %collective-permute-start.15 = (f32[4,16,128]{2,1,0:T(8,128)S(1)}, f32[4,16,128]{2,1,0:T(8,128)S(1)}, u32[]{:S(2)}, u32[]{:S(2)}) collective-permute-start(f32[4,16,128]{2,1,0:T(8,128)S(1)} %get-tuple-element.213), channel_id=1, source_target_pairs={{0,8},{1,9},{2,10},{3,11},{4,12},{5,13},{6,14},{7,15},{8,0},{9,1},... | collective-permute-start | bytes 98312 | tf_op jit(solution)/shard_map/ppermute | solution.py:441
  30.5 3.9 %collective-permute-start.16 = (f32[4,16,128]{2,1,0:T(8,128)S(1)}, f32[4,16,128]{2,1,0:T(8,128)S(1)}, u32[]{:S(2)}, u32[]{:S(2)}) collective-permute-start(f32[4,16,128]{2,1,0:T(8,128)S(1)} %get-tuple-element.214), channel_id=1, source_target_pairs={{0,2},{1,3},{2,0},{3,1},{4,6},{5,7},{6,4},{7,5},{8,10},{9,11},{10,... | collective-permute-start | bytes 98312 | tf_op jit(solution)/shard_map/ppermute | solution.py:441
  30.5 3.9 %collective-permute-start.17 = (f32[4,16,128]{2,1,0:T(8,128)S(1)}, f32[4,16,128]{2,1,0:T(8,128)S(1)}, u32[]{:S(2)}, u32[]{:S(2)}) collective-permute-start(f32[4,16,128]{2,1,0:T(8,128)S(1)} %get-tuple-element.215), channel_id=1, source_target_pairs={{0,1},{1,0},{2,3},{3,2},{4,5},{5,4},{6,7},{7,6},{8,9},{9,8},{10,11... | collective-permute-start | bytes 98312 | tf_op jit(solution)/shard_map/ppermute | solution.py:441
  35.6 7.4 %collective-permute-start.18 = (f32[4,16,128]{2,1,0:T(8,128)S(1)}, f32[4,16,128]{2,1,0:T(8,128)S(1)}, u32[]{:S(2)}, u32[]{:S(2)}) collective-permute-start(f32[4,16,128]{2,1,0:T(8,128)S(1)} %get-tuple-element.221), channel_id=1, source_target_pairs={{0,31},{1,2},{2,1},{3,4},{4,3},{5,6},{6,5},{7,8},{8,7},{9,10},{10,... | collective-permute-start | bytes 98312 | tf_op jit(solution)/shard_map/ppermute | solution.py:441
  38.2 7.9 %collective-permute-start.19 = (f32[4,16,128]{2,1,0:T(8,128)S(1)}, f32[4,16,128]{2,1,0:T(8,128)S(1)}, u32[]{:S(2)}, u32[]{:S(2)}) collective-permute-start(f32[4,16,128]{2,1,0:T(8,128)S(1)} %get-tuple-element.222), channel_id=1, source_target_pairs={{0,30},{1,31},{2,4},{3,5},{4,2},{5,3},{6,8},{7,9},{8,6},{9,7},{10,... | collective-permute-start | bytes 98312 | tf_op jit(solution)/shard_map/ppermute | solution.py:441
  40.9 5.8 %collective-permute-start.20 = (f32[4,16,128]{2,1,0:T(8,128)S(1)}, f32[4,16,128]{2,1,0:T(8,128)S(1)}, u32[]{:S(2)}, u32[]{:S(2)}) collective-permute-start(f32[4,16,128]{2,1,0:T(8,128)S(1)} %get-tuple-element.223), channel_id=1, source_target_pairs={{0,24},{1,25},{2,26},{3,27},{4,28},{5,29},{6,30},{7,31},{8,16},{9,... | collective-permute-start | bytes 98312 | tf_op jit(solution)/shard_map/ppermute | solution.py:441
  41.9 4.8 %collective-permute-start.21 = (f32[4,16,128]{2,1,0:T(8,128)S(1)}, f32[4,16,128]{2,1,0:T(8,128)S(1)}, u32[]{:S(2)}, u32[]{:S(2)}) collective-permute-start(f32[4,16,128]{2,1,0:T(8,128)S(1)} %get-tuple-element.224), channel_id=1, source_target_pairs={{0,8},{1,9},{2,10},{3,11},{4,12},{5,13},{6,14},{7,15},{8,0},{9,1},... | collective-permute-start | bytes 98312 | tf_op jit(solution)/shard_map/ppermute | solution.py:441
  43.0 3.9 %collective-permute-start.22 = (f32[4,16,128]{2,1,0:T(8,128)S(1)}, f32[4,16,128]{2,1,0:T(8,128)S(1)}, u32[]{:S(2)}, u32[]{:S(2)}) collective-permute-start(f32[4,16,128]{2,1,0:T(8,128)S(1)} %get-tuple-element.225), channel_id=1, source_target_pairs={{0,2},{1,3},{2,0},{3,1},{4,6},{5,7},{6,4},{7,5},{8,10},{9,11},{10,... | collective-permute-start | bytes 98312 | tf_op jit(solution)/shard_map/ppermute | solution.py:441
  43.0 3.9 %collective-permute-start.23 = (f32[4,16,128]{2,1,0:T(8,128)S(1)}, f32[4,16,128]{2,1,0:T(8,128)S(1)}, u32[]{:S(2)}, u32[]{:S(2)}) collective-permute-start(f32[4,16,128]{2,1,0:T(8,128)S(1)} %get-tuple-element.226), channel_id=1, source_target_pairs={{0,1},{1,0},{2,3},{3,2},{4,5},{5,4},{6,7},{7,6},{8,9},{9,8},{10,11... | collective-permute-start | bytes 98312 | tf_op jit(solution)/shard_map/ppermute | solution.py:441
  48.9 15.0 %copy-start.1 = (f32[1,6,4,128,128]{4,3,2,1,0:T(8,128)S(1)}, f32[1,6,4,128,128]{4,3,2,1,0:T(8,128)}, u32[]{:S(2)}) copy-start(f32[1,6,4,128,128]{4,3,2,1,0:T(8,128)} %link_hbm.1) | copy-start | bytes 4718596
  48.9 14.9 %copy-start.3 = (f32[32,16,128]{2,1,0:T(8,128)S(1)}, f32[32,16,128]{2,1,0:T(8,128)}, u32[]{:S(2)}) copy-start(f32[32,16,128]{2,1,0:T(8,128)} %field_hbm.3) | copy-start | bytes 786436
  48.9 14.9 %copy-start.4 = (s32[1,6,4]{1,2,0:T(4,128)S(1)}, s32[1,6,4]{1,2,0:T(4,128)}, u32[]{:S(2)}) copy-start(s32[1,6,4]{1,2,0:T(4,128)} %param.14) | copy-start | bytes 292

commit v5 on v4

--- a/solution.py
+++ b/solution.py
@@ -115,7 +115,7 @@
         pair_product(weights_ref, split_ref, out_ref, pair)
         return carry
 
-    lax.fori_loop(0, out_ref.shape[0] // 2, body, 0, unroll=4)
+    lax.fori_loop(0, out_ref.shape[0] // 2, body, 0, unroll=True)
 
 
 def prepare_kernel(
@@ -179,7 +179,7 @@
             links_ref[face, slot // 2, size:, cols] = low
         return carry
 
-    lax.fori_loop(0, faces, convert_links, 0)
+    lax.fori_loop(0, faces, convert_links, 0, unroll=True)
 
 
 def add_links(dev_count, rows_ref, base_ref, links_ref, far_refs, field_ref):
@@ -354,7 +354,7 @@
             residual_ref[index * step + k] = total[width:, k * 128 : (k + 1) * 128]
         return carry
 
-    lax.fori_loop(0, block_rows // step, body, 0, unroll=2)
+    lax.fori_loop(0, block_rows // step, body, 0, unroll=True)
 
 
 def gram_matrix(left, right):

time: 65.1 us -> 63.6 us (0.977)
  Pallas kernels: 21.3 us -> 19.8 us
    pallas_call x2, Pallas kernels: 5.02 us -> 4.12 us  [shards(): pl.pallas_call(functools.partial(band_kernel, half), out_shape=[field, sp...]
  transfers between devices with their start and end apart: 18 -> 18, of which waited for: 4 -> 4; matrix products, arithmetic and copies ran while one was open for 0% -> 0% of each run, Pallas kernels for 20% -> 18%
where the time goes in v5:
time: 63.6 us; the launch traced here: 63.4 us
  starting transfers between devices  24.1 us (38%)
  Pallas kernels  19.8 us (31%)
  blocking collectives  11.6 us (18%)
  waiting for transfers between devices  6.06 us (10%)
  between operations  1 us (2%)
  loops' own time  0.88 us (1%)
    ppermute x18, starting transfers between devices, exchange(): lax.ppermute(messages[index], 'dom', matching_pairs(dev_count, pair, phase))  24.1 us
    all_to_all x1, blocking collectives, shards(): gathered = lax.all_to_all(mine, 'dom', 0, 0)  11.6 us
    pallas_call x1, Pallas kernels, shards(): pl.pallas_call(functools.partial(prepare_kernel, half), out_shape=[pltpu....  6.48 us
    ppermute x18, waiting for transfers between devices, exchange(): lax.ppermute(messages[index], 'dom', matching_pairs(dev_count, pair, phase))  6.06 us
    pallas_call x2, Pallas kernels, shards(): pl.pallas_call(functools.partial(band_kernel, half), out_shape=[field, sp...  4.12 us
    pallas_call x1, Pallas kernels, shards(): pl.pallas_call(functools.partial(finish_kernel, half), out_shape=[field,...  3.03 us
    pallas_call x2, Pallas kernels, shards(): pl.pallas_call(functools.partial(link_kernel, dev_count), out_shape=[fiel...  2.23 us
    pallas_call x1, Pallas kernels, shards(): pl.pallas_call(functools.partial(last_link_kernel, dev_count, half), out_...  1.92 us
  transfers between devices with their start and end apart: 18, of which 4 were waited for; matrix products, arithmetic and copies ran while one was open for 0% of the time, Pallas kernels for 18%

profile of v5, /device:TPU:0, one launch (start us, length us, event | category | flops | bytes accessed | tf_op | source)
XLA Modules:
  0.0 63.4 jit_solution(7688052565647768173)
XLA Ops:
  0.6 1.0 %first_send.1 = (f32[4,16,128]{2,1,0:T(8,128)S(1)}, f32[4,16,128]{2,1,0:T(8,128)S(1)}, f32[4,16,128]{2,1,0:T(8,128)S(1)}, f32[4,16,128]{2,1,0:T(8,128)S(1)}, f32...) custom-call(s32[1,4,6]{2,1,0:T(4,128)} %bitcast.240, f32[32,16,128]{2,1,0:T(8,128)} %field_hbm.3), custom_call_target="tpu_custom_call" | custom-call | tf_op jit(solution)/shard_map/first_send/pallas_call | solution.py:449
  1.6 6.5 %collective-permute-start.6 = (f32[4,16,128]{2,1,0:T(8,128)S(1)}, f32[4,16,128]{2,1,0:T(8,128)S(1)}, u32[]{:S(2)}, u32[]{:S(2)}) collective-permute-start(f32[4,16,128]{2,1,0:T(8,128)S(1)} %get-tuple-element.202), channel_id=1, source_target_pairs={{0,31},{1,2},{2,1},{3,4},{4,3},{5,6},{6,5},{7,8},{8,7},{9,10},{10,... | collective-permute-start | bytes 98312 | tf_op jit(solution)/shard_map/ppermute | solution.py:441
  8.1 0.6 %collective-permute-start.7 = (f32[4,16,128]{2,1,0:T(8,128)S(1)}, f32[4,16,128]{2,1,0:T(8,128)S(1)}, u32[]{:S(2)}, u32[]{:S(2)}) collective-permute-start(f32[4,16,128]{2,1,0:T(8,128)S(1)} %get-tuple-element.203), channel_id=1, source_target_pairs={{0,30},{1,31},{2,4},{3,5},{4,2},{5,3},{6,8},{7,9},{8,6},{9,7},{10,... | collective-permute-start | bytes 98312 | tf_op jit(solution)/shard_map/ppermute | solution.py:441
  8.7 0.4 collective-permute-start.8
  9.2 0.0 collective-permute-start.9
  9.2 1.4 %collective-permute-start.10 = (f32[4,16,128]{2,1,0:T(8,128)S(1)}, f32[4,16,128]{2,1,0:T(8,128)S(1)}, u32[]{:S(2)}, u32[]{:S(2)}) collective-permute-start(f32[4,16,128]{2,1,0:T(8,128)S(1)} %get-tuple-element.206), channel_id=1, source_target_pairs={{0,2},{1,3},{2,0},{3,1},{4,6},{5,7},{6,4},{7,5},{8,10},{9,11},{10,... | collective-permute-start | bytes 98312 | tf_op jit(solution)/shard_map/ppermute | solution.py:441
  10.6 0.0 collective-permute-done.6.refs_0_
  10.6 0.0 collective-permute-start.11
  10.6 6.5 %prepare.1 = (bf16[18,12,128,256]{3,2,1,0:T(8,128)(2,1)S(1)}, bf16[6,2,256,256]{3,2,1,0:T(8,128)(2,1)S(1)}, bf16[48,4608]{1,0:T(8,128)(2,1)S(1)}, f32[32,16,128]{2,1,0:T(8,128)S(1)}) custom-call(f32[32,16,128]{2,1,0:T(8,128)} %field_hbm.3, f32[32,5,128,128]{3,2,1,0:T(8,128)} %band_hbm.1, f32[1,6,4,128,128]{4,3,2,1,0:T(8,128)} %link_hbm.1), custom_call_target="tpu_custom_call" | custom-call | flops 1000000000 | bytes 12000000 | tf_op jit(solution)/shard_map/prepare/pallas_call | solution.py:463
  17.1 0.0 collective-permute-done.7.refs_1_
  17.2 0.0 collective-permute-done.8.refs_2_
  17.2 0.0 collective-permute-done.9.refs_3_
  17.2 0.0 collective-permute-done.10.refs_4_
  17.2 0.0 collective-permute-done.11.refs_5_
  17.2 1.1 %link.2 = (f32[32,16,128]{2,1,0:T(8,128)S(1)}, f32[4,16,128]{2,1,0:T(8,128)S(1)}, f32[4,16,128]{2,1,0:T(8,128)S(1)}, f32[4,16,128]{2,1,0:T(8,128)S(1)}, f32[4,16...) custom-call(s32[1,4,6]{2,1,0:T(4,128)} %bitcast.241, ...), custom_call_target="tpu_custom_call" | custom-call | tf_op jit(solution)/shard_map/link/pallas_call | solution.py:510
  18.3 4.5 %collective-permute-start.12 = (f32[4,16,128]{2,1,0:T(8,128)S(1)}, f32[4,16,128]{2,1,0:T(8,128)S(1)}, u32[]{:S(2)}, u32[]{:S(2)}) collective-permute-start(f32[4,16,128]{2,1,0:T(8,128)S(1)} %get-tuple-element.210), channel_id=1, source_target_pairs={{0,31},{1,2},{2,1},{3,4},{4,3},{5,6},{6,5},{7,8},{8,7},{9,10},{10,... | collective-permute-start | bytes 98312 | tf_op jit(solution)/shard_map/ppermute | solution.py:441
  22.8 0.8 %collective-permute-start.13 = (f32[4,16,128]{2,1,0:T(8,128)S(1)}, f32[4,16,128]{2,1,0:T(8,128)S(1)}, u32[]{:S(2)}, u32[]{:S(2)}) collective-permute-start(f32[4,16,128]{2,1,0:T(8,128)S(1)} %get-tuple-element.211), channel_id=1, source_target_pairs={{0,30},{1,31},{2,4},{3,5},{4,2},{5,3},{6,8},{7,9},{8,6},{9,7},{10,... | collective-permute-start | bytes 98312 | tf_op jit(solution)/shard_map/ppermute | solution.py:441
  23.6 2.0 %collective-permute-start.14 = (f32[4,16,128]{2,1,0:T(8,128)S(1)}, f32[4,16,128]{2,1,0:T(8,128)S(1)}, u32[]{:S(2)}, u32[]{:S(2)}) collective-permute-start(f32[4,16,128]{2,1,0:T(8,128)S(1)} %get-tuple-element.212), channel_id=1, source_target_pairs={{0,24},{1,25},{2,26},{3,27},{4,28},{5,29},{6,30},{7,31},{8,16},{9,... | collective-permute-start | bytes 98312 | tf_op jit(solution)/shard_map/ppermute | solution.py:441
  25.7 2.0 %collective-permute-start.15 = (f32[4,16,128]{2,1,0:T(8,128)S(1)}, f32[4,16,128]{2,1,0:T(8,128)S(1)}, u32[]{:S(2)}, u32[]{:S(2)}) collective-permute-start(f32[4,16,128]{2,1,0:T(8,128)S(1)} %get-tuple-element.213), channel_id=1, source_target_pairs={{0,8},{1,9},{2,10},{3,11},{4,12},{5,13},{6,14},{7,15},{8,0},{9,1},... | collective-permute-start | bytes 98312 | tf_op jit(solution)/shard_map/ppermute | solution.py:441
  27.7 2.0 %band.2 = (f32[32,16,128]{2,1,0:T(8,128)S(1)}, bf16[48,4608]{1,0:T(8,128)(2,1)S(1)}) custom-call(bf16[18,12,128,256]{3,2,1,0:T(8,128)(2,1)S(1)} %get-tuple-element.199.weights_ref, f32[32,16,128]{2,1,0:T(8,128)S(1)} %get-tuple-element.208.field_ref), custom_call_target="tpu_custom_call" | custom-call | flops 1000000000 | bytes 12000000 | tf_op jit(solution)/shard_map/band/pallas_call | solution.py:489
  29.7 0.0 collective-permute-start.16
  29.7 0.0 collective-permute-done.12.refs_0_
  29.7 0.1 collective-permute-start.17
  29.8 0.5 gram.2.early_ref
  30.3 0.0 collective-permute-done.13.refs_1_
  30.3 0.0 collective-permute-done.14.refs_2_
  30.4 0.0 collective-permute-done.15.refs_3_
  30.4 3.3 %collective-permute-done.16.refs_4_ = f32[4,16,128]{2,1,0:T(8,128)S(1)} collective-permute-done((f32[4,16,128]{2,1,0:T(8,128)S(1)}, f32[4,16,128]{2,1,0:T(8,128)S(1)}, u32[]{:S(2)}, u32[]{:S(2)}) %collective-permute-start.16) | collective-permute-done | bytes 32800 | tf_op jit(solution)/shard_map/ppermute | solution.py:441
  33.7 0.0 collective-permute-done.17.refs_5_
  33.7 1.1 %link.3 = (f32[32,16,128]{2,1,0:T(8,128)S(1)}, f32[4,16,128]{2,1,0:T(8,128)S(1)}, f32[4,16,128]{2,1,0:T(8,128)S(1)}, f32[4,16,128]{2,1,0:T(8,128)S(1)}, f32[4,16...) custom-call(s32[1,4,6]{2,1,0:T(4,128)} %bitcast.242, ...), custom_call_target="tpu_custom_call" | custom-call | tf_op jit(solution)/shard_map/link/pallas_call | solution.py:510
  34.8 0.1 collective-permute-start.18
  34.9 2.1 %band.3 = (f32[32,16,128]{2,1,0:T(8,128)S(1)}, bf16[48,4608]{1,0:T(8,128)(2,1)S(1)}) custom-call(bf16[18,12,128,256]{3,2,1,0:T(8,128)(2,1)S(1)} %get-tuple-element.199.weights_ref, f32[32,16,128]{2,1,0:T(8,128)S(1)} %get-tuple-element.216.field_ref), custom_call_target="tpu_custom_call" | custom-call | flops 1000000000 | bytes 12000000 | tf_op jit(solution)/shard_map/band/pallas_call | solution.py:489
  36.9 2.7 %collective-permute-start.19 = (f32[4,16,128]{2,1,0:T(8,128)S(1)}, f32[4,16,128]{2,1,0:T(8,128)S(1)}, u32[]{:S(2)}, u32[]{:S(2)}) collective-permute-start(f32[4,16,128]{2,1,0:T(8,128)S(1)} %get-tuple-element.222), channel_id=1, source_target_pairs={{0,30},{1,31},{2,4},{3,5},{4,2},{5,3},{6,8},{7,9},{8,6},{9,7},{10,... | collective-permute-start | bytes 98312 | tf_op jit(solution)/shard_map/ppermute | solution.py:441
  39.6 1.0 %collective-permute-start.20 = (f32[4,16,128]{2,1,0:T(8,128)S(1)}, f32[4,16,128]{2,1,0:T(8,128)S(1)}, u32[]{:S(2)}, u32[]{:S(2)}) collective-permute-start(f32[4,16,128]{2,1,0:T(8,128)S(1)} %get-tuple-element.223), channel_id=1, source_target_pairs={{0,24},{1,25},{2,26},{3,27},{4,28},{5,29},{6,30},{7,31},{8,16},{9,... | collective-permute-start | bytes 98312 | tf_op jit(solution)/shard_map/ppermute | solution.py:441
  40.7 1.1 %collective-permute-start.21 = (f32[4,16,128]{2,1,0:T(8,128)S(1)}, f32[4,16,128]{2,1,0:T(8,128)S(1)}, u32[]{:S(2)}, u32[]{:S(2)}) collective-permute-start(f32[4,16,128]{2,1,0:T(8,128)S(1)} %get-tuple-element.224), channel_id=1, source_target_pairs={{0,8},{1,9},{2,10},{3,11},{4,12},{5,13},{6,14},{7,15},{8,0},{9,1},... | collective-permute-start | bytes 98312 | tf_op jit(solution)/shard_map/ppermute | solution.py:441
  41.8 0.7 %collective-permute-start.23 = (f32[4,16,128]{2,1,0:T(8,128)S(1)}, f32[4,16,128]{2,1,0:T(8,128)S(1)}, u32[]{:S(2)}, u32[]{:S(2)}) collective-permute-start(f32[4,16,128]{2,1,0:T(8,128)S(1)} %get-tuple-element.226), channel_id=1, source_target_pairs={{0,1},{1,0},{2,3},{3,2},{4,5},{5,4},{6,7},{7,6},{8,9},{9,8},{10,11... | collective-permute-start | bytes 98312 | tf_op jit(solution)/shard_map/ppermute | solution.py:441
  42.5 0.5 gram.3.moments_ref
  42.9 1.9 %collective-permute-done.19.refs_1_ = f32[4,16,128]{2,1,0:T(8,128)S(1)} collective-permute-done((f32[4,16,128]{2,1,0:T(8,128)S(1)}, f32[4,16,128]{2,1,0:T(8,128)S(1)}, u32[]{:S(2)}, u32[]{:S(2)}) %collective-permute-start.19) | collective-permute-done | bytes 32800 | tf_op jit(solution)/shard_map/ppermute | solution.py:441
  44.8 0.6 collective-permute-done.20.refs_2_
  45.5 0.0 collective-permute-done.21.refs_3_
  45.5 0.2 collective-permute-done.22.refs_4_
  45.7 1.9 %last_link.1 = (bf16[48,4608]{1,0:T(8,128)(2,1)S(1)}, f32[32,8,128]{2,1,0:T(8,128)S(1)}) custom-call(s32[1,4,6]{2,1,0:T(4,128)} %bitcast.243, f32[32,16,128]{2,1,0:T(8,128)S(1)} %get-tuple-element.217.base_ref, bf16[6,2,256,256]{3,2,1,0:T(8,128)(2,1)S(1)} %get-tuple-element.201.links_ref, bf16[48,4608]{1,0:T(8,128)(2,1)S(1)} %get-tuple-element.218.split2, ...), custom_call_target="tpu_custom_call" | custom-call | tf_op jit(solution)/shard_map/last_link/pallas_call | solution.py:519
  47.6 0.0 copy-start.1
  47.6 0.0 copy-start.3
  47.7 0.0 copy-start.4
  47.7 11.6 %all_to_all.5.gathered_ref = f32[32,8,128]{2,1,0:T(8,128)S(1)} all-to-all(f32[32,8,128]{2,1,0:T(8,128)S(1)} %get-tuple-element.227), channel_id=1, replica_groups=mesh['dom'=32] {'dom'}, dimensions={0} | all-to-all | bytes 262144 | tf_op jit(solution)/shard_map/all_to_all | solution.py:529
  59.3 3.0 %finish.1 = (f32[32,16,128]{2,1,0:T(8,128)}, f32[32,16,128]{2,1,0:T(8,128)}, s32[1]{0:T(128)}) custom-call(f32[32,8,128]{2,1,0:T(8,128)S(1)} %all_to_all.5.gathered_ref, bf16[48,4608]{1,0:T(8,128)(2,1)S(1)} %get-tuple-element.220.split0, bf16[48,4608]{1,0:T(8,128)(2,1)S(1)} %get-tuple-element.219.split1, bf16[48,4608]{1,0:T(8,128)(2,1)S(1)} %get-tuple-element.218.split2, ...), custom_call_target="tpu_custom_call" | custom-call | tf_op jit(solution)/shard_map/finish/pallas_call | solution.py:530
  62.3 0.9 %while.30 = (s32[1]{0:T(128)}, f32[32,16,128]{2,1,0:T(8,128)}, f32[32,16,128]{2,1,0:T(8,128)}, f32[32,16,128]{2,1,0:T(8,128)S(1)}, f32[32,5,128,128]{3,2,1,0:T(8...) while((s32[1]{0:T(128)}, f32[32,16,128]{2,1,0:T(8,128)}, ...), condition=%region_8.11_spmd, body=%region_0.10_spmd | while | flops 189602848 | bytes 16476032 | solution.py:544
  (6 shorter events, 0.0 us)
Async XLA Ops:
  1.6 9.0 %collective-permute-start.6 = (f32[4,16,128]{2,1,0:T(8,128)S(1)}, f32[4,16,128]{2,1,0:T(8,128)S(1)}, u32[]{:S(2)}, u32[]{:S(2)}) collective-permute-start(f32[4,16,128]{2,1,0:T(8,128)S(1)} %get-tuple-element.202), channel_id=1, source_target_pairs={{0,31},{1,2},{2,1},{3,4},{4,3},{5,6},{6,5},{7,8},{8,7},{9,10},{10,... | collective-permute-start | bytes 98312 | tf_op jit(solution)/shard_map/ppermute | solution.py:441
  8.1 9.0 %collective-permute-start.7 = (f32[4,16,128]{2,1,0:T(8,128)S(1)}, f32[4,16,128]{2,1,0:T(8,128)S(1)}, u32[]{:S(2)}, u32[]{:S(2)}) collective-permute-start(f32[4,16,128]{2,1,0:T(8,128)S(1)} %get-tuple-element.203), channel_id=1, source_target_pairs={{0,30},{1,31},{2,4},{3,5},{4,2},{5,3},{6,8},{7,9},{8,6},{9,7},{10,... | collective-permute-start | bytes 98312 | tf_op jit(solution)/shard_map/ppermute | solution.py:441
  8.7 8.4 %collective-permute-start.8 = (f32[4,16,128]{2,1,0:T(8,128)S(1)}, f32[4,16,128]{2,1,0:T(8,128)S(1)}, u32[]{:S(2)}, u32[]{:S(2)}) collective-permute-start(f32[4,16,128]{2,1,0:T(8,128)S(1)} %get-tuple-element.204), channel_id=1, source_target_pairs={{0,24},{1,25},{2,26},{3,27},{4,28},{5,29},{6,30},{7,31},{8,16},{9,... | collective-permute-start | bytes 98312 | tf_op jit(solution)/shard_map/ppermute | solution.py:441
  9.2 8.0 %collective-permute-start.9 = (f32[4,16,128]{2,1,0:T(8,128)S(1)}, f32[4,16,128]{2,1,0:T(8,128)S(1)}, u32[]{:S(2)}, u32[]{:S(2)}) collective-permute-start(f32[4,16,128]{2,1,0:T(8,128)S(1)} %get-tuple-element.205), channel_id=1, source_target_pairs={{0,8},{1,9},{2,10},{3,11},{4,12},{5,13},{6,14},{7,15},{8,0},{9,1},... | collective-permute-start | bytes 98312 | tf_op jit(solution)/shard_map/ppermute | solution.py:441
  9.2 8.0 %collective-permute-start.10 = (f32[4,16,128]{2,1,0:T(8,128)S(1)}, f32[4,16,128]{2,1,0:T(8,128)S(1)}, u32[]{:S(2)}, u32[]{:S(2)}) collective-permute-start(f32[4,16,128]{2,1,0:T(8,128)S(1)} %get-tuple-element.206), channel_id=1, source_target_pairs={{0,2},{1,3},{2,0},{3,1},{4,6},{5,7},{6,4},{7,5},{8,10},{9,11},{10,... | collective-permute-start | bytes 98312 | tf_op jit(solution)/shard_map/ppermute | solution.py:441
  10.6 6.5 %collective-permute-start.11 = (f32[4,16,128]{2,1,0:T(8,128)S(1)}, f32[4,16,128]{2,1,0:T(8,128)S(1)}, u32[]{:S(2)}, u32[]{:S(2)}) collective-permute-start(f32[4,16,128]{2,1,0:T(8,128)S(1)} %get-tuple-element.207), channel_id=1, source_target_pairs={{0,1},{1,0},{2,3},{3,2},{4,5},{5,4},{6,7},{7,6},{8,9},{9,8},{10,11... | collective-permute-start | bytes 98312 | tf_op jit(solution)/shard_map/ppermute | solution.py:441
  18.3 11.4 %collective-permute-start.12 = (f32[4,16,128]{2,1,0:T(8,128)S(1)}, f32[4,16,128]{2,1,0:T(8,128)S(1)}, u32[]{:S(2)}, u32[]{:S(2)}) collective-permute-start(f32[4,16,128]{2,1,0:T(8,128)S(1)} %get-tuple-element.210), channel_id=1, source_target_pairs={{0,31},{1,2},{2,1},{3,4},{4,3},{5,6},{6,5},{7,8},{8,7},{9,10},{10,... | collective-permute-start | bytes 98312 | tf_op jit(solution)/shard_map/ppermute | solution.py:441
  22.8 7.5 %collective-permute-start.13 = (f32[4,16,128]{2,1,0:T(8,128)S(1)}, f32[4,16,128]{2,1,0:T(8,128)S(1)}, u32[]{:S(2)}, u32[]{:S(2)}) collective-permute-start(f32[4,16,128]{2,1,0:T(8,128)S(1)} %get-tuple-element.211), channel_id=1, source_target_pairs={{0,30},{1,31},{2,4},{3,5},{4,2},{5,3},{6,8},{7,9},{8,6},{9,7},{10,... | collective-permute-start | bytes 98312 | tf_op jit(solution)/shard_map/ppermute | solution.py:441
  23.6 6.7 %collective-permute-start.14 = (f32[4,16,128]{2,1,0:T(8,128)S(1)}, f32[4,16,128]{2,1,0:T(8,128)S(1)}, u32[]{:S(2)}, u32[]{:S(2)}) collective-permute-start(f32[4,16,128]{2,1,0:T(8,128)S(1)} %get-tuple-element.212), channel_id=1, source_target_pairs={{0,24},{1,25},{2,26},{3,27},{4,28},{5,29},{6,30},{7,31},{8,16},{9,... | collective-permute-start | bytes 98312 | tf_op jit(solution)/shard_map/ppermute | solution.py:441
  25.7 4.7 %collective-permute-start.15 = (f32[4,16,128]{2,1,0:T(8,128)S(1)}, f32[4,16,128]{2,1,0:T(8,128)S(1)}, u32[]{:S(2)}, u32[]{:S(2)}) collective-permute-start(f32[4,16,128]{2,1,0:T(8,128)S(1)} %get-tuple-element.213), channel_id=1, source_target_pairs={{0,8},{1,9},{2,10},{3,11},{4,12},{5,13},{6,14},{7,15},{8,0},{9,1},... | collective-permute-start | bytes 98312 | tf_op jit(solution)/shard_map/ppermute | solution.py:441
  29.7 3.9 %collective-permute-start.16 = (f32[4,16,128]{2,1,0:T(8,128)S(1)}, f32[4,16,128]{2,1,0:T(8,128)S(1)}, u32[]{:S(2)}, u32[]{:S(2)}) collective-permute-start(f32[4,16,128]{2,1,0:T(8,128)S(1)} %get-tuple-element.214), channel_id=1, source_target_pairs={{0,2},{1,3},{2,0},{3,1},{4,6},{5,7},{6,4},{7,5},{8,10},{9,11},{10,... | collective-permute-start | bytes 98312 | tf_op jit(solution)/shard_map/ppermute | solution.py:441
  29.7 3.9 %collective-permute-start.17 = (f32[4,16,128]{2,1,0:T(8,128)S(1)}, f32[4,16,128]{2,1,0:T(8,128)S(1)}, u32[]{:S(2)}, u32[]{:S(2)}) collective-permute-start(f32[4,16,128]{2,1,0:T(8,128)S(1)} %get-tuple-element.215), channel_id=1, source_target_pairs={{0,1},{1,0},{2,3},{3,2},{4,5},{5,4},{6,7},{7,6},{8,9},{9,8},{10,11... | collective-permute-start | bytes 98312 | tf_op jit(solution)/shard_map/ppermute | solution.py:441
  34.8 7.0 %collective-permute-start.18 = (f32[4,16,128]{2,1,0:T(8,128)S(1)}, f32[4,16,128]{2,1,0:T(8,128)S(1)}, u32[]{:S(2)}, u32[]{:S(2)}) collective-permute-start(f32[4,16,128]{2,1,0:T(8,128)S(1)} %get-tuple-element.221), channel_id=1, source_target_pairs={{0,31},{1,2},{2,1},{3,4},{4,3},{5,6},{6,5},{7,8},{8,7},{9,10},{10,... | collective-permute-start | bytes 98312 | tf_op jit(solution)/shard_map/ppermute | solution.py:441
  36.9 7.9 %collective-permute-start.19 = (f32[4,16,128]{2,1,0:T(8,128)S(1)}, f32[4,16,128]{2,1,0:T(8,128)S(1)}, u32[]{:S(2)}, u32[]{:S(2)}) collective-permute-start(f32[4,16,128]{2,1,0:T(8,128)S(1)} %get-tuple-element.222), channel_id=1, source_target_pairs={{0,30},{1,31},{2,4},{3,5},{4,2},{5,3},{6,8},{7,9},{8,6},{9,7},{10,... | collective-permute-start | bytes 98312 | tf_op jit(solution)/shard_map/ppermute | solution.py:441
  39.6 5.8 %collective-permute-start.20 = (f32[4,16,128]{2,1,0:T(8,128)S(1)}, f32[4,16,128]{2,1,0:T(8,128)S(1)}, u32[]{:S(2)}, u32[]{:S(2)}) collective-permute-start(f32[4,16,128]{2,1,0:T(8,128)S(1)} %get-tuple-element.223), channel_id=1, source_target_pairs={{0,24},{1,25},{2,26},{3,27},{4,28},{5,29},{6,30},{7,31},{8,16},{9,... | collective-permute-start | bytes 98312 | tf_op jit(solution)/shard_map/ppermute | solution.py:441
  40.7 4.8 %collective-permute-start.21 = (f32[4,16,128]{2,1,0:T(8,128)S(1)}, f32[4,16,128]{2,1,0:T(8,128)S(1)}, u32[]{:S(2)}, u32[]{:S(2)}) collective-permute-start(f32[4,16,128]{2,1,0:T(8,128)S(1)} %get-tuple-element.224), channel_id=1, source_target_pairs={{0,8},{1,9},{2,10},{3,11},{4,12},{5,13},{6,14},{7,15},{8,0},{9,1},... | collective-permute-start | bytes 98312 | tf_op jit(solution)/shard_map/ppermute | solution.py:441
  41.8 3.9 %collective-permute-start.22 = (f32[4,16,128]{2,1,0:T(8,128)S(1)}, f32[4,16,128]{2,1,0:T(8,128)S(1)}, u32[]{:S(2)}, u32[]{:S(2)}) collective-permute-start(f32[4,16,128]{2,1,0:T(8,128)S(1)} %get-tuple-element.225), channel_id=1, source_target_pairs={{0,2},{1,3},{2,0},{3,1},{4,6},{5,7},{6,4},{7,5},{8,10},{9,11},{10,... | collective-permute-start | bytes 98312 | tf_op jit(solution)/shard_map/ppermute | solution.py:441
  41.8 3.9 %collective-permute-start.23 = (f32[4,16,128]{2,1,0:T(8,128)S(1)}, f32[4,16,128]{2,1,0:T(8,128)S(1)}, u32[]{:S(2)}, u32[]{:S(2)}) collective-permute-start(f32[4,16,128]{2,1,0:T(8,128)S(1)} %get-tuple-element.226), channel_id=1, source_target_pairs={{0,1},{1,0},{2,3},{3,2},{4,5},{5,4},{6,7},{7,6},{8,9},{9,8},{10,11... | collective-permute-start | bytes 98312 | tf_op jit(solution)/shard_map/ppermute | solution.py:441
  47.6 14.7 %copy-start.1 = (f32[1,6,4,128,128]{4,3,2,1,0:T(8,128)S(1)}, f32[1,6,4,128,128]{4,3,2,1,0:T(8,128)}, u32[]{:S(2)}) copy-start(f32[1,6,4,128,128]{4,3,2,1,0:T(8,128)} %link_hbm.1) | copy-start | bytes 4718596
  47.6 14.7 %copy-start.3 = (f32[32,16,128]{2,1,0:T(8,128)S(1)}, f32[32,16,128]{2,1,0:T(8,128)}, u32[]{:S(2)}) copy-start(f32[32,16,128]{2,1,0:T(8,128)} %field_hbm.3) | copy-start | bytes 786436
  47.7 14.7 %copy-start.4 = (s32[1,6,4]{1,2,0:T(4,128)S(1)}, s32[1,6,4]{1,2,0:T(4,128)}, u32[]{:S(2)}) copy-start(s32[1,6,4]{1,2,0:T(4,128)} %param.14) | copy-start | bytes 292
